TPU v7x, 8 devices: a whole 2x2x1 slice. The times are simulated.
8 devices in a mesh: part: 1 (over z), dp: 8 (over y, x, core).
Axes of the slice: x: 2, y: 2, z: 1, core: 2. Of those that a mesh axis runs over, the one named last changes fastest.
Arguments:
- hidden: bfloat16 [32, 512, 2048], P(('part', 'dp'))
- prompt_lens: int32 [32], P(('part', 'dp'))
- g_attn: bfloat16 [2, 2048], P(None, 'dp')
- w_query: bfloat16 [2, 2048, 32, 64], P(None, 'dp')
- w_key: bfloat16 [2, 2048, 32, 64], P(None, 'dp')
- w_value: bfloat16 [2, 2048, 32, 64], P(None, 'dp')
- w_out: bfloat16 [2, 2048, 2048], P(None, 'dp')
- g_mlp: bfloat16 [2, 2048], P(None, 'dp')
- w_gate: bfloat16 [2, 2048, 8192], P(None, 'dp')
- w_up: bfloat16 [2, 2048, 8192], P(None, 'dp')
- w_down: bfloat16 [2, 8192, 2048], P(None, 'dp')
- g_final: bfloat16 [2048], P('dp')
- embedding: bfloat16 [49152, 2048], P('dp')
Outputs:
- output 1: bfloat16 [2, 32, 512, 32, 64], P(None, ('part', 'dp'))
- output 2: bfloat16 [2, 32, 512, 32, 64], P(None, ('part', 'dp'))
- output 3: float32 [32, 49152], P(('part', 'dp'))
All inputs are finite; a program needn't handle non-finite values.
Results may differ from a plain program's by a relative error of at most 0.0160224.
Values are sent between devices in bfloat16 or wider.
A program may use at most 1 GiB of HBM per device.

v0:
```python
import math
import jax
import jax.numpy as jnp
from jax import lax
from jax.sharding import PartitionSpec as P


def rope_tables(seq_len, head_dim):
    half_dim = head_dim // 2
    exponent = jnp.arange(half_dim, dtype=jnp.float32) * (2.0 / head_dim)
    inv_freq = 1.0 / (500000.0 ** exponent)
    wave_len = 2.0 * math.pi / inv_freq
    smooth = (8192.0 / wave_len - 1.0) / 3.0
    blended = (1.0 - smooth) * inv_freq / 8.0 + smooth * inv_freq
    scaled = jnp.where(wave_len > 8192.0, inv_freq / 8.0, jnp.where(wave_len < 2048.0, inv_freq, blended))
    angles = jnp.arange(seq_len, dtype=jnp.float32)[:, None] * scaled[None, :]
    return jnp.cos(angles), jnp.sin(angles)


def apply_rope(values, cos_tab, sin_tab):
    half_dim = values.shape[-1] // 2
    low_half = values[..., :half_dim]
    high_half = values[..., half_dim:]
    cos_view = cos_tab[:, None, :]
    sin_view = sin_tab[:, None, :]
    return jnp.concatenate([low_half * cos_view - high_half * sin_view, high_half * cos_view + low_half * sin_view], axis=-1)


def rms_norm(values, gain_vec):
    values_f32 = values.astype(jnp.float32)
    mean_sq = jnp.mean(values_f32 * values_f32, axis=-1, keepdims=True)
    return (values_f32 * lax.rsqrt(mean_sq + 1e-5) * gain_vec.astype(jnp.float32)).astype(jnp.bfloat16)


def decoder_layer(hidden, prompt_lens, weights, cos_tab, sin_tab):
    g_attn, w_query, w_key, w_value, w_out, g_mlp, w_gate, w_up, w_down = weights
    batch_rows = hidden.shape[0]
    seq_len = hidden.shape[1]
    kv_heads = w_key.shape[1]
    head_dim = w_key.shape[2]
    group_size = w_query.shape[1] // kv_heads
    normed = rms_norm(hidden, g_attn)
    query_lin = jnp.einsum("bsd,dhe->bshe", normed, w_query, preferred_element_type=jnp.float32)
    query_rot = apply_rope(query_lin, cos_tab, sin_tab).astype(jnp.bfloat16)
    query_rot = query_rot.reshape(batch_rows, seq_len, kv_heads, group_size, head_dim)
    key_lin = jnp.einsum("bsd,dke->bske", normed, w_key, preferred_element_type=jnp.float32)
    key_rot = apply_rope(key_lin, cos_tab, sin_tab).astype(jnp.bfloat16)
    value_vec = jnp.einsum("bsd,dke->bske", normed, w_value, preferred_element_type=jnp.float32).astype(jnp.bfloat16)
    scores = jnp.einsum("bskgd,btkd->bkgst", query_rot, key_rot, preferred_element_type=jnp.float32) * head_dim ** -0.5
    positions = jnp.arange(seq_len)
    causal = positions[None, :] <= positions[:, None]
    in_prompt = positions[None, :] < prompt_lens[:, None]
    allowed = causal[None, :, :] & in_prompt[:, None, :]
    scores = jnp.where(allowed[:, None, None, :, :], scores, -jnp.inf)
    row_max = jnp.max(scores, axis=-1, keepdims=True)
    exp_scores = jnp.exp(scores - row_max)
    attn_probs = (exp_scores / jnp.sum(exp_scores, axis=-1, keepdims=True)).astype(jnp.bfloat16)
    attended = jnp.einsum("bkgst,btkd->bskgd", attn_probs, value_vec, preferred_element_type=jnp.float32)
    attended = attended.astype(jnp.bfloat16).reshape(batch_rows, seq_len, -1)
    attn_proj = jnp.einsum("bsh,hd->bsd", attended, w_out, preferred_element_type=jnp.float32)
    hidden_mid = (hidden.astype(jnp.float32) + attn_proj).astype(jnp.bfloat16)
    normed_mlp = rms_norm(hidden_mid, g_mlp)
    gate_val = jnp.einsum("bsd,df->bsf", normed_mlp, w_gate, preferred_element_type=jnp.float32)
    up_val = jnp.einsum("bsd,df->bsf", normed_mlp, w_up, preferred_element_type=jnp.float32)
    mlp_act = (jax.nn.silu(gate_val) * up_val).astype(jnp.bfloat16)
    down_proj = jnp.einsum("bsf,fd->bsd", mlp_act, w_down, preferred_element_type=jnp.float32)
    hidden_out = (hidden_mid.astype(jnp.float32) + down_proj).astype(jnp.bfloat16)
    return hidden_out, key_rot, value_vec


def solution(mesh):
    row_spec = P(("part", "dp"))
    layer_spec = P(None, "dp")

    def device_step(hidden, prompt_lens, g_attn, w_query, w_key, w_value, w_out, g_mlp, w_gate, w_up, w_down, g_final, embedding):
        seq_len = hidden.shape[1]
        cos_tab, sin_tab = rope_tables(seq_len, w_query.shape[3])
        layer_weights = (g_attn, w_query, w_key, w_value, w_out, g_mlp, w_gate, w_up, w_down)
        key_list = []
        value_list = []
        for layer_idx in range(w_query.shape[0]):
            weights = [lax.all_gather(weight_shard[layer_idx], "dp", axis=0, tiled=True) for weight_shard in layer_weights]
            hidden, key_rot, value_vec = decoder_layer(hidden, prompt_lens, weights, cos_tab, sin_tab)
            key_list.append(key_rot)
            value_list.append(value_vec)
        positions = jnp.arange(seq_len)
        select = (positions[None, :] == prompt_lens[:, None] - 1).astype(jnp.bfloat16)
        last_rows = jnp.einsum("bs,bsd->bd", select, hidden, preferred_element_type=jnp.float32).astype(jnp.bfloat16)
        normed_last = rms_norm(last_rows, lax.all_gather(g_final, "dp", axis=0, tiled=True))
        full_table = lax.all_gather(embedding, "dp", axis=0, tiled=True)
        logits = jnp.einsum("bd,vd->bv", normed_last, full_table, preferred_element_type=jnp.float32)
        return jnp.stack(key_list), jnp.stack(value_list), logits

    cache_spec = P(None, ("part", "dp"))
    return jax.shard_map(
        device_step,
        mesh=mesh,
        in_specs=(row_spec, row_spec) + (layer_spec,) * 9 + (P("dp"), P("dp")),
        out_specs=(cache_spec, cache_spec, row_spec),
        check_vma=False,
    )
```

profile of v0, /device:TPU:0, one launch (start us, length us, event | category | flops | bytes accessed | tf_op | source)
XLA Modules:
  0.0 2309.0 jit_solution(12204320141941475070)
XLA Ops:
  7.2 3.2 fusion.141
  10.5 3.2 fusion.143
  13.8 3.1 fusion.142
  17.0 1.4 fusion.140
  18.5 6.0 fusion.138
  24.6 6.1 fusion.137
  30.8 6.1 fusion.139
  36.9 0.7 all-gather.51.cloned.1.call-update
  42.2 13.7 all-gather
  56.0 10.7 all-gather.5
  67.3 10.8 all-gather.9
  78.7 10.8 all-gather.14
  90.1 10.9 all-gather.18
  102.3 5.1 fusion.20
  107.8 0.9 broadcast_and_fusion
  108.8 24.9 %fusion.64 = f32[4,512,32,64]{1,3,2,0:T(8,128)} fusion(bf16[1,2048,32,64]{1,3,2,0:T(8,128)(2,1)} %all-gather.41.cloned.1.call-done, bf16[4,512,2048]{2,1,0:T(8,128)(2,1)} %param.13, f32[2048]{0:T(1024)S(1)} %bitcast.203, f32[4,512]{1,0:T(4,128)S(1)} %add_rsqrt_fusion.3), kind=kOutput, calls=%fused_computation.85 | convolution fusion | flops 17196646400 | bytes 33570816 | tf_op jit(solution)/shard_map/bsd,dhe->bshe/dot_general | solution.py:43
  133.6 24.5 %fusion.68 = f32[4,512,32,64]{1,3,2,0:T(8,128)} fusion(bf16[1,2048,32,64]{1,3,2,0:T(8,128)(2,1)} %all-gather.37.cloned.1.call-done, bf16[4,512,2048]{2,1,0:T(8,128)(2,1)} %param.13, f32[2048]{0:T(1024)S(1)} %bitcast.204, f32[4,512]{1,0:T(4,128)S(1)} %add_rsqrt_fusion.3), kind=kOutput, calls=%fused_computation.89 | convolution fusion | flops 17196646400 | bytes 33570816 | tf_op jit(solution)/shard_map/bsd,dke->bske/dot_general | solution.py:46
  158.1 19.1 subtract_convert_fusion.2
  177.2 24.4 %fusion.70 = bf16[4,512,32,64]{1,3,2,0:T(8,128)(2,1)} fusion(bf16[1,2048,32,64]{1,3,2,0:T(8,128)(2,1)} %all-gather.39.cloned.1.call-done, bf16[4,512,2048]{2,1,0:T(8,128)(2,1)} %param.13, f32[2048]{0:T(1024)S(1)} %bitcast.205, f32[4,512]{1,0:T(4,128)S(1)} %add_rsqrt_fusion.3), kind=kOutput, calls=%fused_computation.99 | convolution fusion | flops 17200840704 | bytes 25182208 | tf_op jit(solution)/shard_map/bsd,dke->bske/dot_general | solution.py:48
  201.7 51.2 %fusion.2 = (f32[4,32,512]{2,1,0:T(8,128)S(1)}, f32[4,32,512,512]{3,2,1,0:T(8,128)}) fusion(pred[4,512,512]{1,2,0:T(8,128)(4,1)S(1)} %broadcast_and_fusion, bf16[4,512,32,32]{1,3,2,0:T(8,128)(2,1)} %get-tuple-element.8, bf16[4,512,32,32]{1,3,2,0:T(8,128)(2,1)} %get-tuple-element.7, bf16[4,512,32,32]{1,3,2,0:T(8,128)(2,1)} %get-tuple-element.27, ...), kind=kOutput, calls=%fused_computation.8 | convolution fusion | flops 4429119488 | bytes 152305664 | tf_op jit(solution)/shard_map/bskgd,btkd->bkgst/dot_general | solution.py:49
  252.9 41.1 %fusion = f32[4,32,512]{2,1,0:T(8,128)S(1)} fusion(f32[4,32,512,512]{3,2,1,0:T(8,128)} %get-tuple-element.36, f32[4,32,512]{2,1,0:T(8,128)S(1)} %get-tuple-element.35, pred[4,512,512]{1,2,0:T(8,128)(4,1)S(1)} %broadcast_and_fusion), kind=kLoop, calls=%fused_computation.6 | loop fusion | flops 134152192 | bytes 135790592 | tf_op jit(solution)/shard_map/reduce_sum | solution.py:57
  294.0 54.7 %fusion.76 = bf16[4,32,64,512]{3,2,1,0:T(8,128)(2,1)} fusion(bf16[4,512,32,64]{1,3,2,0:T(8,128)(2,1)} %fusion.70, f32[4,32,512]{2,1,0:T(8,128)S(1)} %fusion, f32[4,32,512]{2,1,0:T(8,128)S(1)} %get-tuple-element.35, f32[4,32,512,512]{3,2,1,0:T(8,128)} %get-tuple-element.36, pred[4,512,512]{1,2,0:T(8,128)(4,1)S(1)} %broadcast_and_fusion), kind=kOutput, calls=%fused_computation.101 | convolution fusion | flops 4466933760 | bytes 152567808 | tf_op jit(solution)/shard_map/bkgst,btkd->bskgd/dot_general | solution.py:58
  348.7 26.0 %fusion.24 = (f32[4,512]{1,0:T(4,128)S(1)}, bf16[4,512,2048]{2,1,0:T(8,128)(2,1)}) fusion(bf16[4,512,2048]{1,2,0:T(8,128)(2,1)} %bitcast.207, bf16[1,2048,2048]{2,1,0:T(8,128)(2,1)} %all-gather.43.cloned.1.call-done, bf16[4,512,2048]{2,1,0:T(8,128)(2,1)} %param.13), kind=kOutput, calls=%fused_computation.44 | convolution fusion | flops 17205032960 | bytes 33562624 | tf_op jit(solution)/shard_map/bsh,hd->bsd/dot_general | solution.py:60
  375.1 79.7 %fusion.16 = f32[4,512,8192]{2,1,0:T(8,128)} fusion(bf16[1,2048,8192]{2,1,0:T(8,128)(2,1)} %all-gather.47.cloned.1.call-done, bf16[4,512,2048]{2,1,0:T(8,128)(2,1)} %get-tuple-element.38, f32[2048]{0:T(1024)S(1)} %bitcast.201, f32[4,512]{1,0:T(4,128)S(1)} %add_rsqrt_fusion.2), kind=kOutput, calls=%fused_computation.24 | convolution fusion | flops 68736253952 | bytes 109068288 | tf_op jit(solution)/shard_map/bsd,df->bsf/dot_general | solution.py:64
  454.8 77.2 %all-gather.45.cloned.1.call-done = bf16[1,2048,8192]{2,1,0:T(8,128)(2,1)} async-done(((bf16[1,256,8192]{2,1,0:T(8,128)(2,1)}), bf16[1,2048,8192]{2,1,0:T(8,128)(2,1)}) %all-gather.45.cloned.1.call-update) | async-done | bytes 33554448 | tf_op jit(solution)/shard_map/all_gather | solution.py:82
  532.0 91.5 %multiply_convert_fusion.5.clone.4 = bf16[4,512,8192]{2,1,0:T(8,128)(2,1)} fusion(f32[4,512,8192]{2,1,0:T(8,128)} %fusion.16, bf16[1,2048,8192]{2,1,0:T(8,128)(2,1)} %all-gather.45.cloned.1.call-done, bf16[4,512,2048]{2,1,0:T(8,128)(2,1)} %get-tuple-element.38, f32[2048]{0:T(1024)S(1)} %bitcast.202, ...), kind=kOutput, calls=%fused_computation.15.clone.clone.clone.clone.clone.clone.1 | convolution fusion | flops 68836917248 | bytes 142622720 | tf_op jit(solution)/shard_map/bsd,df->bsf/dot_general | solution.py:63
  623.5 65.6 %all-gather.49.cloned.1.call-done = bf16[1,8192,2048]{2,1,0:T(8,128)(2,1)} async-done(((bf16[1,1024,2048]{2,1,0:T(8,128)(2,1)}), bf16[1,8192,2048]{2,1,0:T(8,128)(2,1)}) %all-gather.49.cloned.1.call-update) | async-done | bytes 33554448 | tf_op jit(solution)/shard_map/all_gather | solution.py:82
  689.1 85.1 %fusion.28 = (f32[4,512]{1,0:T(4,128)S(1)}, bf16[4,512,2048]{2,1,0:T(8,128)(2,1)}) fusion(bf16[1,8192,2048]{2,1,0:T(8,128)(2,1)} %all-gather.49.cloned.1.call-done, bf16[4,512,2048]{2,1,0:T(8,128)(2,1)} %get-tuple-element.38, bf16[4,512,8192]{2,1,0:T(8,128)(2,1)} %multiply_convert_fusion.5.clone.4), kind=kOutput, calls=%fused_computation.48 | convolution fusion | flops 68744642560 | bytes 83894272 | tf_op jit(solution)/shard_map/bsf,fd->bsd/dot_general | solution.py:66
  774.2 24.5 %fusion.60 = f32[4,512,32,64]{1,3,2,0:T(8,128)} fusion(bf16[1,2048,32,64]{1,3,2,0:T(8,128)(2,1)} %all-gather.51.cloned.1.call-done, bf16[4,512,2048]{2,1,0:T(8,128)(2,1)} %get-tuple-element.40, f32[2048]{0:T(1024)S(1)} %bitcast.198, f32[4,512]{1,0:T(4,128)S(1)} %add_rsqrt_fusion.1), kind=kOutput, calls=%fused_computation.81 | convolution fusion | flops 17196646400 | bytes 33570816 | tf_op jit(solution)/shard_map/bsd,dke->bske/dot_general | solution.py:46
  798.7 24.7 %fusion.56 = f32[4,512,32,64]{1,3,2,0:T(8,128)} fusion(bf16[1,2048,32,64]{1,3,2,0:T(8,128)(2,1)} %all-gather.55.cloned.1.call-done, bf16[4,512,2048]{2,1,0:T(8,128)(2,1)} %get-tuple-element.40, f32[2048]{0:T(1024)S(1)} %bitcast.199, f32[4,512]{1,0:T(4,128)S(1)} %add_rsqrt_fusion.1), kind=kOutput, calls=%fused_computation.77 | convolution fusion | flops 17196646400 | bytes 33570816 | tf_op jit(solution)/shard_map/bsd,dhe->bshe/dot_general | solution.py:43
  823.5 19.0 subtract_convert_fusion
  842.5 1.8 all-gather.53.cloned.1.call-done
  844.3 23.8 %fusion.73 = bf16[4,512,32,64]{1,3,2,0:T(8,128)(2,1)} fusion(bf16[1,2048,32,64]{1,3,2,0:T(8,128)(2,1)} %all-gather.53.cloned.1.call-done, bf16[4,512,2048]{2,1,0:T(8,128)(2,1)} %get-tuple-element.40, f32[2048]{0:T(1024)S(1)} %bitcast.200, f32[4,512]{1,0:T(4,128)S(1)} %add_rsqrt_fusion.1), kind=kOutput, calls=%fused_computation.100 | convolution fusion | flops 17200840704 | bytes 25182208 | tf_op jit(solution)/shard_map/bsd,dke->bske/dot_general | solution.py:48
  868.1 51.6 %fusion.3 = (f32[4,32,512]{2,1,0:T(8,128)S(1)}, f32[4,32,512,512]{3,2,1,0:T(8,128)}) fusion(pred[4,512,512]{1,2,0:T(8,128)(4,1)S(1)} %copy-done.5, bf16[4,512,32,32]{1,3,2,0:T(8,128)(2,1)} %get-tuple-element.4, bf16[4,512,32,32]{1,3,2,0:T(8,128)(2,1)} %get-tuple-element.3, bf16[4,512,32,32]{1,3,2,0:T(8,128)(2,1)} %get-tuple-element.25, ...), kind=kOutput, calls=%fused_computation.9 | convolution fusion | flops 4429119488 | bytes 152305664 | tf_op jit(solution)/shard_map/bskgd,btkd->bkgst/dot_general | solution.py:49
  919.7 41.1 %fusion.1 = f32[4,32,512]{2,1,0:T(8,128)S(1)} fusion(f32[4,32,512,512]{3,2,1,0:T(8,128)} %get-tuple-element.42, f32[4,32,512]{2,1,0:T(8,128)S(1)} %get-tuple-element.41, pred[4,512,512]{1,2,0:T(8,128)(4,1)S(1)} %copy-done.5), kind=kLoop, calls=%fused_computation.7 | loop fusion | flops 134152192 | bytes 135790592 | tf_op jit(solution)/shard_map/reduce_sum | solution.py:57
  960.9 54.5 %fusion.79 = bf16[4,32,64,512]{3,2,1,0:T(8,128)(2,1)} fusion(bf16[4,512,32,64]{1,3,2,0:T(8,128)(2,1)} %fusion.73, f32[4,32,512]{2,1,0:T(8,128)S(1)} %fusion.1, f32[4,32,512]{2,1,0:T(8,128)S(1)} %get-tuple-element.41, f32[4,32,512,512]{3,2,1,0:T(8,128)} %get-tuple-element.42, pred[4,512,512]{1,2,0:T(8,128)(4,1)S(1)} %copy-done.5), kind=kOutput, calls=%fused_computation.102 | convolution fusion | flops 4466933760 | bytes 152567808 | tf_op jit(solution)/shard_map/bkgst,btkd->bskgd/dot_general | solution.py:58
  1015.4 26.2 %fusion.32 = (f32[4,512]{1,0:T(4,128)S(1)}, bf16[4,512,2048]{2,1,0:T(8,128)(2,1)}) fusion(bf16[4,512,2048]{1,2,0:T(8,128)(2,1)} %bitcast.206, bf16[1,2048,2048]{2,1,0:T(8,128)(2,1)} %all-gather.57.cloned.1.call-done, bf16[4,512,2048]{2,1,0:T(8,128)(2,1)} %get-tuple-element.40), kind=kOutput, calls=%fused_computation.52 | convolution fusion | flops 17205032960 | bytes 33562624 | tf_op jit(solution)/shard_map/bsh,hd->bsd/dot_general | solution.py:60
  1041.6 9.8 all-gather.61.cloned.1.call-done
  1051.4 79.5 %fusion.10 = f32[4,512,8192]{2,1,0:T(8,128)} fusion(bf16[1,2048,8192]{2,1,0:T(8,128)(2,1)} %all-gather.61.cloned.1.call-done, bf16[4,512,2048]{2,1,0:T(8,128)(2,1)} %get-tuple-element.44, f32[2048]{0:T(1024)S(1)} %bitcast.196, f32[4,512]{1,0:T(4,128)S(1)} %add_rsqrt_fusion), kind=kOutput, calls=%fused_computation.18 | convolution fusion | flops 68736253952 | bytes 109068288 | tf_op jit(solution)/shard_map/bsd,df->bsf/dot_general | solution.py:64
  1130.9 77.5 %all-gather.59.cloned.1.call-done = bf16[1,2048,8192]{2,1,0:T(8,128)(2,1)} async-done(((bf16[1,256,8192]{2,1,0:T(8,128)(2,1)}), bf16[1,2048,8192]{2,1,0:T(8,128)(2,1)}) %all-gather.59.cloned.1.call-update) | async-done | bytes 33554448 | tf_op jit(solution)/shard_map/all_gather | solution.py:82
  1208.5 91.3 %multiply_convert_fusion.8 = bf16[4,512,8192]{2,1,0:T(8,128)(2,1)} fusion(f32[4,512,8192]{2,1,0:T(8,128)} %fusion.10, bf16[1,2048,8192]{2,1,0:T(8,128)(2,1)} %all-gather.59.cloned.1.call-done, bf16[4,512,2048]{2,1,0:T(8,128)(2,1)} %get-tuple-element.44, f32[2048]{0:T(1024)S(1)} %bitcast.197, f32[4,512]{1,0:T(4,128)S(1)} %add_rsqrt_fusion), kind=kOutput, calls=%fused_computation.14.clone.clone.1 | convolution fusion | flops 68836917248 | bytes 142622720 | tf_op jit(solution)/shard_map/bsd,df->bsf/dot_general | solution.py:63
  1299.8 65.6 %all-gather.63.cloned.1.call-done = bf16[1,8192,2048]{2,1,0:T(8,128)(2,1)} async-done(((bf16[1,1024,2048]{2,1,0:T(8,128)(2,1)}), bf16[1,8192,2048]{2,1,0:T(8,128)(2,1)}) %all-gather.63.cloned.1.call-update) | async-done | bytes 33554448 | tf_op jit(solution)/shard_map/all_gather | solution.py:82
  1365.4 79.7 %fusion.8 = f32[4,512,2048]{2,1,0:T(8,128)} fusion(bf16[1,8192,2048]{2,1,0:T(8,128)(2,1)} %all-gather.63.cloned.1.call-done, bf16[4,512,8192]{2,1,0:T(8,128)(2,1)} %multiply_convert_fusion.8), kind=kOutput, calls=%fused_computation.16 | convolution fusion | flops 68719476736 | bytes 83886080 | tf_op jit(solution)/shard_map/bsf,fd->bsd/dot_general | solution.py:66
  1445.1 7.6 fusion.36
  1453.2 14.7 pad_maximum_fusion
  1468.0 6.5 maximum_maximum_fusion
  1474.5 757.7 %all-gather.35.cloned.1.call-done = bf16[49152,2048]{1,0:T(8,128)(2,1)} async-done(((bf16[6144,2048]{1,0:T(8,128)(2,1)}), bf16[49152,2048]{1,0:T(8,128)(2,1)}) %all-gather.35.cloned.1.call-update) | async-done | bytes 201326608 | tf_op jit(solution)/shard_map/all_gather | solution.py:90
  2232.3 69.8 %fusion.124 = f32[4,49152]{1,0:T(4,128)} fusion(bf16[49152,2048]{1,0:T(8,128)(2,1)} %all-gather.35.cloned.1.call-done, f32[2048]{0:T(1024)S(1)} %bitcast.195, f32[4]{0:T(128)S(1)} %add_rsqrt_fusion.4, bf16[4,1,2048]{2,1,0:T(2,128)(2,1)S(1)} %fusion.36), kind=kOutput, calls=%fused_computation.115 | convolution fusion | flops 805339136 | bytes 202137616 | tf_op jit(solution)/shard_map/bd,vd->bv/dot_general | solution.py:91
  (101 shorter events, 9.4 us)
Async XLA Ops:
  7.2 9.8 copy-start.8
  7.2 101.6 %all-gather.41.cloned.1.call-start = ((), (), s32[]{:S(2)}) async-start(), calls=%async_computation.3 | async-start | bytes 9437184 | tf_op jit(solution)/shard_map/all_gather | solution.py:82
  10.5 123.1 %all-gather.37.cloned.1.call-start = ((), (), s32[]{:S(2)}) async-start(), calls=%async_computation.1 | async-start | bytes 9437184 | tf_op jit(solution)/shard_map/all_gather | solution.py:82
  13.8 163.5 %all-gather.39.cloned.1.call-start = ((), (), s32[]{:S(2)}) async-start(), calls=%async_computation.2 | async-start | bytes 9437184 | tf_op jit(solution)/shard_map/all_gather | solution.py:82
  17.0 331.7 %all-gather.43.cloned.1.call-start = ((), (), s32[]{:S(2)}) async-start(), calls=%async_computation.4 | async-start | bytes 9437184 | tf_op jit(solution)/shard_map/all_gather | solution.py:82
  18.5 356.6 %all-gather.47.cloned.1.call-start = ((), (), s32[]{:S(2)}) async-start(), calls=%async_computation.6 | async-start | bytes 37748736 | tf_op jit(solution)/shard_map/all_gather | solution.py:82
  24.6 507.4 %all-gather.45.cloned.1.call-start = ((), (), s32[]{:S(2)}) async-start(), calls=%async_computation.5 | async-start | bytes 37748736 | tf_op jit(solution)/shard_map/all_gather | solution.py:82
  30.7 658.4 %all-gather.49.cloned.1.call-start = ((), (), s32[]{:S(2)}) async-start(), calls=%async_computation.7 | async-start | bytes 37748736 | tf_op jit(solution)/shard_map/all_gather | solution.py:82
  36.9 737.3 %all-gather.51.cloned.1.call-start = ((), (), s32[]{:S(2)}) async-start(), calls=%async_computation.8 | async-start | bytes 9437184 | tf_op jit(solution)/shard_map/all_gather | solution.py:82
  37.6 761.1 %all-gather.55.cloned.1.call-start = ((), (), s32[]{:S(2)}) async-start(), calls=%async_computation.10 | async-start | bytes 9437184 | tf_op jit(solution)/shard_map/all_gather | solution.py:82
  38.4 805.9 %all-gather.53.cloned.1.call-start = ((), (), s32[]{:S(2)}) async-start(), calls=%async_computation.9 | async-start | bytes 9437184 | tf_op jit(solution)/shard_map/all_gather | solution.py:82
  38.9 976.5 %all-gather.57.cloned.1.call-start = ((), (), s32[]{:S(2)}) async-start(), calls=%async_computation.11 | async-start | bytes 9437184 | tf_op jit(solution)/shard_map/all_gather | solution.py:82
  39.7 1011.7 %all-gather.61.cloned.1.call-start = ((), (), s32[]{:S(2)}) async-start(), calls=%async_computation.13 | async-start | bytes 37748736 | tf_op jit(solution)/shard_map/all_gather | solution.py:82
  40.3 1168.2 %all-gather.59.cloned.1.call-start = ((), (), s32[]{:S(2)}) async-start(), calls=%async_computation.12 | async-start | bytes 37748736 | tf_op jit(solution)/shard_map/all_gather | solution.py:82
  40.3 1.9 copy-start.18
  40.3 15.6 copy-start.19
  40.3 49.7 %copy-start.21 = (bf16[256]{0:T(256)(128)(2,1)S(1)}, bf16[256]{0:T(256)(128)(2,1)}, u32[]{:S(2)}) copy-start(bf16[256]{0:T(256)(128)(2,1)} %param.24) | copy-start | bytes 1540
  40.3 61.3 %copy-start.20 = (s32[4]{0:T(128)S(1)}, s32[4]{0:T(128)}, u32[]{:S(2)}) copy-start(s32[4]{0:T(128)} %param.14) | copy-start | bytes 52
  41.0 1324.4 %all-gather.63.cloned.1.call-start = ((), (), s32[]{:S(2)}) async-start(), calls=%async_computation.14 | async-start | bytes 37748736 | tf_op jit(solution)/shard_map/all_gather | solution.py:82
  41.6 2190.7 %all-gather.35.cloned.1.call-start = ((), (), s32[]{:S(2)}) async-start(), calls=%async_computation | async-start | bytes 226492416 | tf_op jit(solution)/shard_map/all_gather | solution.py:90
  107.8 50.4 %copy-start.9 = (f32[512,32]{0,1:T(8,128)}, f32[512,32]{0,1:T(8,128)S(1)}, u32[]{:S(2)}) copy-start(f32[512,32]{0,1:T(8,128)S(1)} %get-tuple-element.33) | copy-start | bytes 196612
  107.8 50.4 %copy-start.11 = (f32[512,32]{0,1:T(8,128)}, f32[512,32]{0,1:T(8,128)S(1)}, u32[]{:S(2)}) copy-start(f32[512,32]{0,1:T(8,128)S(1)} %get-tuple-element.34) | copy-start | bytes 196612
  108.7 185.3 %copy-start.4 = (pred[4,512,512]{1,2,0:T(8,128)(4,1)}, pred[4,512,512]{1,2,0:T(8,128)(4,1)S(1)}, u32[]{:S(2)}) copy-start(pred[4,512,512]{1,2,0:T(8,128)(4,1)S(1)} %broadcast_and_fusion) | copy-start | bytes 3145732
  348.7 26.4 %copy-start.17 = (f32[1,2048]{1,0:T(1,128)S(1)}, f32[1,2048]{1,0:T(1,128)}, u32[]{:S(2)}) copy-start(f32[1,2048]{1,0:T(1,128)} %convert_element_type.156) | copy-start | bytes 24580
  623.5 150.7 %copy-start.16 = (f32[1,2048]{1,0:T(1,128)S(1)}, f32[1,2048]{1,0:T(1,128)}, u32[]{:S(2)}) copy-start(f32[1,2048]{1,0:T(1,128)} %convert_element_type.157) | copy-start | bytes 24580
  798.7 24.8 %copy-start.10 = (f32[512,32]{0,1:T(8,128)S(1)}, f32[512,32]{0,1:T(8,128)}, u32[]{:S(2)}) copy-start(f32[512,32]{0,1:T(8,128)} %copy-done.9) | copy-start | bytes 196612
  798.7 24.8 %copy-start.12 = (f32[512,32]{0,1:T(8,128)S(1)}, f32[512,32]{0,1:T(8,128)}, u32[]{:S(2)}) copy-start(f32[512,32]{0,1:T(8,128)} %copy-done.11) | copy-start | bytes 196612
  842.5 25.7 %copy-start.5 = (pred[4,512,512]{1,2,0:T(8,128)(4,1)S(1)}, pred[4,512,512]{1,2,0:T(8,128)(4,1)}, u32[]{:S(2)}) copy-start(pred[4,512,512]{1,2,0:T(8,128)(4,1)} %copy-done.4) | copy-start | bytes 3145732
  1015.4 36.0 %copy-start.15 = (f32[1,2048]{1,0:T(1,128)S(1)}, f32[1,2048]{1,0:T(1,128)}, u32[]{:S(2)}) copy-start(f32[1,2048]{1,0:T(1,128)} %convert_element_type.158) | copy-start | bytes 24580
  1299.8 145.3 %copy-start.13 = (pred[4,512,1]{1,0,2:T(4,128)(4,1)S(1)}, pred[4,512,1]{1,0,2:T(4,128)(4,1)}, u32[]{:S(2)}) copy-start(pred[4,512,1]{1,0,2:T(4,128)(4,1)} %fusion.128) | copy-start | bytes 6148
  1365.4 79.7 %copy-start.6 = (bf16[4,512,2048]{2,1,0:T(8,128)(2,1)S(1)}, bf16[4,512,2048]{2,1,0:T(8,128)(2,1)}, u32[]{:S(2)}) copy-start(bf16[4,512,2048]{2,1,0:T(8,128)(2,1)} %get-tuple-element.44) | copy-start | bytes 25165828
  1445.1 8.2 copy-start.7
  1453.2 14.7 copy-start
  1453.2 14.7 copy-start.1
  1453.2 14.7 copy-start.2
  1453.2 14.7 copy-start.3
  1468.0 764.3 %copy-start.14 = (f32[8,1,256]{2,1,0:T(1,128)S(1)}, f32[8,1,256]{2,1,0:T(1,128)}, u32[]{:S(2)}) copy-start(f32[8,1,256]{2,1,0:T(1,128)} %convert_element_type.159) | copy-start | bytes 24580
Sparse Core Ops, SparseCore 0:
  10.6 52.9 all-gather.40
  66.0 50.2 all-gather.36
  118.2 49.9 all-gather.38
  169.8 48.3 all-gather.42
  219.8 155.2 all-gather.46
  376.8 155.1 all-gather.44
  533.8 155.2 all-gather.48
  690.9 49.9 all-gather.50
  742.7 49.9 all-gather.54
  794.3 49.9 all-gather.52
  846.1 48.3 all-gather.56
  896.2 155.1 all-gather.60
  1053.2 155.2 all-gather.58
  1210.1 155.2 all-gather.62
  1367.0 865.1 all-gather.34
where the time goes:
time: 2310 us
  waiting for transfers between devices  1060 us (46%)
  matrix products  995 us (43%)
  other arithmetic  151 us (7%)
  blocking collectives  56.9 us (2%)
  local copies, waits for them, and re-layouts  29.6 us (1%)
    all_gather x1, waiting for transfers between devices, device_step(): full_table = lax.all_gather(embedding, 'dp', axis=0, tiled=True)  758 us
    all_gather x14, waiting for transfers between devices, device_step(): lax.all_gather(weight_shard[layer_idx], 'dp', axis=0, tiled=True)  298 us
    dot_general x2, matrix products, decoder_layer(): jnp.einsum('bsd,df->bsf', normed_mlp, w_gate, preferred_element_type=jnp....  183 us
    dot_general x2, matrix products, decoder_layer(): jnp.einsum('bsf,fd->bsd', mlp_act, w_down, preferred_element_type=jnp.flo...  165 us
    dot_general x2, matrix products, decoder_layer(): jnp.einsum('bsd,df->bsf', normed_mlp, w_up, preferred_element_type=jnp.fl...  159 us
    dot_general x2, matrix products, decoder_layer(): jnp.einsum('bkgst,btkd->bskgd', attn_probs, value_vec, preferred_element_...  109 us
    dot_general x2, matrix products, decoder_layer(): jnp.einsum('bskgd,btkd->bkgst', query_rot, key_rot, preferred_element_typ...  103 us
    reduce_sum x2, other arithmetic, decoder_layer(): jnp.sum(exp_scores, axis=-1, keepdims=True)  82.3 us
  transfers between devices with their start and end apart: 15, of which 8 were waited for; matrix products, arithmetic and copies ran while one was open for 48% of the time, Pallas kernels for 0%

commit v1 on v0

v1 whole, which is shorter than its diff:
```python
import math
import jax
import jax.numpy as jnp
from jax import lax
from jax.sharding import PartitionSpec as P

F32 = jnp.float32
BF16 = jnp.bfloat16


def rope_tables(seq_len, head_dim):
    half_dim = head_dim // 2
    exponent = jnp.arange(half_dim, dtype=jnp.float32) * (2.0 / head_dim)
    inv_freq = 1.0 / (500000.0 ** exponent)
    wave_len = 2.0 * math.pi / inv_freq
    smooth = (8192.0 / wave_len - 1.0) / 3.0
    blended = (1.0 - smooth) * inv_freq / 8.0 + smooth * inv_freq
    scaled = jnp.where(wave_len > 8192.0, inv_freq / 8.0, jnp.where(wave_len < 2048.0, inv_freq, blended))
    angles = jnp.arange(seq_len, dtype=jnp.float32)[:, None] * scaled[None, :]
    return jnp.cos(angles), jnp.sin(angles)


def rms_norm(values, gain_f32):
    values_f32 = values.astype(F32)
    mean_sq = jnp.mean(values_f32 * values_f32, axis=-1, keepdims=True)
    return (values_f32 * lax.rsqrt(mean_sq + 1e-5) * gain_f32).astype(BF16)


def rope_bhes(x, cos_es, sin_es):
    half = x.shape[2] // 2
    low, high = x[:, :, :half], x[:, :, half:]
    return jnp.concatenate([low * cos_es - high * sin_es, high * cos_es + low * sin_es], axis=2)


def solution(mesh):
    row_spec = P(("part", "dp"))
    layer_spec = P(None, "dp")

    def device_step(hidden, prompt_lens, g_attn, w_query, w_key, w_value, w_out, g_mlp, w_gate, w_up, w_down, g_final, embedding):
        batch, seq_len, dim = hidden.shape
        heads, head_dim = w_query.shape[2], w_query.shape[3]
        n_dev = dim // w_query.shape[1]
        cos_tab, sin_tab = rope_tables(seq_len, head_dim)
        cos_es, sin_es = cos_tab.T, sin_tab.T

        def headed(w):
            return w.transpose(1, 2, 0).reshape(heads * head_dim, -1)

        gains_loc = jnp.concatenate([g_attn, g_mlp, g_final[None]], axis=0)
        w_a = jnp.concatenate([headed(w_query[0]), headed(w_key[0]), headed(w_value[0]), w_out[0].T], axis=0)
        w_a = lax.all_gather(w_a, "dp", axis=1, tiled=True)
        gains = lax.all_gather(gains_loc, "dp", axis=1, tiled=True).astype(F32)
        wg = lax.all_gather(w_gate[0], "dp", axis=0, tiled=True)
        wu = lax.all_gather(w_up[0], "dp", axis=0, tiled=True)
        wd = lax.all_gather(w_down[0], "dp", axis=0, tiled=True)
        w_b = jnp.concatenate([headed(w_key[1]), headed(w_value[1])], axis=0)
        w_b = lax.all_gather(w_b, "dp", axis=1, tiled=True)
        ga0, ga1, gm0, gm1, gf = gains[0], gains[1], gains[2], gains[3], gains[4]
        hd = heads * head_dim

        normed = rms_norm(hidden, ga0)

        def project(a, w_t):
            return jnp.einsum("kd,bsd->bks", w_t, a, preferred_element_type=F32).reshape(batch, heads, head_dim, seq_len)

        q = rope_bhes(project(normed, w_a[:hd]), cos_es, sin_es).astype(BF16)
        k0 = rope_bhes(project(normed, w_a[hd:2 * hd]), cos_es, sin_es).astype(BF16)
        v0 = project(normed, w_a[2 * hd:3 * hd]).astype(BF16)
        scores = jnp.einsum("bhes,bhet->bhst", q, k0, preferred_element_type=F32) * head_dim ** -0.5
        positions = jnp.arange(seq_len)
        in_prompt = positions[None, :] < prompt_lens[:, None]
        allowed = (positions[None, :] <= positions[:, None])[None] & in_prompt[:, None, :]
        scores = jnp.where(allowed[:, None], scores, -jnp.inf)
        exp_scores = jnp.exp(scores - jnp.max(scores, axis=-1, keepdims=True))
        probs = (exp_scores / jnp.sum(exp_scores, axis=-1, keepdims=True)).astype(BF16)
        attended = jnp.einsum("bhet,bhst->bhes", v0, probs, preferred_element_type=F32)
        attended = attended.astype(BF16).reshape(batch, hd, seq_len)
        proj = jnp.einsum("bks,dk->bsd", attended, w_a[3 * hd:], preferred_element_type=F32)
        mid = (hidden.astype(F32) + proj).astype(BF16)
        normed_mlp = rms_norm(mid, gm0)
        gate_val = jnp.einsum("bsd,df->bsf", normed_mlp, wg, preferred_element_type=F32)
        up_val = jnp.einsum("bsd,df->bsf", normed_mlp, wu, preferred_element_type=F32)
        act = (jax.nn.silu(gate_val) * up_val).astype(BF16)
        down = jnp.einsum("bsf,fd->bsd", act, wd, preferred_element_type=F32)
        h1 = (mid.astype(F32) + down).astype(BF16)

        normed1 = rms_norm(h1, ga1)
        k1 = rope_bhes(project(normed1, w_b[:hd]), cos_es, sin_es).astype(BF16)
        v1 = project(normed1, w_b[hd:]).astype(BF16)

        last = prompt_lens - 1
        x = jnp.take_along_axis(h1, last[:, None, None], axis=1)[:, 0]
        me = lax.axis_index("dp")

        def spread(rows, width):
            every = lax.all_gather(rows, "dp", axis=0, tiled=True)
            return lax.dynamic_slice_in_dim(every, me * width, width, axis=1)

        def row_parallel(rows, w_loc):
            part = jnp.dot(spread(rows, w_loc.shape[0]), w_loc, preferred_element_type=F32)
            return lax.psum_scatter(part, "dp", scatter_dimension=0, tiled=True)

        a_last = rms_norm(x, ga1)
        part = jnp.einsum("bd,kd->bk", spread(a_last, dim // n_dev), headed(w_query[1]), preferred_element_type=F32)
        q1 = lax.psum_scatter(part, "dp", scatter_dimension=0, tiled=True).reshape(batch, heads, head_dim)
        half = head_dim // 2
        cos_b, sin_b = jnp.take(cos_tab, last, axis=0)[:, None], jnp.take(sin_tab, last, axis=0)[:, None]
        low, high = q1[..., :half], q1[..., half:]
        q1 = jnp.concatenate([low * cos_b - high * sin_b, high * cos_b + low * sin_b], axis=-1).astype(BF16)
        sc1 = jnp.einsum("bhe,bhet->bht", q1, k1, preferred_element_type=F32) * head_dim ** -0.5
        sc1 = jnp.where(in_prompt[:, None], sc1, -jnp.inf)
        ex1 = jnp.exp(sc1 - jnp.max(sc1, axis=-1, keepdims=True))
        pr1 = (ex1 / jnp.sum(ex1, axis=-1, keepdims=True)).astype(BF16)
        o1 = jnp.einsum("bht,bhet->bhe", pr1, v1, preferred_element_type=F32).astype(BF16).reshape(batch, hd)
        mid1 = (x.astype(F32) + row_parallel(o1, w_out[1])).astype(BF16)
        m1 = spread(rms_norm(mid1, gm1), dim // n_dev)
        ffn = w_gate.shape[2]
        parts = jnp.stack([jnp.dot(m1, w_gate[1], preferred_element_type=F32), jnp.dot(m1, w_up[1], preferred_element_type=F32)])
        sums = lax.psum_scatter(parts, "dp", scatter_dimension=2, tiled=True)
        u1 = (jax.nn.silu(sums[0]) * sums[1]).astype(BF16)
        part = jnp.dot(u1, w_down[1], preferred_element_type=F32)
        h2 = (mid1.astype(F32) + lax.psum_scatter(part, "dp", scatter_dimension=0, tiled=True)).astype(BF16)
        z = lax.all_gather(rms_norm(h2, gf), "dp", axis=0, tiled=True)
        logits = jnp.einsum("bd,vd->bv", z, embedding, preferred_element_type=F32)
        logits = lax.all_to_all(logits, "dp", split_axis=0, concat_axis=1, tiled=True)

        def cache(first, second):
            return jnp.stack([first, second]).transpose(0, 1, 4, 2, 3)

        return cache(k0, k1), cache(v0, v1), logits

    cache_spec = P(None, ("part", "dp"))
    return jax.shard_map(
        device_step,
        mesh=mesh,
        in_specs=(row_spec, row_spec) + (layer_spec,) * 9 + (P("dp"), P("dp")),
        out_specs=(cache_spec, cache_spec, row_spec),
        check_vma=False,
    )
```

time: 2310 us -> 1070 us (0.46)
  waiting for transfers between devices: 1060 us -> 275 us
  matrix products: 995 us -> 545 us
  other arithmetic: 151 us -> 66.1 us
  local copies, waits for them, and re-layouts: 29.6 us -> 101 us
    all_gather x15 -> x5, waiting for transfers between devices: 1060 us -> 157 us  [the longest x1 124 us: device_step(): w_a = lax.all_gather(w_a, 'dp', axis=1, tiled=True)]
    dot_general x20 -> x18, matrix products: 995 us -> 487 us  [the longest x5 123 us: project(): jnp.einsum('kd,bsd->bks', w_t, a, preferred_element_type=F32)]
    reduce_sum x2 -> x0, other arithmetic: 82.3 us -> none  [decoder_layer(): jnp.sum(exp_scores, axis=-1, keepdims=True)]
    unnamed x15 -> x12, waiting for transfers between devices: 4.93 us -> 85.6 us
    sub x0 -> x1, matrix products: none -> 57.5 us  [device_step(): exp_scores = jnp.exp(scores - jnp.max(scores, axis=-1, keepdims=True))]
    transpose x0 -> x3, local copies, waits for them, and re-layouts: none -> 48.9 us  [project(): jnp.einsum('kd,bsd->bks', w_t, a, preferred_element_type=F32)]
    another operation x4, other arithmetic: 59.4 us -> 25.7 us
    reduce_scatter x0 -> x1, waiting for transfers between devices: none -> 32.7 us  [device_step(): sums = lax.psum_scatter(parts, 'dp', scatter_dimension=2, tiled=True)]
  transfers between devices with their start and end apart: 15 -> 10, of which waited for: 8 -> 5; matrix products, arithmetic and copies ran while one was open for 48% -> 62% of each run, Pallas kernels for 0% -> 0%
where the time goes in v1:
time: 1070 us; the launch traced here: 1060 us
  matrix products  545 us (51%)
  waiting for transfers between devices  275 us (26%)
  local copies, waits for them, and re-layouts  101 us (9%)
  other arithmetic  66.1 us (6%)
  blocking collectives  58.9 us (6%)
  between operations  14.5 us (1%)
    all_gather x1, waiting for transfers between devices, device_step(): w_a = lax.all_gather(w_a, 'dp', axis=1, tiled=True)  124 us
    dot_general x5, matrix products, project(): jnp.einsum('kd,bsd->bks', w_t, a, preferred_element_type=F32)  123 us
    dot_general x1, matrix products, device_step(): jnp.einsum('bsd,df->bsf', normed_mlp, wg, preferred_element_type=F32)  91.2 us
    unnamed x12, waiting for transfers between devices  85.6 us
    dot_general x1, matrix products, device_step(): down = jnp.einsum('bsf,fd->bsd', act, wd, preferred_element_type=F32)  85.3 us
    dot_general x1, matrix products, device_step(): jnp.einsum('bsd,df->bsf', normed_mlp, wu, preferred_element_type=F32)  79.7 us
    sub x1, matrix products, device_step(): exp_scores = jnp.exp(scores - jnp.max(scores, axis=-1, keepdims=True))  57.5 us
    transpose x3, local copies, waits for them, and re-layouts, project(): jnp.einsum('kd,bsd->bks', w_t, a, preferred_element_type=F32)  48.9 us
  transfers between devices with their start and end apart: 10, of which 5 were waited for; matrix products, arithmetic and copies ran while one was open for 62% of the time, Pallas kernels for 0%

profile of v1, /device:TPU:0, one launch (start us, length us, event | category | flops | bytes accessed | tf_op | source)
XLA Modules:
  0.0 1062.6 jit_solution(1457953478282466026)
XLA Ops:
  7.2 3.3 fusion.133
  10.5 2.7 fusion.134
  14.3 1.3 copy.67
  15.6 3.7 pad_maximum_fusion.12
  19.4 4.6 slice.120
  24.0 4.6 slice.119
  28.8 4.8 slice.121
  33.7 1.4 pad_maximum_fusion.13
  37.3 14.5 %all_gather.30 = bf16[5,2048]{1,0:T(8,128)(2,1)S(1)} all-gather(bf16[5,256]{1,0:T(8,128)(2,1)S(1)} %pad_maximum_fusion.15), channel_id=1, replica_groups=mesh['part'=1,'dp'=8] {'dp'}, dimensions={1}, use_global_device_ids=true | all-gather | bytes 23040 | tf_op jit(solution)/shard_map/all_gather | solution.py:52
  52.4 5.1 fusion.17
  60.8 124.1 %all-gather.13.cloned.1.call-done = bf16[8192,2048]{1,0:T(8,128)(2,1)} async-done(((bf16[8192,256]{1,0:T(8,128)(2,1)}), bf16[8192,2048]{1,0:T(8,128)(2,1)}) %all-gather.13.cloned.1.call-update) | async-done | bytes 33554448 | tf_op jit(solution)/shard_map/all_gather | solution.py:51
  184.9 24.5 %fusion.38 = f32[4,2048,512]{1,2,0:T(8,128)} fusion(bf16[8192,2048]{1,0:T(8,128)(2,1)} %all-gather.13.cloned.1.call-done, bf16[4,512,2048]{2,1,0:T(8,128)(2,1)} %param.15, f32[2048]{0:T(1024)S(1)} %bitcast.208, f32[4,512]{1,0:T(4,128)S(1)} %add_rsqrt_fusion.2), kind=kOutput, calls=%fused_computation.72 | convolution fusion | flops 17196646400 | bytes 33570816 | tf_op jit(solution)/shard_map/kd,bsd->bks/dot_general | solution.py:64
  209.3 16.3 %copy.51 = f32[4,2048,512]{2,1,0:T(8,128)} copy(f32[4,2048,512]{1,2,0:T(8,128)} %fusion.38) | data formatting | bytes 33554432 | tf_op jit(solution)/shard_map/kd,bsd->bks/transpose | solution.py:64
  225.7 24.4 %fusion.39 = f32[4,2048,512]{1,2,0:T(8,128)} fusion(bf16[8192,2048]{1,0:T(8,128)(2,1)} %all-gather.13.cloned.1.call-done, bf16[4,512,2048]{2,1,0:T(8,128)(2,1)} %param.15, f32[2048]{0:T(1024)S(1)} %bitcast.209, f32[4,512]{1,0:T(4,128)S(1)} %add_rsqrt_fusion.2), kind=kOutput, calls=%fused_computation.73 | convolution fusion | flops 17196646400 | bytes 33570816 | tf_op jit(solution)/shard_map/kd,bsd->bks/dot_general | solution.py:64
  250.1 16.3 %copy.53 = f32[4,2048,512]{2,1,0:T(8,128)} copy(f32[4,2048,512]{1,2,0:T(8,128)} %fusion.39) | data formatting | bytes 33554432 | tf_op jit(solution)/shard_map/kd,bsd->bks/transpose | solution.py:64
  266.4 24.7 %convert_bitcast_fusion.1 = bf16[4,2048,512]{1,2,0:T(8,128)(2,1)} fusion(bf16[8192,2048]{1,0:T(8,128)(2,1)} %all-gather.13.cloned.1.call-done, bf16[4,512,2048]{2,1,0:T(8,128)(2,1)} %param.15, f32[2048]{0:T(1024)S(1)} %bitcast.210, f32[4,512]{1,0:T(4,128)S(1)} %add_rsqrt_fusion.2), kind=kOutput, calls=%fused_computation.68 | convolution fusion | flops 17200840704 | bytes 25182208 | tf_op jit(solution)/shard_map/kd,bsd->bks/dot_general | solution.py:64
  291.2 11.5 %copy.52 = bf16[4,2048,512]{2,1,0:T(8,128)(2,1)} copy(bf16[4,2048,512]{1,2,0:T(8,128)(2,1)} %convert_bitcast_fusion.1) | data formatting | bytes 16777216 | tf_op jit(solution)/shard_map/convert_element_type | solution.py:68
  302.6 19.0 %subtract_convert_fusion.1 = (bf16[4,32,32,512]{3,2,1,0:T(8,128)(2,1)}, bf16[4,32,32,512]{3,2,1,0:T(8,128)(2,1)}, bf16[4,32,32,512]{3,2,1,0:T(8,128)(2,1)}, bf16[4,32,32,512]{3,2,1,0:T(8,128)(2,1)}) fusion(f32[4,32,64,512]{3,2,1,0:T(8,128)} %bitcast.182, f32[32,512]{1,0:T(8,128)S(1)} %get-tuple-element.37, f32[32,512]{1,0:T(8,128)S(1)} %get-tuple-element.36, ...), kind=kLoop, calls=%fused_computation.67 | loop fusion | flops 33554432 | bytes 50462720 | tf_op jit(solution)/shard_map/convert.10
  321.6 57.5 %fusion.137 = (f32[4,32,512]{2,1,0:T(8,128)S(1)}, f32[4,32,512,512]{2,3,1,0:T(8,128)}) fusion(pred[4,512,512]{1,2,0:T(8,128)(4,1)S(1)} %broadcast_and_fusion, bf16[4,32,32,512]{3,2,1,0:T(8,128)(2,1)} %get-tuple-element.22, bf16[4,32,32,512]{3,2,1,0:T(8,128)(2,1)} %get-tuple-element.23, bf16[4,32,32,512]{3,2,1,0:T(8,128)(2,1)} %get-tuple-element.13, ...), kind=kOutput, calls=%fused_computation.183 | convolution fusion | flops 4462739968 | bytes 152305664 | tf_op jit(solution)/shard_map/sub | solution.py:74
  379.1 47.1 %fusion.37 = bf16[4,32,64,512]{3,2,1,0:T(8,128)(2,1)} fusion(bf16[4,32,64,512]{3,2,1,0:T(8,128)(2,1)} %bitcast.184, f32[4,32,512,512]{2,3,1,0:T(8,128)} %get-tuple-element.39, f32[4,32,512]{2,1,0:T(8,128)S(1)} %get-tuple-element.38), kind=kOutput, calls=%fused_computation.71 | convolution fusion | flops 4366270464 | bytes 151257088 | tf_op jit(solution)/shard_map/bhet,bhst->bhes/dot_general | solution.py:76
  426.2 26.3 %fusion.21 = (f32[4,512]{1,0:T(4,128)S(1)}, bf16[4,512,2048]{2,1,0:T(8,128)(2,1)}) fusion(bf16[4,2048,512]{2,1,0:T(8,128)(2,1)} %bitcast.211, bf16[8192,2048]{1,0:T(8,128)(2,1)} %all-gather.13.cloned.1.call-done, bf16[4,512,2048]{2,1,0:T(8,128)(2,1)} %param.15), kind=kOutput, calls=%fused_computation.36 | convolution fusion | flops 17205032960 | bytes 33562624 | tf_op jit(solution)/shard_map/bks,dk->bsd/dot_general | solution.py:78
  452.5 79.7 %fusion.10 = f32[4,512,8192]{2,1,0:T(8,128)} fusion(bf16[1,2048,8192]{2,1,0:T(8,128)(2,1)} %all-gather.19.cloned.1.call-done, bf16[4,512,2048]{2,1,0:T(8,128)(2,1)} %get-tuple-element.41, f32[2048]{0:T(1024)S(1)} %bitcast.206, f32[4,512]{1,0:T(4,128)S(1)} %add_rsqrt_fusion.1), kind=kOutput, calls=%fused_computation.17 | convolution fusion | flops 68736253952 | bytes 109068288 | tf_op jit(solution)/shard_map/bsd,df->bsf/dot_general | solution.py:82
  532.2 91.2 %multiply_convert_fusion.3.clone.4 = bf16[4,512,8192]{2,1,0:T(8,128)(2,1)} fusion(f32[4,512,8192]{2,1,0:T(8,128)} %fusion.10, bf16[1,2048,8192]{2,1,0:T(8,128)(2,1)} %all-gather.17.cloned.1.call-done, bf16[4,512,2048]{2,1,0:T(8,128)(2,1)} %get-tuple-element.41, f32[2048]{0:T(1024)S(1)} %bitcast.207, ...), kind=kOutput, calls=%fused_computation.10.clone.clone.clone.clone.clone.clone.1 | convolution fusion | flops 68836917248 | bytes 142622720 | tf_op jit(solution)/shard_map/bsd,df->bsf/dot_general | solution.py:81
  623.4 32.5 %all-gather.21.cloned.1.call-done = bf16[1,8192,2048]{2,1,0:T(8,128)(2,1)} async-done(((bf16[1,1024,2048]{2,1,0:T(8,128)(2,1)}), bf16[1,8192,2048]{2,1,0:T(8,128)(2,1)}) %all-gather.21.cloned.1.call-update) | async-done | bytes 33554448 | tf_op jit(solution)/shard_map/all_gather | solution.py:55
  655.9 85.3 %fusion.14 = (f32[4,512]{1,0:T(4,128)S(1)}, bf16[4,512,2048]{2,1,0:T(8,128)(2,1)}) fusion(bf16[1,8192,2048]{2,1,0:T(8,128)(2,1)} %all-gather.21.cloned.1.call-done, bf16[4,512,2048]{2,1,0:T(8,128)(2,1)} %get-tuple-element.41, bf16[4,512,8192]{2,1,0:T(8,128)(2,1)} %multiply_convert_fusion.3.clone.4), kind=kOutput, calls=%fused_computation.29 | convolution fusion | flops 68744642560 | bytes 83894272 | tf_op jit(solution)/shard_map/bsf,fd->bsd/dot_general | solution.py:84
  741.2 1.4 gather_fusion
  743.0 11.1 %all-gather.3 = bf16[8,4,2048]{2,1,0:T(4,128)(2,1)S(1)} all-gather(bf16[1,4,2048]{2,1,0:T(4,128)(2,1)S(1)} %fusion.108), channel_id=1, replica_groups=mesh['part'=1,'dp'=8] {'dp'}, dimensions={0}, use_global_device_ids=true | all-gather | bytes 147456 | tf_op jit(solution)/shard_map/all_gather | solution.py:96
  754.1 1.1 fusion.111
  755.4 24.6 %fusion.40 = f32[4,2048,512]{1,2,0:T(8,128)} fusion(bf16[4096,2048]{1,0:T(8,128)(2,1)} %all-gather.15.cloned.1.call-done, bf16[4,512,2048]{2,1,0:T(8,128)(2,1)} %get-tuple-element.43, f32[2048]{0:T(1024)S(1)} %bitcast.204, f32[4,512]{1,0:T(4,128)S(1)} %add_rsqrt_fusion), kind=kOutput, calls=%fused_computation.74 | convolution fusion | flops 17196646400 | bytes 33570816 | tf_op jit(solution)/shard_map/kd,bsd->bks/dot_general | solution.py:64
  780.0 16.3 %copy.56 = f32[4,2048,512]{2,1,0:T(8,128)} copy(f32[4,2048,512]{1,2,0:T(8,128)} %fusion.40) | data formatting | bytes 33554432 | tf_op jit(solution)/shard_map/kd,bsd->bks/transpose | solution.py:64
  796.3 24.6 %convert_bitcast_fusion = bf16[4,2048,512]{1,2,0:T(8,128)(2,1)} fusion(bf16[4096,2048]{1,0:T(8,128)(2,1)} %all-gather.15.cloned.1.call-done, bf16[4,512,2048]{2,1,0:T(8,128)(2,1)} %get-tuple-element.43, f32[2048]{0:T(1024)S(1)} %bitcast.205, f32[4,512]{1,0:T(4,128)S(1)} %add_rsqrt_fusion), kind=kOutput, calls=%fused_computation.63 | convolution fusion | flops 17200840704 | bytes 25182208 | tf_op jit(solution)/shard_map/kd,bsd->bks/dot_general | solution.py:64
  820.9 5.2 subtract_convert_fusion
  826.2 11.6 %copy.58 = bf16[4,2048,512]{2,1,0:T(8,128)(2,1)} copy(bf16[4,2048,512]{1,2,0:T(8,128)(2,1)} %convert_bitcast_fusion) | data formatting | bytes 16777216 | tf_op jit(solution)/shard_map/convert_element_type | solution.py:89
  839.0 4.7 fusion.33
  843.9 5.7 fusion.81
  849.8 11.1 %all-gather.4 = bf16[8,4,2048]{2,1,0:T(4,128)(2,1)S(1)} all-gather(bf16[1,4,2048]{2,1,0:T(4,128)(2,1)S(1)} %reshape.347), channel_id=1, replica_groups=mesh['part'=1,'dp'=8] {'dp'}, dimensions={0}, use_global_device_ids=true | all-gather | bytes 147456 | tf_op jit(solution)/shard_map/all_gather | solution.py:96
  862.0 42.7 %all-reduce.9.cloned.1.call-done = f32[32,2048]{1,0:T(8,128)} async-done(((f32[32,2048]{1,0:T(8,128)}), f32[32,2048]{1,0:T(8,128)}) %all-reduce.9.cloned.1.call-update) | async-done | bytes 262160
  905.8 11.1 %all-gather.5 = bf16[8,4,2048]{2,1,0:T(4,128)(2,1)S(1)} all-gather(bf16[1,4,2048]{2,1,0:T(4,128)(2,1)S(1)} %fusion.107), channel_id=1, replica_groups=mesh['part'=1,'dp'=8] {'dp'}, dimensions={0}, use_global_device_ids=true | all-gather | bytes 147456 | tf_op jit(solution)/shard_map/all_gather | solution.py:96
  916.9 3.0 convolution_bitcast_fusion.1
  920.0 3.0 convolution_bitcast_fusion
  923.0 1.5 pad_maximum_fusion.14
  924.5 32.7 %reduce-scatter.2.cloned.1.call-done = f32[2,32,1024]{2,1,0:T(8,128)} async-done(((f32[2,32,8192]{2,1,0:T(8,128)}), f32[2,32,1024]{2,1,0:T(8,128)}) %reduce-scatter.2.cloned.1.call-update) | async-done | bytes 262160 | tf_op jit(solution)/shard_map/reduce_scatter | solution.py:119
  957.2 3.8 fusion.65
  961.1 42.7 %all-reduce.11.cloned.1.call-done = f32[32,2048]{1,0:T(8,128)} async-done(((f32[32,2048]{1,0:T(8,128)}), f32[32,2048]{1,0:T(8,128)}) %all-reduce.11.cloned.1.call-update) | async-done | bytes 262160
  1004.9 11.1 %all-gather.6 = bf16[8,4,2048]{2,1,0:T(4,128)(2,1)S(1)} all-gather(bf16[1,4,2048]{2,1,0:T(4,128)(2,1)S(1)} %fusion.109), channel_id=1, replica_groups=mesh['part'=1,'dp'=8] {'dp'}, dimensions={0}, use_global_device_ids=true | all-gather | bytes 147456 | tf_op jit(solution)/shard_map/all_gather | solution.py:123
  1016.0 12.3 %fusion.144 = f32[32,6144]{1,0:T(8,128)S(1)} fusion(bf16[32,2048]{1,0:T(8,128)(2,1)S(1)} %reshape.352, bf16[6144,2048]{1,0:T(8,128)(2,1)} %param.27), kind=kOutput, calls=%fused_computation.184 | convolution fusion | flops 805306368 | bytes 26083328 | tf_op jit(solution)/shard_map/bd,vd->bv/dot_general | solution.py:124
  1029.4 2.3 all-to-all-start
  1031.7 23.2 %maximum_bitcast_fusion = (bf16[2,4,512,32,64]{2,4,3,1,0:T(8,128)(2,1)}, bf16[2,4,512,32,64]{2,4,3,1,0:T(8,128)(2,1)}) fusion(bf16[1,4,32,32,512]{4,3,2,1,0:T(8,128)(2,1)} %bitcast.191, bf16[1,4,32,32,512]{4,3,2,1,0:T(8,128)(2,1)} %bitcast.190, bf16[1,4,32,32,512]{4,3,2,1,0:T(8,128)(2,1)} %bitcast.188, bf16[1,4,32,32,512]{4,3,2,1,0:T(8,128)(2,1)} %bitcast.189, ...), kind=kLoop, calls=%fused_computation.40 | loop fusion | flops 100663296 | bytes 67108864 | tf_op jit(solution)/shard_map/transpose | solution.py:128
  (114 shorter events, 14.8 us)
Async XLA Ops:
  7.2 7.2 slice-start
  7.2 177.7 %all-gather.13.cloned.1.call-start = ((), (), s32[]{:S(2)}) async-start(), calls=%async_computation.2 | async-start | bytes 37748736 | tf_op jit(solution)/shard_map/all_gather | solution.py:51
  7.2 6.0 copy-start.3
  19.3 433.1 %all-gather.19.cloned.1.call-start = ((), (), s32[]{:S(2)}) async-start(), calls=%async_computation.6 | async-start | bytes 37748736 | tf_op jit(solution)/shard_map/all_gather | solution.py:54
  24.0 508.3 %all-gather.17.cloned.1.call-start = ((), (), s32[]{:S(2)}) async-start(), calls=%async_computation.5 | async-start | bytes 37748736 | tf_op jit(solution)/shard_map/all_gather | solution.py:53
  28.7 6.6 copy-start.18
  28.7 8.5 copy-start.21
  28.7 8.5 copy-start.19
  28.7 8.5 copy-start.20
  28.7 627.2 %all-gather.21.cloned.1.call-start = ((), (), s32[]{:S(2)}) async-start(), calls=%async_computation.7 | async-start | bytes 37748736 | tf_op jit(solution)/shard_map/all_gather | solution.py:55
  33.6 721.7 %all-gather.15.cloned.1.call-start = ((), (), s32[]{:S(2)}) async-start(), calls=%async_computation.3 | async-start | bytes 18874368 | tf_op jit(solution)/shard_map/all_gather | solution.py:57
  35.1 802.7 %all-reduce.7.cloned.1.call-start = ((), (), s32[]{:S(2)}) async-start(), calls=%async_computation.8 | async-start | bytes 524288
  35.4 174.0 %copy-start.14 = (pred[4,512]{1,0:T(4,128)(4,1)}, pred[4,512]{1,0:T(4,128)(4,1)S(1)}, u32[]{:S(2)}) copy-start(pred[4,512]{1,0:T(4,128)(4,1)S(1)} %iota_compare_fusion.1) | copy-start | bytes 6148
  36.2 266.4 %copy-start.4 = (f32[32,512]{1,0:T(8,128)}, f32[32,512]{1,0:T(8,128)S(1)}, u32[]{:S(2)}) copy-start(f32[32,512]{1,0:T(8,128)S(1)} %get-tuple-element.36) | copy-start | bytes 196612
  36.2 266.4 %copy-start.6 = (f32[32,512]{1,0:T(8,128)}, f32[32,512]{1,0:T(8,128)S(1)}, u32[]{:S(2)}) copy-start(f32[32,512]{1,0:T(8,128)S(1)} %get-tuple-element.37) | copy-start | bytes 196612
  426.2 26.3 %copy-start.17 = (f32[1,2048]{1,0:T(1,128)S(1)}, f32[1,2048]{1,0:T(1,128)}, u32[]{:S(2)}) copy-start(f32[1,2048]{1,0:T(1,128)} %get-tuple-element.29) | copy-start | bytes 24580
  623.4 117.8 %copy-start.11 = (s32[4]{0:T(128)S(1)}, s32[4]{0:T(128)}, u32[]{:S(2)}) copy-start(s32[4]{0:T(128)} %or_bitcast_fusion) | copy-start | bytes 52
  623.4 119.3 %copy-start.16 = (pred[4]{0:T(512)(128)(4,1)S(1)}, pred[4]{0:T(512)(128)(4,1)}, u32[]{:S(2)}) copy-start(pred[4]{0:T(512)(128)(4,1)} %get-tuple-element.35) | copy-start | bytes 16
  623.4 119.5 %copy-start.10 = (f32[1,2048]{1,0:T(1,128)S(1)}, f32[1,2048]{1,0:T(1,128)}, u32[]{:S(2)}) copy-start(f32[1,2048]{1,0:T(1,128)} %get-tuple-element.28) | copy-start | bytes 24580
  623.4 130.7 %copy-start.2 = (bf16[1,256,32,64]{1,3,2,0:T(8,128)(2,1)S(1)}, bf16[1,256,32,64]{1,3,2,0:T(8,128)(2,1)}, u32[]{:S(2)}) copy-start(bf16[1,256,32,64]{1,3,2,0:T(8,128)(2,1)} %get-tuple-element.16) | copy-start | bytes 3145732
  755.3 149.4 %all-reduce.9.cloned.1.call-start = ((), (), s32[]{:S(2)}) async-start(), calls=%async_computation.9 | async-start | bytes 524288
  796.3 24.7 %copy-start = (f32[4,2048,512]{2,1,0:T(8,128)S(1)}, f32[4,2048,512]{2,1,0:T(8,128)}, u32[]{:S(2)}) copy-start(f32[4,2048,512]{2,1,0:T(8,128)} %copy.56) | copy-start | bytes 50331652
  796.3 24.7 %copy-start.5 = (f32[32,512]{1,0:T(8,128)S(1)}, f32[32,512]{1,0:T(8,128)}, u32[]{:S(2)}) copy-start(f32[32,512]{1,0:T(8,128)} %copy-done.4) | copy-start | bytes 196612
  796.3 24.7 %copy-start.7 = (f32[32,512]{1,0:T(8,128)S(1)}, f32[32,512]{1,0:T(8,128)}, u32[]{:S(2)}) copy-start(f32[32,512]{1,0:T(8,128)} %copy-done.6) | copy-start | bytes 196612
  826.2 12.7 %copy-start.12 = (f32[4,32]{1,0:T(4,128)S(1)}, f32[4,32]{1,0:T(4,128)}, u32[]{:S(2)}) copy-start(f32[4,32]{1,0:T(4,128)} %get-tuple-element.31) | copy-start | bytes 1540
  826.2 12.7 %copy-start.13 = (f32[4,32]{1,0:T(4,128)S(1)}, f32[4,32]{1,0:T(4,128)}, u32[]{:S(2)}) copy-start(f32[4,32]{1,0:T(4,128)} %get-tuple-element.32) | copy-start | bytes 1540
  837.8 5.8 copy-start.15
  843.7 17.2 %copy-start.1 = (bf16[2,256,2048]{2,1,0:T(8,128)(2,1)S(1)}, bf16[2,256,2048]{2,1,0:T(8,128)(2,1)}, u32[]{:S(2)}) copy-start(bf16[2,256,2048]{2,1,0:T(8,128)(2,1)} %param.21) | copy-start | bytes 6291460
  843.7 62.0 %copy-start.9 = (f32[1,2048]{1,0:T(1,128)S(1)}, f32[1,2048]{1,0:T(1,128)}, u32[]{:S(2)}) copy-start(f32[1,2048]{1,0:T(1,128)} %get-tuple-element.27) | copy-start | bytes 24580
  861.9 95.3 %reduce-scatter.2.cloned.1.call-start = ((), (), s32[]{:S(2)}) async-start(), calls=%async_computation.4 | async-start | bytes 2359296 | tf_op jit(solution)/shard_map/reduce_scatter | solution.py:119
  920.0 84.8 %copy-start.8 = (f32[1,2048]{1,0:T(1,128)S(1)}, f32[1,2048]{1,0:T(1,128)}, u32[]{:S(2)}) copy-start(f32[1,2048]{1,0:T(1,128)} %get-tuple-element.26) | copy-start | bytes 24580
  924.5 79.3 %all-reduce.11.cloned.1.call-start = ((), (), s32[]{:S(2)}) async-start(), calls=%async_computation.10 | async-start | bytes 524288
  1029.4 25.5 %all-to-all-start = ((f32[8,4,6144]{2,1,0:T(4,128)}), f32[8,4,6144]{2,1,0:T(4,128)S(1)}, u32[]{:S(2)}, u32[]{:S(2)}) async-start(f32[8,4,6144]{2,1,0:T(4,128)} %all_to_all.14), calls=%async_computation.1 | async-start | bytes 1572864 | tf_op jit(solution)/shard_map/all_to_all | solution.py:125
Sparse Core Ops, SparseCore 0:
  19.4 165.3 all-gather.12
  186.7 155.2 all-gather.18
  343.8 155.2 all-gather.16
  500.7 155.1 all-gather.20
  657.6 87.3 all-gather.14
  755.4 42.5 all-reduce.6
  862.1 42.5 all-reduce.8
  924.6 32.5 reduce-scatter.1
  961.2 42.5 all-reduce.10

commit v2 on v1

v2 whole, which is shorter than its diff:
```python
import functools
import math
import jax
import jax.numpy as jnp
from jax import lax
from jax.experimental import pallas as pl
from jax.experimental.pallas import tpu as pltpu
from jax.sharding import PartitionSpec as P

F32 = jnp.float32
BF16 = jnp.bfloat16
ANY = pl.BlockSpec(memory_space=pl.ANY)
VM = pl.BlockSpec(memory_space=pltpu.VMEM)
NT = (((1,), (1,)), ((), ()))


def dot(a, b):
    return jnp.dot(a, b, preferred_element_type=F32)


def dot_nt(a, b):
    return lax.dot_general(a, b, NT, preferred_element_type=F32)


def rope_tables(seq_len, head_dim):
    half_dim = head_dim // 2
    exponent = jnp.arange(half_dim, dtype=jnp.float32) * (2.0 / head_dim)
    inv_freq = 1.0 / (500000.0 ** exponent)
    wave_len = 2.0 * math.pi / inv_freq
    smooth = (8192.0 / wave_len - 1.0) / 3.0
    blended = (1.0 - smooth) * inv_freq / 8.0 + smooth * inv_freq
    scaled = jnp.where(wave_len > 8192.0, inv_freq / 8.0, jnp.where(wave_len < 2048.0, inv_freq, blended))
    angles = jnp.arange(seq_len, dtype=jnp.float32)[:, None] * scaled[None, :]
    return jnp.cos(angles), jnp.sin(angles)


def rms_norm(values, gain_f32):
    values_f32 = values.astype(F32)
    mean_sq = jnp.mean(values_f32 * values_f32, axis=-1, keepdims=True)
    return (values_f32 * lax.rsqrt(mean_sq + 1e-5) * gain_f32).astype(BF16)


ROWS = 512


def proj_body(rope, head_dim, w_ref, a_ref, cos_ref, sin_ref, *rest):
    out_ref = rest[-1]
    y = dot_nt(w_ref[...], a_ref[pl.program_id(1)])
    if not rope:
        out_ref[0, 0] = y.astype(BF16)
        return
    half = head_dim // 2
    cos, sin = cos_ref[...], sin_ref[...]
    for i in range(y.shape[0] // head_dim):
        low = y[i * head_dim:i * head_dim + half]
        high = y[i * head_dim + half:(i + 1) * head_dim]
        out_ref[0, 0, pl.ds(i * head_dim, half)] = (low * cos - high * sin).astype(BF16)
        out_ref[0, 0, pl.ds(i * head_dim + half, half)] = (high * cos + low * sin).astype(BF16)


def project(a, w, first, width, cos, sin, head_dim, rope, layers, layer, prev=None):
    b, s, d = a.shape
    grid = (width // ROWS, b)
    in_specs = [
        pl.BlockSpec((ROWS, d), lambda i, j: (first // ROWS + i, 0)),
        pl.BlockSpec((b, s, d), lambda i, j: (0, 0, 0)),
        pl.BlockSpec(cos.shape, lambda i, j: (0, 0)),
        pl.BlockSpec(sin.shape, lambda i, j: (0, 0)),
    ]
    args = [w, a, cos, sin]
    alias = {}
    if prev is not None:
        in_specs.append(ANY)
        args.append(prev)
        alias = {4: 0}
    return pl.pallas_call(
        functools.partial(proj_body, rope, head_dim),
        out_shape=jax.ShapeDtypeStruct((layers, b, width, s), BF16),
        grid=grid,
        in_specs=in_specs,
        out_specs=pl.BlockSpec((1, 1, ROWS, s), lambda i, j: (layer, j, i, 0)),
        input_output_aliases=alias,
        compiler_params=pltpu.CompilerParams(vmem_limit_bytes=40 << 20),
        cost_estimate=pl.CostEstimate(flops=2 * b * s * d * width, bytes_accessed=2 * (width * d + b * s * d + b * s * width), transcendentals=0),
        name="project",
    )(*args)


HEADS_STEP = 8


def attn_body(head_dim, lens_ref, q_ref, k_ref, v_ref, o_ref):
    s = q_ref.shape[-1]
    length = lens_ref[pl.program_id(0)]
    t_pos = lax.broadcasted_iota(jnp.int32, (s, s), 0)
    s_pos = lax.broadcasted_iota(jnp.int32, (s, s), 1)
    allowed = (t_pos <= s_pos) & (t_pos < length)
    for i in range(HEADS_STEP):
        rows = pl.ds(i * head_dim, head_dim)
        sc = lax.dot_general(k_ref[0, 0, rows], q_ref[0, 0, rows], (((0,), (0,)), ((), ())), preferred_element_type=F32)
        sc = jnp.where(allowed, sc * head_dim ** -0.5, -jnp.inf)
        ex = jnp.exp(sc - jnp.max(sc, axis=0, keepdims=True))
        p = (ex * (1.0 / jnp.sum(ex, axis=0, keepdims=True))).astype(BF16)
        o_ref[0, rows] = dot(v_ref[0, 0, rows], p).astype(BF16)


def attention(lens, q, k, v, head_dim):
    _, b, width, s = q.shape
    step = HEADS_STEP * head_dim
    spec = pl.BlockSpec((1, 1, step, s), lambda i, j, lens: (0, i, j, 0))
    return pl.pallas_call(
        functools.partial(attn_body, head_dim),
        out_shape=jax.ShapeDtypeStruct((b, width, s), BF16),
        grid_spec=pltpu.PrefetchScalarGridSpec(
            num_scalar_prefetch=1,
            grid=(b, width // step),
            in_specs=[spec, spec, spec],
            out_specs=pl.BlockSpec((1, step, s), lambda i, j, lens: (i, j, 0)),
        ),
        compiler_params=pltpu.CompilerParams(vmem_limit_bytes=40 << 20),
        cost_estimate=pl.CostEstimate(flops=4 * b * s * s * width * 8, bytes_accessed=8 * b * s * width, transcendentals=b * s * s * width // head_dim),
        name="attention",
    )(lens, q, k, v)


def last_body(head_dim, lens_ref, q_ref, k_ref, v_ref, o_ref):
    length = lens_ref[pl.program_id(0)]
    sc = dot(q_ref[0], k_ref[0, 0]) * head_dim ** -0.5
    t_pos = lax.broadcasted_iota(jnp.int32, sc.shape, 1)
    sc = jnp.where(t_pos < length, sc, -jnp.inf)
    ex = jnp.exp(sc - jnp.max(sc, axis=-1, keepdims=True))
    p = (ex / jnp.sum(ex, axis=-1, keepdims=True)).astype(BF16)
    full = dot_nt(p, v_ref[0, 0])
    head = lax.broadcasted_iota(jnp.int32, full.shape, 0)
    col = lax.broadcasted_iota(jnp.int32, full.shape, 1)
    own = (col >= head * head_dim) & (col < (head + 1) * head_dim)
    o = jnp.sum(jnp.where(own, full, 0.0), axis=0, keepdims=True)
    o_ref[0] = o.astype(BF16).astype(F32)


def last_attention(lens, q_diag, k, v, head_dim, layer):
    b, heads, width = q_diag.shape
    s = k.shape[-1]
    kv = pl.BlockSpec((1, 1, width, s), lambda i, lens: (layer, i, 0, 0))
    return pl.pallas_call(
        functools.partial(last_body, head_dim),
        out_shape=jax.ShapeDtypeStruct((b, 1, width), F32),
        grid_spec=pltpu.PrefetchScalarGridSpec(
            num_scalar_prefetch=1,
            grid=(b,),
            in_specs=[pl.BlockSpec((1, heads, width), lambda i, lens: (i, 0, 0)), kv, kv],
            out_specs=pl.BlockSpec((1, 1, width), lambda i, lens: (i, 0, 0)),
        ),
        compiler_params=pltpu.CompilerParams(vmem_limit_bytes=40 << 20),
        cost_estimate=pl.CostEstimate(flops=4 * b * s * width * heads, bytes_accessed=4 * b * s * width, transcendentals=b * s * heads),
        name="last_attention",
    )(lens, q_diag, k, v)[:, 0]


class Exchange:
    def __init__(self, n, send_sems, recv_sems):
        self.n, self.send_sems, self.recv_sems = n, send_sems, recv_sems
        self.me = lax.axis_index("dp")

    def peer(self, j):
        return lax.rem(self.me + j, self.n)

    def barrier(self):
        sem = pltpu.get_barrier_semaphore()
        for j in range(1, self.n):
            pl.semaphore_signal(sem, inc=1, device_id={"dp": self.peer(j)}, device_id_type=pl.DeviceIdType.MESH)
        pl.semaphore_wait(sem, self.n - 1)

    def copy(self, stage, j, src, dst):
        return pltpu.make_async_remote_copy(
            src_ref=src, dst_ref=dst, send_sem=self.send_sems.at[stage, j], recv_sem=self.recv_sems.at[stage, self.me],
            device_id={"dp": self.peer(j)}, device_id_type=pl.DeviceIdType.MESH)

    def arrival(self, stage, j, src, dst):
        return pltpu.make_async_remote_copy(
            src_ref=src, dst_ref=dst, send_sem=self.send_sems.at[stage, j], recv_sem=self.recv_sems.at[stage, self.peer(j)],
            device_id={"dp": self.peer(j)}, device_id_type=pl.DeviceIdType.MESH)

    def start(self, stage, src_of, dst):
        for j in range(1, self.n):
            self.copy(stage, j, src_of(j), dst).start()

    def wait(self, stage, src_of, dst_from):
        for j in range(1, self.n):
            self.arrival(stage, j, src_of(j), dst_from(self.peer(j))).wait_recv()
        for j in range(1, self.n):
            self.arrival(stage, j, src_of(j), dst_from(self.peer(j))).wait_send()


def columns(ref, index, width):
    return ref.at[:, pl.ds(pl.multiple_of(index * width, width), width)]


def spread(ex, stage, rows_ref, got_ref, lhs_ref):
    n, rows, width = got_ref.shape
    src = lambda j: columns(rows_ref, ex.peer(j), width)
    ex.start(stage, src, got_ref.at[ex.me])
    got_ref[ex.me] = columns(rows_ref, ex.me, width)[...]
    ex.wait(stage, src, lambda p: got_ref.at[p])
    for i in range(n):
        lhs_ref[pl.ds(i * rows, rows)] = got_ref[i]
    return lhs_ref[...].astype(BF16)


def reduce_rows(ex, stage, part, send_ref, got_ref):
    n, rows, _ = got_ref.shape
    for i in range(n):
        send_ref[i] = part[i * rows:(i + 1) * rows]
    src = lambda j: send_ref.at[ex.peer(j)]
    ex.start(stage, src, got_ref.at[ex.me])
    got_ref[ex.me] = send_ref[ex.me]
    ex.wait(stage, src, lambda p: got_ref.at[p])
    total = got_ref[0]
    for i in range(1, n):
        total = total + got_ref[i]
    return total


def query_body(n, a_ref, w_ref, q_ref, got, lhs, send, back, send_sems, recv_sems):
    ex = Exchange(n, send_sems, recv_sems)
    ex.barrier()
    x = spread(ex, 0, a_ref, got, lhs)
    q_ref[...] = reduce_rows(ex, 1, dot_nt(x, w_ref[...]), send, back)


def last_query(a_last, w_rows, n):
    rows, d = a_last.shape
    width, kd = w_rows.shape
    return pl.pallas_call(
        functools.partial(query_body, n),
        out_shape=jax.ShapeDtypeStruct((rows, width), F32),
        in_specs=[VM, VM],
        out_specs=VM,
        scratch_shapes=[
            pltpu.VMEM((n, rows, kd), F32), pltpu.VMEM((n * rows, kd), F32),
            pltpu.VMEM((n, rows, width), F32), pltpu.VMEM((n, rows, width), F32),
            pltpu.SemaphoreType.DMA((2, n)), pltpu.SemaphoreType.DMA((2, n)),
        ],
        compiler_params=pltpu.CompilerParams(collective_id=0, has_side_effects=True, vmem_limit_bytes=16 << 20),
        cost_estimate=pl.CostEstimate(flops=2 * n * rows * width * kd, bytes_accessed=2 * width * kd, transcendentals=0),
        name="last_query",
    )(a_last, w_rows)


GROUPS = 3
TABLE_STEP = 512


def tail_body(n, layer, o_ref, x_ref, gm_ref, gf_ref, wo_hbm, wg_hbm, wu_hbm, wd_hbm, emb_hbm, out_ref,
              wo, wg, wu, wd, emb, got, lhs, send, back, mid_ref, rows_ref, gate_send, gate_got, z_got, z_lhs,
              log_send, log_got, local_sems, send_sems, recv_sems):
    ex = Exchange(n, send_sems, recv_sems)
    me = ex.me
    loads = [
        pltpu.make_async_copy(wo_hbm.at[layer], wo, local_sems.at[0]),
        pltpu.make_async_copy(wg_hbm.at[layer], wg, local_sems.at[1]),
        pltpu.make_async_copy(wu_hbm.at[layer], wu, local_sems.at[2]),
        pltpu.make_async_copy(wd_hbm.at[layer], wd, local_sems.at[3]),
        pltpu.make_async_copy(emb_hbm, emb, local_sems.at[4]),
    ]
    for load in loads:
        load.start()
    ex.barrier()

    x = spread(ex, 0, o_ref, got, lhs)
    loads[0].wait()
    mid = (x_ref[...] + reduce_rows(ex, 1, dot(x, wo[...]), send, back)).astype(BF16).astype(F32)
    mid_ref[...] = mid

    rows_ref[...] = rms_norm(mid, gm_ref[...]).astype(F32)
    x = spread(ex, 2, rows_ref, got, lhs)
    loads[1].wait()
    loads[2].wait()
    block = wd.shape[0]

    def gate_up(p):
        cols = pl.ds(pl.multiple_of(p * block, block), block)
        return dot(x, wg[:, cols]), dot(x, wu[:, cols])

    for j in range(1, n):
        gate, up = gate_up(ex.peer(j))
        gate_send[j, 0] = gate
        gate_send[j, 1] = up
        ex.copy(3, j, gate_send.at[j], gate_got.at[me]).start()
    gate, up = gate_up(me)
    gate_got[me, 0] = gate
    gate_got[me, 1] = up
    ex.wait(3, lambda j: gate_send.at[j], lambda p: gate_got.at[p])
    gate, up = gate_got[0, 0], gate_got[0, 1]
    for i in range(1, n):
        gate = gate + gate_got[i, 0]
        up = up + gate_got[i, 1]
    act = (gate * (1.0 / (1.0 + jnp.exp(-gate))) * up).astype(BF16)

    loads[3].wait()
    h = (mid_ref[...] + reduce_rows(ex, 4, dot(act, wd[...]), send, back)).astype(BF16).astype(F32)

    rows_ref[...] = rms_norm(h, gf_ref[...]).astype(F32)
    rows = rows_ref.shape[0]
    ex.start(5, lambda j: rows_ref, z_got.at[me])
    z_got[me] = rows_ref[...]
    ex.wait(5, lambda j: rows_ref, lambda p: z_got.at[p])
    for i in range(n):
        z_lhs[pl.ds(i * rows, rows)] = z_got[i]
    z = z_lhs[...].astype(BF16)
    loads[4].wait()
    vocab = emb.shape[0]
    group = vocab // GROUPS
    for g in range(GROUPS):
        def step(c, carry):
            first = pl.multiple_of(g * group + c * TABLE_STEP, TABLE_STEP)
            part = dot_nt(z, emb[pl.ds(first, TABLE_STEP)])
            for i in range(n):
                log_send[i, :, pl.ds(first, TABLE_STEP)] = part[i * rows:(i + 1) * rows]
            return carry

        lax.fori_loop(0, group // TABLE_STEP, step, 0)
        src = lambda j, g=g: log_send.at[ex.peer(j), :, pl.ds(g * group, group)]
        dst = lambda p, g=g: log_got.at[:, pl.ds(pl.multiple_of(p * vocab + g * group, group), group)]
        ex.start(6 + g, src, dst(me))
    log_got[:, pl.ds(pl.multiple_of(me * vocab, vocab), vocab)] = log_send[me]
    for g in range(GROUPS):
        src = lambda j, g=g: log_send.at[ex.peer(j), :, pl.ds(g * group, group)]
        dst = lambda p, g=g: log_got.at[:, pl.ds(pl.multiple_of(p * vocab + g * group, group), group)]
        ex.wait(6 + g, src, dst)
    out_ref[...] = log_got[...]


def tail(o, x, gm, gf, w_out, w_gate, w_up, w_down, emb, layer, n):
    rows, d = x.shape
    kd, ffn, block, vocab = w_gate.shape[1], w_gate.shape[2], w_down.shape[1], emb.shape[0]
    stages = 6 + GROUPS
    flops = 2 * n * rows * (kd * d + 2 * kd * ffn + block * d + vocab * d)
    return pl.pallas_call(
        functools.partial(tail_body, n, layer),
        out_shape=jax.ShapeDtypeStruct((rows, n * vocab), F32),
        in_specs=[VM, VM, VM, VM] + [ANY] * 5,
        out_specs=VM,
        scratch_shapes=[
            pltpu.VMEM((kd, d), BF16), pltpu.VMEM((kd, ffn), BF16), pltpu.VMEM((kd, ffn), BF16),
            pltpu.VMEM((block, d), BF16), pltpu.VMEM((vocab, d), BF16),
            pltpu.VMEM((n, rows, kd), F32), pltpu.VMEM((n * rows, kd), F32),
            pltpu.VMEM((n, rows, d), F32), pltpu.VMEM((n, rows, d), F32),
            pltpu.VMEM((rows, d), F32), pltpu.VMEM((rows, d), F32),
            pltpu.VMEM((n, 2, n * rows, block), F32), pltpu.VMEM((n, 2, n * rows, block), F32),
            pltpu.VMEM((n, rows, d), F32), pltpu.VMEM((n * rows, d), F32),
            pltpu.VMEM((n, rows, vocab), F32), pltpu.VMEM((rows, n * vocab), F32),
            pltpu.SemaphoreType.DMA((5,)), pltpu.SemaphoreType.DMA((stages, n)), pltpu.SemaphoreType.DMA((stages, n)),
        ],
        compiler_params=pltpu.CompilerParams(collective_id=1, has_side_effects=True, vmem_limit_bytes=58 << 20),
        cost_estimate=pl.CostEstimate(flops=flops, bytes_accessed=flops // (n * rows), transcendentals=0),
        name="tail",
    )(o, x, gm, gf, w_out, w_gate, w_up, w_down, emb)


def solution(mesh):
    row_spec = P(("part", "dp"))
    layer_spec = P(None, "dp")

    def device_step(hidden, prompt_lens, g_attn, w_query, w_key, w_value, w_out, g_mlp, w_gate, w_up, w_down, g_final, embedding):
        batch, seq_len, dim = hidden.shape
        heads, head_dim = w_query.shape[2], w_query.shape[3]
        n_dev = dim // w_query.shape[1]
        cos_tab, sin_tab = rope_tables(seq_len, head_dim)
        cos_es, sin_es = cos_tab.T, sin_tab.T

        def headed(w):
            return w.transpose(1, 2, 0).reshape(heads * head_dim, -1)

        gains_loc = jnp.concatenate([g_attn, g_mlp, g_final[None]], axis=0)
        w_a = jnp.concatenate([headed(w_query[0]), headed(w_key[0]), headed(w_value[0]), w_out[0].T], axis=0)
        w_a = lax.all_gather(w_a, "dp", axis=1, tiled=True)
        gains = lax.all_gather(gains_loc, "dp", axis=1, tiled=True).astype(F32)
        wg = lax.all_gather(w_gate[0], "dp", axis=0, tiled=True)
        wu = lax.all_gather(w_up[0], "dp", axis=0, tiled=True)
        wd = lax.all_gather(w_down[0], "dp", axis=0, tiled=True)
        w_b = jnp.concatenate([headed(w_key[1]), headed(w_value[1])], axis=0)
        w_b = lax.all_gather(w_b, "dp", axis=1, tiled=True)
        ga0, ga1, gm0, gm1, gf = gains[0], gains[1], gains[2], gains[3], gains[4]
        hd = heads * head_dim

        lens = prompt_lens
        rope = (cos_es, sin_es, head_dim)
        normed = rms_norm(hidden, ga0)
        q0 = project(normed, w_a, 0, hd, *rope, True, 1, 0)
        k_cache = project(normed, w_a, hd, hd, *rope, True, 2, 0)
        v_cache = project(normed, w_a, 2 * hd, hd, *rope, False, 2, 0)
        attended = attention(lens, q0, k_cache, v_cache, head_dim)
        proj = jnp.einsum("bks,dk->bsd", attended, w_a[3 * hd:], preferred_element_type=F32)
        mid = (hidden.astype(F32) + proj).astype(BF16)
        normed_mlp = rms_norm(mid, gm0)
        gate_val = jnp.einsum("bsd,df->bsf", normed_mlp, wg, preferred_element_type=F32)
        up_val = jnp.einsum("bsd,df->bsf", normed_mlp, wu, preferred_element_type=F32)
        act = (jax.nn.silu(gate_val) * up_val).astype(BF16)
        down = jnp.einsum("bsf,fd->bsd", act, wd, preferred_element_type=F32)
        h1 = (mid.astype(F32) + down).astype(BF16)

        last = lens - 1
        x = jnp.take_along_axis(h1, last[:, None, None], axis=1)[:, 0]
        q1 = last_query(rms_norm(x, ga1).astype(F32), headed(w_query[1]), n_dev).reshape(batch, heads, head_dim)
        half = head_dim // 2
        cos_b, sin_b = jnp.take(cos_tab, last, axis=0)[:, None], jnp.take(sin_tab, last, axis=0)[:, None]
        low, high = q1[..., :half], q1[..., half:]
        q1 = jnp.concatenate([low * cos_b - high * sin_b, high * cos_b + low * sin_b], axis=-1).astype(BF16)
        own = jnp.arange(hd)[None, :] // head_dim == jnp.arange(heads)[:, None]
        q_diag = jnp.where(own[None], q1.reshape(batch, 1, hd), jnp.zeros((), BF16))

        normed1 = rms_norm(h1, ga1)
        k_cache = project(normed1, w_b, 0, hd, *rope, True, 2, 1, k_cache)
        v_cache = project(normed1, w_b, hd, hd, *rope, False, 2, 1, v_cache)

        o1 = last_attention(lens, q_diag, k_cache, v_cache, head_dim, 1)
        logits = tail(o1, x.astype(F32), gm1[None], gf[None], w_out, w_gate, w_up, w_down, embedding, 1, n_dev)

        def cache(c):
            return c.reshape(2, batch, heads, head_dim, seq_len).transpose(0, 1, 4, 2, 3)

        return cache(k_cache), cache(v_cache), logits

    cache_spec = P(None, ("part", "dp"))
    return jax.shard_map(
        device_step,
        mesh=mesh,
        in_specs=(row_spec, row_spec) + (layer_spec,) * 9 + (P("dp"), P("dp")),
        out_specs=(cache_spec, cache_spec, row_spec),
        check_vma=False,
    )
```

time: 1070 us -> 909 us (0.85)
  Pallas kernels: 0 us -> 275 us
  matrix products: 545 us -> 282 us
  local copies, waits for them, and re-layouts: 101 us -> 41.3 us
  blocking collectives: 58.9 us -> 14.5 us
  waiting for transfers between devices: 275 us -> 241 us
  other arithmetic: 66.1 us -> 33.7 us
    pallas_call x0 -> x9, Pallas kernels: none -> 275 us  [the longest x5 125 us: project(): pl.pallas_call(functools.partial(proj_body, rope, head_dim), out_shape=ja...]
    dot_general x14 -> x0, matrix products: 205 us -> none  [the longest x5 123 us: project(): jnp.einsum('kd,bsd->bks', w_t, a, preferred_element_type=F32)]
    unnamed x12 -> x5, waiting for transfers between devices: 85.6 us -> 0.08 us
    all_gather x1, waiting for transfers between devices: 0.01 us -> 60.5 us  [device_step(): wg = lax.all_gather(w_gate[0], 'dp', axis=0, tiled=True)]
    sub x1 -> x0, matrix products: 57.5 us -> none  [device_step(): exp_scores = jnp.exp(scores - jnp.max(scores, axis=-1, keepdims=True))]
    transpose x3 -> x0, local copies, waits for them, and re-layouts: 48.9 us -> none  [project(): jnp.einsum('kd,bsd->bks', w_t, a, preferred_element_type=F32)]
    all_gather x4 -> x0, blocking collectives: 44.4 us -> none  [the longest x3 33.3 us: spread(): every = lax.all_gather(rows, 'dp', axis=0, tiled=True)]
    all_gather x1, waiting for transfers between devices: 32.5 us -> 65.5 us  [device_step(): wd = lax.all_gather(w_down[0], 'dp', axis=0, tiled=True)]
  transfers between devices with their start and end apart: 10 -> 5, of which waited for: 5 -> 3; matrix products, arithmetic and copies ran while one was open for 62% -> 37% of each run, Pallas kernels for 0% -> 17%
where the time goes in v2:
time: 909 us; the launch traced here: 901 us
  matrix products  282 us (31%)
  Pallas kernels  275 us (30%)
  waiting for transfers between devices  241 us (27%)
  local copies, waits for them, and re-layouts  41.3 us (5%)
  other arithmetic  33.7 us (4%)
  blocking collectives  14.5 us (2%)
  between operations  14.3 us (2%)
    pallas_call x5, Pallas kernels, project(): pl.pallas_call(functools.partial(proj_body, rope, head_dim), out_shape=ja...  125 us
    all_gather x1, waiting for transfers between devices, device_step(): w_a = lax.all_gather(w_a, 'dp', axis=1, tiled=True)  115 us
    dot_general x1, matrix products, device_step(): jnp.einsum('bsd,df->bsf', normed_mlp, wg, preferred_element_type=F32)  91.4 us
    dot_general x1, matrix products, device_step(): down = jnp.einsum('bsf,fd->bsd', act, wd, preferred_element_type=F32)  85 us
    dot_general x1, matrix products, device_step(): jnp.einsum('bsd,df->bsf', normed_mlp, wu, preferred_element_type=F32)  79.7 us
    pallas_call x1, Pallas kernels, attention(): pl.pallas_call(functools.partial(attn_body, head_dim), out_shape=jax.Shap...  66.1 us
    all_gather x1, waiting for transfers between devices, device_step(): wd = lax.all_gather(w_down[0], 'dp', axis=0, tiled=True)  65.5 us
    pallas_call x1, Pallas kernels, tail(): pl.pallas_call(functools.partial(tail_body, n, layer), out_shape=jax.Shap...  63.9 us
  transfers between devices with their start and end apart: 5, of which 3 were waited for; matrix products, arithmetic and copies ran while one was open for 37% of the time, Pallas kernels for 17%

profile of v2, /device:TPU:0, one launch (start us, length us, event | category | flops | bytes accessed | tf_op | source)
XLA Modules:
  0.0 901.1 jit_solution(4544136089403625283)
XLA Ops:
  7.2 2.7 fusion.46
  9.9 3.1 fusion.47
  13.0 2.8 fusion.45
  15.8 1.3 slice.59
  17.1 1.3 copy.22
  18.4 3.7 pad_maximum_fusion
  22.1 4.6 slice.64
  26.9 4.6 slice.63
  31.6 4.7 slice.65
  36.4 2.7 pad_maximum_fusion.1
  39.2 0.6 compare_and_fusion
  39.8 0.3 fusion.36
  40.1 1.0 fusion.35
  41.1 14.5 %all_gather.20 = bf16[5,2048]{1,0:T(8,128)(2,1)S(1)} all-gather(bf16[5,256]{1,0:T(8,128)(2,1)S(1)} %pad_maximum_fusion.3), channel_id=1, replica_groups=mesh['part'=1,'dp'=8] {'dp'}, dimensions={1}, use_global_device_ids=true | all-gather | bytes 23040 | tf_op jit(solution)/shard_map/all_gather | solution.py:378
  55.6 0.6 fusion.48
  56.3 5.1 fusion.9
  61.4 0.5 or_bitcast_fusion
  61.9 0.6 gather_fusion.1
  62.5 0.6 gather_fusion.2
  63.1 0.7 iota_compare_fusion
  63.7 8.6 fusion.11.a_ref
  72.3 0.7 broadcast_select_fusion.3
  73.0 114.7 %all-gather.11.cloned.1.call-done.w_ref = bf16[8192,2048]{1,0:T(8,128)(2,1)} async-done(((bf16[8192,256]{1,0:T(8,128)(2,1)}), bf16[8192,2048]{1,0:T(8,128)(2,1)}) %all-gather.11.cloned.1.call-update) | async-done | bytes 33554448 | tf_op jit(solution)/shard_map/all_gather | solution.py:377
  187.7 3.4 copy-done
  191.0 25.0 %project.6.k_ref.rest_0_ = bf16[2,4,2048,512]{3,2,1,0:T(8,128)(2,1)} custom-call(bf16[8192,2048]{1,0:T(8,128)(2,1)} %all-gather.11.cloned.1.call-done.w_ref, bf16[4,512,2048]{2,1,0:T(8,128)(2,1)S(1)} %copy-done, f32[32,512]{1,0:T(8,128)S(1)} %get-tuple-element.25.cos_ref, f32[32,512]{1,0:T(8,128)S(1)} %get-tuple-element.24.sin_ref), custom_call_target="tpu_custom_call" | custom-call | flops 17179869184 | bytes 25165824 | tf_op jit(solution)/shard_map/project/pallas_call | solution.py:76
  216.1 24.7 %project.7.v_ref.rest_0_ = bf16[2,4,2048,512]{3,2,1,0:T(8,128)(2,1)} custom-call(bf16[8192,2048]{1,0:T(8,128)(2,1)} %all-gather.11.cloned.1.call-done.w_ref, bf16[4,512,2048]{2,1,0:T(8,128)(2,1)S(1)} %copy-done, f32[32,512]{1,0:T(8,128)S(1)} %get-tuple-element.25.cos_ref, f32[32,512]{1,0:T(8,128)S(1)} %get-tuple-element.24.sin_ref), custom_call_target="tpu_custom_call" | custom-call | flops 17179869184 | bytes 25165824 | tf_op jit(solution)/shard_map/project/pallas_call | solution.py:76
  240.7 26.0 %project.5.q_ref = bf16[1,4,2048,512]{3,2,1,0:T(8,128)(2,1)S(1)} custom-call(bf16[8192,2048]{1,0:T(8,128)(2,1)} %all-gather.11.cloned.1.call-done.w_ref, bf16[4,512,2048]{2,1,0:T(8,128)(2,1)} %fusion.11.a_ref, f32[32,512]{1,0:T(8,128)S(1)} %get-tuple-element.25.cos_ref, f32[32,512]{1,0:T(8,128)S(1)} %get-tuple-element.24.sin_ref), custom_call_target="tpu_custom_call" | custom-call | flops 17179869184 | bytes 25165824 | tf_op jit(solution)/shard_map/project/pallas_call | solution.py:76
  266.8 3.2 copy-done.8
  270.0 66.1 %attention.1 = bf16[4,2048,512]{2,1,0:T(8,128)(2,1)S(1)} custom-call(s32[4]{0:T(128)S(1)} %copy-done.6, bf16[1,4,2048,512]{3,2,1,0:T(8,128)(2,1)} %copy-done.8, bf16[2,4,2048,512]{3,2,1,0:T(8,128)(2,1)} %project.6.k_ref.rest_0_, bf16[2,4,2048,512]{3,2,1,0:T(8,128)(2,1)} %project.7.v_ref.rest_0_), custom_call_target="tpu_custom_call" | custom-call | flops 68719476736 | bytes 33554432 | tf_op jit(solution)/shard_map/attention/pallas_call | solution.py:111
  336.1 25.4 %fusion.13 = (f32[4,512]{1,0:T(4,128)S(1)}, bf16[4,512,2048]{2,1,0:T(8,128)(2,1)}) fusion(bf16[4,2048,512]{2,1,0:T(8,128)(2,1)S(1)} %attention.1, bf16[8192,2048]{1,0:T(8,128)(2,1)} %all-gather.11.cloned.1.call-done.w_ref, bf16[4,512,2048]{2,1,0:T(8,128)(2,1)S(1)} %bitcast.91), kind=kOutput, calls=%fused_computation.25 | convolution fusion | flops 17205032960 | bytes 33562624 | tf_op jit(solution)/shard_map/bks,dk->bsd/dot_general | solution.py:394
  361.6 79.7 %fusion.2 = f32[4,512,8192]{2,1,0:T(8,128)} fusion(bf16[1,2048,8192]{2,1,0:T(8,128)(2,1)} %all-gather.15.cloned.1.call-done, bf16[4,512,2048]{2,1,0:T(8,128)(2,1)} %get-tuple-element.27, f32[2048]{0:T(1024)S(1)} %bitcast.104, f32[4,512]{1,0:T(4,128)S(1)} %add_rsqrt_fusion.1), kind=kOutput, calls=%fused_computation.6 | convolution fusion | flops 68736253952 | bytes 109068288 | tf_op jit(solution)/shard_map/bsd,df->bsf/dot_general | solution.py:398
  441.3 60.5 %all-gather.13.cloned.1.call-done = bf16[1,2048,8192]{2,1,0:T(8,128)(2,1)} async-done(((bf16[1,256,8192]{2,1,0:T(8,128)(2,1)}), bf16[1,2048,8192]{2,1,0:T(8,128)(2,1)}) %all-gather.13.cloned.1.call-update) | async-done | bytes 33554448 | tf_op jit(solution)/shard_map/all_gather | solution.py:379
  501.8 91.4 %multiply_convert_fusion.3.clone.4 = bf16[4,512,8192]{2,1,0:T(8,128)(2,1)} fusion(f32[4,512,8192]{2,1,0:T(8,128)} %fusion.2, bf16[1,2048,8192]{2,1,0:T(8,128)(2,1)} %all-gather.13.cloned.1.call-done, bf16[4,512,2048]{2,1,0:T(8,128)(2,1)} %get-tuple-element.27, f32[2048]{0:T(1024)S(1)} %bitcast.105, ...), kind=kOutput, calls=%fused_computation.3.clone.clone.clone.clone.clone.clone.1 | convolution fusion | flops 68836917248 | bytes 142622720 | tf_op jit(solution)/shard_map/bsd,df->bsf/dot_general | solution.py:397
  593.2 65.5 %all-gather.17.cloned.1.call-done = bf16[1,8192,2048]{2,1,0:T(8,128)(2,1)} async-done(((bf16[1,1024,2048]{2,1,0:T(8,128)(2,1)}), bf16[1,8192,2048]{2,1,0:T(8,128)(2,1)}) %all-gather.17.cloned.1.call-update) | async-done | bytes 33554448 | tf_op jit(solution)/shard_map/all_gather | solution.py:381
  658.7 85.0 %fusion.6 = (f32[4,512]{1,0:T(4,128)S(1)}, bf16[4,512,2048]{2,1,0:T(8,128)(2,1)}) fusion(bf16[1,8192,2048]{2,1,0:T(8,128)(2,1)} %all-gather.17.cloned.1.call-done, bf16[4,512,2048]{2,1,0:T(8,128)(2,1)} %get-tuple-element.27, bf16[4,512,8192]{2,1,0:T(8,128)(2,1)} %multiply_convert_fusion.3.clone.4), kind=kOutput, calls=%fused_computation.18 | convolution fusion | flops 68744642560 | bytes 83894272 | tf_op jit(solution)/shard_map/bsf,fd->bsd/dot_general | solution.py:400
  743.8 1.4 gather_fusion
  745.2 0.2 multiply_reduce_fusion
  745.5 10.3 %last_query.1 = f32[4,2048]{1,0:T(4,128)S(1)} custom-call(f32[4,2048]{1,0:T(4,128)S(1)} %fusion.38.a_ref, bf16[2048,256]{1,0:T(8,128)(2,1)S(1)} %bitcast.89), custom_call_target="tpu_custom_call" | custom-call | flops 33554432 | bytes 1048576 | tf_op jit(solution)/shard_map/last_query/pallas_call | solution.py:234
  755.8 0.1 reshape.188
  756.2 0.7 fusion.44.x_ref
  756.9 8.6 fusion.8.a_ref
  765.5 3.4 copy-done.1
  768.9 24.7 %project.9.v_ref = bf16[2,4,2048,512]{3,2,1,0:T(8,128)(2,1)} custom-call(bf16[4096,2048]{1,0:T(8,128)(2,1)} %all-gather.9.cloned.1.call-done.w_ref, bf16[4,512,2048]{2,1,0:T(8,128)(2,1)S(1)} %copy-done.1, f32[32,512]{1,0:T(8,128)S(1)} %copy-done.5, f32[32,512]{1,0:T(8,128)S(1)} %copy-done.3, ...), custom_call_target="tpu_custom_call", output_to_operand_aliasing={{}: (4, {})} | custom-call | flops 17179869184 | bytes 25165824 | tf_op jit(solution)/shard_map/project/pallas_call | solution.py:76
  793.6 25.0 %project.8.k_ref = bf16[2,4,2048,512]{3,2,1,0:T(8,128)(2,1)} custom-call(bf16[4096,2048]{1,0:T(8,128)(2,1)} %all-gather.9.cloned.1.call-done.w_ref, bf16[4,512,2048]{2,1,0:T(8,128)(2,1)S(1)} %copy-done.1, f32[32,512]{1,0:T(8,128)S(1)} %copy-done.5, f32[32,512]{1,0:T(8,128)S(1)} %copy-done.3, ...), custom_call_target="tpu_custom_call", output_to_operand_aliasing={{}: (4, {})} | custom-call | flops 17179869184 | bytes 25165824 | tf_op jit(solution)/shard_map/project/pallas_call | solution.py:76
  818.5 9.2 %last_attention.1 = f32[4,1,2048]{2,1,0:T(1,128)S(1)} custom-call(s32[4]{0:T(128)S(1)} %copy-done.7, bf16[4,32,2048]{2,1,0:T(8,128)(2,1)S(1)} %broadcast_select_fusion.q_ref, bf16[2,4,2048,512]{3,2,1,0:T(8,128)(2,1)} %project.8.k_ref, bf16[2,4,2048,512]{3,2,1,0:T(8,128)(2,1)} %project.9.v_ref), custom_call_target="tpu_custom_call" | custom-call | flops 536870912 | bytes 16777216 | tf_op jit(solution)/shard_map/last_attention/pallas_call | solution.py:145
  827.7 0.6 copy.24
  828.4 63.9 %tail.1 = f32[4,49152]{1,0:T(4,128)} custom-call(f32[4,2048]{1,0:T(4,128)} %bitcast.100, f32[4,2048]{1,0:T(4,128)} %fusion.44.x_ref, f32[1,2048]{1,0:T(1,128)} %get-tuple-element.15.gm_ref, f32[1,2048]{1,0:T(1,128)} %get-tuple-element.14.gf_ref, bf16[2,256,2048]{2,1,0:T(8,128)(2,1)} %wo_hbm.1, bf16[2,256,8192]{2,1,0:T(8,128)(2,1)} %wg_hbm.1, ...), custom_call_target="tpu_custom_call" | custom-call | flops 1241513984 | bytes 38797312 | tf_op jit(solution)/shard_map/tail/pallas_call | solution.py:339
  892.3 2.1 copy.28
  (69 shorter events, 0.9 us)
Async XLA Ops:
  7.2 180.5 %all-gather.11.cloned.1.call-start = ((), (), s32[]{:S(2)}) async-start(), calls=%async_computation.1 | async-start | bytes 37748736 | tf_op jit(solution)/shard_map/all_gather | solution.py:377
  22.1 339.5 %all-gather.15.cloned.1.call-start = ((), (), s32[]{:S(2)}) async-start(), calls=%async_computation.3 | async-start | bytes 37748736 | tf_op jit(solution)/shard_map/all_gather | solution.py:380
  26.8 12.4 %copy-start.6 = (s32[4]{0:T(128)S(1)}, s32[4]{0:T(128)}, u32[]{:S(2)}) copy-start(s32[4]{0:T(128)} %lens_ref.3) | copy-start | bytes 52
  26.8 14.3 %copy-start.18 = (bf16[256]{0:T(256)(128)(2,1)S(1)}, bf16[256]{0:T(256)(128)(2,1)}, u32[]{:S(2)}) copy-start(bf16[256]{0:T(256)(128)(2,1)} %param.26) | copy-start | bytes 1540
  26.8 14.3 %copy-start.16 = (bf16[2,256]{1,0:T(2,128)(2,1)S(1)}, bf16[2,256]{1,0:T(2,128)(2,1)}, u32[]{:S(2)}) copy-start(bf16[2,256]{1,0:T(2,128)(2,1)} %param.22) | copy-start | bytes 3076
  26.8 14.3 %copy-start.17 = (bf16[2,256]{1,0:T(2,128)(2,1)S(1)}, bf16[2,256]{1,0:T(2,128)(2,1)}, u32[]{:S(2)}) copy-start(bf16[2,256]{1,0:T(2,128)(2,1)} %param.17) | copy-start | bytes 3076
  26.8 475.0 %all-gather.13.cloned.1.call-start = ((), (), s32[]{:S(2)}) async-start(), calls=%async_computation.2 | async-start | bytes 37748736 | tf_op jit(solution)/shard_map/all_gather | solution.py:379
  31.5 627.2 %all-gather.17.cloned.1.call-start = ((), (), s32[]{:S(2)}) async-start(), calls=%async_computation.4 | async-start | bytes 37748736 | tf_op jit(solution)/shard_map/all_gather | solution.py:381
  36.3 729.2 %all-gather.9.cloned.1.call-start = ((), (), s32[]{:S(2)}) async-start(), calls=%async_computation | async-start | bytes 18874368 | tf_op jit(solution)/shard_map/all_gather | solution.py:383
  40.1 200.7 %copy-start.2 = (f32[32,512]{1,0:T(8,128)}, f32[32,512]{1,0:T(8,128)S(1)}, u32[]{:S(2)}) copy-start(f32[32,512]{1,0:T(8,128)S(1)} %get-tuple-element.24.sin_ref) | copy-start | bytes 196612
  40.1 200.6 %copy-start.4 = (f32[32,512]{1,0:T(8,128)}, f32[32,512]{1,0:T(8,128)S(1)}, u32[]{:S(2)}) copy-start(f32[32,512]{1,0:T(8,128)S(1)} %get-tuple-element.25.cos_ref) | copy-start | bytes 196612
  187.7 3.4 copy-start
  240.7 95.3 %slice-start = ((s8[8388608]{0:T(1024)(128)(4,1)}), s8[4194304]{0:T(1024)(128)(4,1)S(1)}, s32[]{:S(2)}) async-start(s8[8388608]{0:T(1024)(128)(4,1)} %bitcast.90), calls=%async_computation.5 | async-start | bytes 8388608
  266.7 3.3 copy-start.8
  270.0 66.1 %slice-start.1 = ((s8[8388608]{0:T(1024)(128)(4,1)}), s8[4194304]{0:T(1024)(128)(4,1)S(1)}, s32[]{:S(2)}) async-start(s8[8388608]{0:T(1024)(128)(4,1)} %bitcast.90), calls=%async_computation.6 | async-start | bytes 8388608
  336.1 25.5 %copy-start.15 = (f32[1,2048]{1,0:T(1,128)S(1)}, f32[1,2048]{1,0:T(1,128)}, u32[]{:S(2)}) copy-start(f32[1,2048]{1,0:T(1,128)} %get-tuple-element.17) | copy-start | bytes 24580
  593.2 150.6 %copy-start.11 = (s32[4]{0:T(128)S(1)}, s32[4]{0:T(128)}, u32[]{:S(2)}) copy-start(s32[4]{0:T(128)} %or_bitcast_fusion) | copy-start | bytes 52
  593.2 152.0 %copy-start.14 = (pred[4]{0:T(512)(128)(4,1)S(1)}, pred[4]{0:T(512)(128)(4,1)}, u32[]{:S(2)}) copy-start(pred[4]{0:T(512)(128)(4,1)} %get-tuple-element.23) | copy-start | bytes 16
  593.2 152.3 %copy-start.10 = (f32[1,2048]{1,0:T(1,128)S(1)}, f32[1,2048]{1,0:T(1,128)}, u32[]{:S(2)}) copy-start(f32[1,2048]{1,0:T(1,128)} %get-tuple-element.16) | copy-start | bytes 24580
  593.2 162.7 %copy-start.12 = (f32[4,32]{1,0:T(4,128)S(1)}, f32[4,32]{1,0:T(4,128)}, u32[]{:S(2)}) copy-start(f32[4,32]{1,0:T(4,128)} %get-tuple-element.19) | copy-start | bytes 1540
  593.2 162.7 %copy-start.13 = (f32[4,32]{1,0:T(4,128)S(1)}, f32[4,32]{1,0:T(4,128)}, u32[]{:S(2)}) copy-start(f32[4,32]{1,0:T(4,128)} %get-tuple-element.20) | copy-start | bytes 1540
  593.2 163.7 %copy-start.9 = (pred[32,2048]{1,0:T(8,128)(4,1)S(1)}, pred[32,2048]{1,0:T(8,128)(4,1)}, u32[]{:S(2)}) copy-start(pred[32,2048]{1,0:T(8,128)(4,1)} %iota_compare_fusion) | copy-start | bytes 196612
  743.8 21.8 %copy-start.3 = (f32[32,512]{1,0:T(8,128)S(1)}, f32[32,512]{1,0:T(8,128)}, u32[]{:S(2)}) copy-start(f32[32,512]{1,0:T(8,128)} %copy-done.2) | copy-start | bytes 196612
  743.8 21.8 %copy-start.5 = (f32[32,512]{1,0:T(8,128)S(1)}, f32[32,512]{1,0:T(8,128)}, u32[]{:S(2)}) copy-start(f32[32,512]{1,0:T(8,128)} %copy-done.4) | copy-start | bytes 196612
  765.5 3.4 copy-start.1
  793.6 25.0 %copy-start.7 = (s32[4]{0:T(128)S(1)}, s32[4]{0:T(128)}, u32[]{:S(2)}) copy-start(s32[4]{0:T(128)} %lens_ref.3) | copy-start | bytes 52
Sparse Core Ops, SparseCore 0:
  22.2 165.3 all-gather.10
  189.5 155.2 all-gather.14
  346.5 155.2 all-gather.12
  503.5 155.2 all-gather.16
  660.4 87.3 all-gather.8

commit v3 on v2

v3 whole, which is shorter than its diff:
```python
import functools
import math
import jax
import jax.numpy as jnp
import numpy as np
from jax import lax
from jax.experimental import pallas as pl
from jax.experimental.pallas import tpu as pltpu
from jax.sharding import PartitionSpec as P

F32 = jnp.float32
BF16 = jnp.bfloat16
ANY = pl.BlockSpec(memory_space=pl.ANY)
HBM = pl.BlockSpec(memory_space=pltpu.HBM)
VM = pl.BlockSpec(memory_space=pltpu.VMEM)
NT = (((1,), (1,)), ((), ()))


def params(mib, collective=None):
    extra = {} if collective is None else dict(collective_id=collective, has_side_effects=True)
    return pltpu.CompilerParams(vmem_limit_bytes=mib << 20, **extra)


def cost(macs, values, exps=0):
    return pl.CostEstimate(flops=2 * macs, bytes_accessed=2 * values, transcendentals=exps)


def dot(a, b):
    return jnp.dot(a, b, preferred_element_type=F32)


def dot_nt(a, b):
    return lax.dot_general(a, b, NT, preferred_element_type=F32)


def rope_frequencies(head_dim):
    half_dim = head_dim // 2
    exponent = np.arange(half_dim, dtype=np.float32) * np.float32(2.0 / head_dim)
    inv_freq = np.float32(1.0) / np.float32(500000.0) ** exponent
    wave_len = np.float32(2.0 * math.pi) / inv_freq
    smooth = (np.float32(8192.0) / wave_len - np.float32(1.0)) / np.float32(3.0)
    blended = (1 - smooth) * inv_freq / 8 + smooth * inv_freq
    scaled = np.where(wave_len > 8192.0, inv_freq / 8, np.where(wave_len < 2048.0, inv_freq, blended))
    return scaled.astype(np.float32)


def rms_norm(values, gain_f32):
    values_f32 = values.astype(F32)
    mean_sq = jnp.mean(values_f32 * values_f32, axis=-1, keepdims=True)
    return (values_f32 * lax.rsqrt(mean_sq + 1e-5) * gain_f32).astype(BF16)


ROWS = 1024
PAIR = 2


def proj_body(ropes, per, head_dim, n_prev, norm, w_ref, a_ref, cos_ref, sin_ref, *rest):
    s = cos_ref.shape[1]
    half = head_dim // 2
    if norm:
        gain_ref, a_src, a_ref = rest[0], a_ref, rest[-1]
        rest = rest[1:-1]

        @pl.when((pl.program_id(0) == 0) & (pl.program_id(1) == 0))
        def _():
            normalize(a_src, gain_ref, a_ref)

    outs = rest[n_prev:]
    first = pl.multiple_of(pl.program_id(1) * PAIR * s, PAIR * s)
    y = dot_nt(w_ref[...], a_ref[pl.ds(first, PAIR * s)])

    def store(rope, out_ref):
        for t in range(PAIR):
            part = y[:, t * s:(t + 1) * s]
            if not rope:
                out_ref[0, t] = part.astype(BF16)
                continue
            cos, sin = cos_ref[...], sin_ref[...]
            for i in range(ROWS // head_dim):
                low = part[i * head_dim:i * head_dim + half]
                high = part[i * head_dim + half:(i + 1) * head_dim]
                out_ref[0, t, pl.ds(i * head_dim, half)] = (low * cos - high * sin).astype(BF16)
                out_ref[0, t, pl.ds(i * head_dim + half, half)] = (high * cos + low * sin).astype(BF16)

    for k, (rope, out_ref) in enumerate(zip(ropes, outs)):
        pl.when(pl.program_id(0) // per == k)(functools.partial(store, rope, out_ref))


def project(a, w, cos, sin, head_dim, ropes, layers, layer, prev=None, gain=None):
    rows, d = a.shape
    s = cos.shape[1]
    b, width = rows // s, w.shape[0] // len(ropes)
    per = width // ROWS
    last = b // PAIR - 1

    def place(k):
        def index(i, j):
            at = i - k * per
            inside = (at >= 0) & (at < per)
            return layer, jnp.where(inside, j, jnp.where(at < 0, 0, last)), jnp.clip(at, 0, per - 1), 0
        return pl.BlockSpec((1, PAIR, ROWS, s), index)

    in_specs = [
        pl.BlockSpec((ROWS, d), lambda i, j: (i, 0)),
        pl.BlockSpec((rows, d), lambda i, j: (0, 0)),
        pl.BlockSpec(cos.shape, lambda i, j: (0, 0)),
        pl.BlockSpec(sin.shape, lambda i, j: (0, 0)),
    ]
    args = [w, a, cos, sin]
    alias = {}
    out_shape = [jax.ShapeDtypeStruct((count, b, width, s), BF16) for count in layers]
    out_specs = [place(k) for k in range(len(ropes))]
    if gain is not None:
        in_specs.append(pl.BlockSpec(gain.shape, lambda i, j: (0, 0)))
        args.append(gain)
        out_shape.append(jax.ShapeDtypeStruct(a.shape, BF16))
        out_specs.append(pl.BlockSpec(a.shape, lambda i, j: (0, 0)))
    if prev is not None:
        alias = {len(args): 0}
        in_specs.append(HBM)
        args.append(prev)
    return pl.pallas_call(
        functools.partial(proj_body, ropes, per, head_dim, len(alias), gain is not None),
        out_shape=out_shape,
        grid=(w.shape[0] // ROWS, b // PAIR),
        in_specs=in_specs,
        out_specs=out_specs,
        input_output_aliases=alias,
        compiler_params=params(58),
        cost_estimate=cost(rows * d * w.shape[0], w.size + a.size + a.size),
        name="project",
    )(*args)


TILE = 512
BAND = 1024


def normalize(src_ref, gain_ref, dst_ref):
    lines = 32

    def step(r, carry):
        rows = pl.ds(pl.multiple_of(r * lines, lines), lines)
        dst_ref[rows] = rms_norm(src_ref[rows], gain_ref[...])
        return carry

    lax.fori_loop(0, src_ref.shape[0] // lines, step, 0, unroll=4)


def gate_up_tile(x, wg_ref, wu_ref, o_ref):
    gate = dot(x, wg_ref[...])
    up = dot(x, wu_ref[...])
    o_ref[...] = (gate * (1.0 / (1.0 + jnp.exp(-gate))) * up).astype(BF16)


def gate_up_first_body(h_ref, gain_ref, wg_ref, wu_ref, o_ref, m_ref):
    @pl.when((pl.program_id(0) == 0) & (pl.program_id(1) == 0))
    def _():
        normalize(h_ref, gain_ref, m_ref)

    gate_up_tile(m_ref[pl.ds(pl.multiple_of(pl.program_id(1) * BAND, BAND), BAND)], wg_ref, wu_ref, o_ref)


def gate_up_rest_body(m_ref, wg_ref, wu_ref, o_ref):
    gate_up_tile(m_ref[pl.ds(pl.multiple_of(pl.program_id(1) * BAND, BAND), BAND)], wg_ref, wu_ref, o_ref)


def gate_up(rows_in, gain, weights, width):
    rows, d = rows_in.shape
    whole = pl.BlockSpec((rows, d), lambda i, j: (0, 0))
    out_shape = [jax.ShapeDtypeStruct((rows, width), BF16)]
    out_specs = [pl.BlockSpec((BAND, TILE), lambda i, j: (j, i))]
    if gain is not None:
        body, lead, args = gate_up_first_body, [whole, pl.BlockSpec(gain.shape, lambda i, j: (0, 0))], (rows_in, gain) + weights
        specs = [pl.BlockSpec((d, TILE), lambda i, j: (0, i))] * 2
        out_shape.append(jax.ShapeDtypeStruct((rows, d), BF16))
        out_specs.append(whole)
    else:
        body, lead, args = gate_up_rest_body, [whole], (rows_in,) + weights * 2
        specs = [pl.BlockSpec((None, d, TILE), lambda i, j, k=k: (k, 0, i)) for k in range(2)]
    return pl.pallas_call(
        body,
        out_shape=out_shape,
        grid=(width // TILE, rows // BAND),
        in_specs=lead + specs,
        out_specs=out_specs,
        compiler_params=params(60),
        cost_estimate=cost(2 * rows * d * width, 2 * d * width + rows * (d + width), rows * width),
        name="gate_up",
    )(*args)


def down_body(has_base, a_ref, w_ref, *rest):
    y = dot(a_ref[...], w_ref[...])
    if has_base:
        base_ref, part_ref, o_ref = rest
        o_ref[...] = (base_ref[...].astype(F32) + (part_ref[...] + y)).astype(BF16)
    else:
        rest[0][...] = y


def down(act, w, band, base=None):
    rows, kd = act.shape
    d = w.shape[1]
    tile = pl.BlockSpec((band, TILE), lambda i, j: (i, j))
    base = base or ()
    return pl.pallas_call(
        functools.partial(down_body, bool(base)),
        out_shape=jax.ShapeDtypeStruct((rows, d), BF16 if base else F32),
        grid=(rows // band, d // TILE),
        in_specs=[pl.BlockSpec((band, kd), lambda i, j: (i, 0)), pl.BlockSpec((kd, TILE), lambda i, j: (0, j))] + [tile] * len(base),
        out_specs=tile,
        compiler_params=params(60),
        cost_estimate=cost(rows * d * kd, rows * kd + kd * d + 3 * rows * d),
        name="down",
    )(act, w, *base)


HEADS_STEP = 8


def attn_body(head_dim, lens_ref, q_ref, k_ref, v_ref, o_ref):
    s = q_ref.shape[-1]
    length = lens_ref[pl.program_id(0)]
    t_pos = lax.broadcasted_iota(jnp.int32, (s, s), 0)
    s_pos = lax.broadcasted_iota(jnp.int32, (s, s), 1)
    allowed = (t_pos <= s_pos) & (t_pos < length)
    for i in range(HEADS_STEP):
        rows = pl.ds(i * head_dim, head_dim)
        q = q_ref[0, 0, rows] * jnp.asarray(head_dim ** -0.5, BF16)
        sc = lax.dot_general(k_ref[0, 0, rows], q, (((0,), (0,)), ((), ())), preferred_element_type=F32)
        sc = jnp.where(allowed, sc, -jnp.inf)
        ex = jnp.exp(sc - jnp.max(sc, axis=0, keepdims=True))
        p = (ex * (1.0 / jnp.sum(ex, axis=0, keepdims=True))).astype(BF16)
        o_ref[0, rows] = dot(v_ref[0, 0, rows], p).astype(BF16)


def attention(lens, q, k, v, head_dim):
    _, b, width, s = q.shape
    step = HEADS_STEP * head_dim
    spec = pl.BlockSpec((1, 1, step, s), lambda i, j, lens: (0, i, j, 0))
    return pl.pallas_call(
        functools.partial(attn_body, head_dim),
        out_shape=jax.ShapeDtypeStruct((b, width, s), BF16),
        grid_spec=pltpu.PrefetchScalarGridSpec(
            num_scalar_prefetch=1,
            grid=(b, width // step),
            in_specs=[spec, spec, spec],
            out_specs=pl.BlockSpec((1, step, s), lambda i, j, lens: (i, j, 0)),
        ),
        compiler_params=params(40),
        cost_estimate=cost(16 * b * s * s * width, 4 * b * s * width, b * s * s * width // head_dim),
        name="attention",
    )(lens, q, k, v)


def last_body(head_dim, lens_ref, q_ref, k_ref, v_ref, o_ref):
    length = lens_ref[pl.program_id(0)]
    sc = dot(q_ref[0], k_ref[0, 0]) * head_dim ** -0.5
    t_pos = lax.broadcasted_iota(jnp.int32, sc.shape, 1)
    sc = jnp.where(t_pos < length, sc, -jnp.inf)
    ex = jnp.exp(sc - jnp.max(sc, axis=-1, keepdims=True))
    p = (ex / jnp.sum(ex, axis=-1, keepdims=True)).astype(BF16)
    full = dot_nt(p, v_ref[0, 0])
    head = lax.broadcasted_iota(jnp.int32, full.shape, 0)
    col = lax.broadcasted_iota(jnp.int32, full.shape, 1)
    own = (col >= head * head_dim) & (col < (head + 1) * head_dim)
    o = jnp.sum(jnp.where(own, full, 0.0), axis=0, keepdims=True)
    o_ref[0] = o.astype(BF16).astype(F32)


def last_attention(lens, q_diag, k, v, head_dim, layer):
    b, heads, width = q_diag.shape
    s = k.shape[-1]
    kv = pl.BlockSpec((1, 1, width, s), lambda i, lens: (layer, i, 0, 0))
    return pl.pallas_call(
        functools.partial(last_body, head_dim),
        out_shape=jax.ShapeDtypeStruct((b, 1, width), F32),
        grid_spec=pltpu.PrefetchScalarGridSpec(
            num_scalar_prefetch=1,
            grid=(b,),
            in_specs=[pl.BlockSpec((1, heads, width), lambda i, lens: (i, 0, 0)), kv, kv],
            out_specs=pl.BlockSpec((1, 1, width), lambda i, lens: (i, 0, 0)),
        ),
        compiler_params=params(40),
        cost_estimate=cost(2 * b * s * width * heads, 2 * b * s * width, b * s * heads),
        name="last_attention",
    )(lens, q_diag, k, v)[:, 0]


class Exchange:
    def __init__(self, n, send_sems, recv_sems):
        self.n, self.send_sems, self.recv_sems = n, send_sems, recv_sems
        self.me = lax.axis_index("dp")

    def peer(self, j):
        return lax.rem(self.me + j, self.n)

    def barrier(self):
        sem = pltpu.get_barrier_semaphore()
        for j in range(1, self.n):
            pl.semaphore_signal(sem, inc=1, device_id={"dp": self.peer(j)}, device_id_type=pl.DeviceIdType.MESH)
        pl.semaphore_wait(sem, self.n - 1)

    def copy(self, stage, j, src, dst):
        return pltpu.make_async_remote_copy(
            src_ref=src, dst_ref=dst, send_sem=self.send_sems.at[stage, j], recv_sem=self.recv_sems.at[stage, self.me],
            device_id={"dp": self.peer(j)}, device_id_type=pl.DeviceIdType.MESH)

    def arrival(self, stage, j, src, dst):
        return pltpu.make_async_remote_copy(
            src_ref=src, dst_ref=dst, send_sem=self.send_sems.at[stage, j], recv_sem=self.recv_sems.at[stage, self.peer(j)],
            device_id={"dp": self.peer(j)}, device_id_type=pl.DeviceIdType.MESH)

    def start(self, stage, src_of, dst):
        for j in range(1, self.n):
            self.copy(stage, j, src_of(j), dst).start()

    def wait(self, stage, src_of, dst_from):
        for j in range(1, self.n):
            self.arrival(stage, j, src_of(j), dst_from(self.peer(j))).wait_recv()
        for j in range(1, self.n):
            self.arrival(stage, j, src_of(j), dst_from(self.peer(j))).wait_send()


def columns(ref, index, width):
    return ref.at[:, pl.ds(pl.multiple_of(index * width, width), width)]


def spread(ex, stage, rows_ref, got_ref, lhs_ref):
    n, rows, width = got_ref.shape
    src = lambda j: columns(rows_ref, ex.peer(j), width)
    ex.start(stage, src, got_ref.at[ex.me])
    got_ref[ex.me] = columns(rows_ref, ex.me, width)[...]
    ex.wait(stage, src, lambda p: got_ref.at[p])
    for i in range(n):
        lhs_ref[pl.ds(i * rows, rows)] = got_ref[i]
    return lhs_ref[...].astype(BF16)


def reduce_rows(ex, stage, part, send_ref, got_ref):
    n, rows, _ = got_ref.shape
    for i in range(n):
        send_ref[i] = part[i * rows:(i + 1) * rows]
    src = lambda j: send_ref.at[ex.peer(j)]
    ex.start(stage, src, got_ref.at[ex.me])
    got_ref[ex.me] = send_ref[ex.me]
    ex.wait(stage, src, lambda p: got_ref.at[p])
    total = got_ref[0]
    for i in range(1, n):
        total = total + got_ref[i]
    return total


def query_body(n, layer, a_ref, w_hbm, q_ref, w, got, lhs, send, back, local_sem, send_sems, recv_sems):
    load = pltpu.make_async_copy(w_hbm.at[layer], w, local_sem)
    load.start()
    ex = Exchange(n, send_sems, recv_sems)
    ex.barrier()
    x = spread(ex, 0, a_ref, got, lhs)
    load.wait()
    q_ref[...] = reduce_rows(ex, 1, dot_nt(x, w[...]), send, back)


def last_query(a_last, w_rows, layer, n):
    rows, d = a_last.shape
    _, width, kd = w_rows.shape
    return pl.pallas_call(
        functools.partial(query_body, n, layer),
        out_shape=jax.ShapeDtypeStruct((rows, width), F32),
        in_specs=[VM, HBM],
        out_specs=VM,
        scratch_shapes=[
            pltpu.VMEM((width, kd), BF16),
            pltpu.VMEM((n, rows, kd), F32), pltpu.VMEM((n * rows, kd), F32),
            pltpu.VMEM((n, rows, width), F32), pltpu.VMEM((n, rows, width), F32),
            pltpu.SemaphoreType.DMA, pltpu.SemaphoreType.DMA((2, n)), pltpu.SemaphoreType.DMA((2, n)),
        ],
        compiler_params=params(16, 0),
        cost_estimate=cost(n * rows * width * kd, width * kd),
        name="last_query",
    )(a_last, w_rows)


class Place:
    def __init__(self):
        me = lax.axis_index("dp")
        core, col, row = lax.rem(me, 2), lax.rem(me // 2, 2), me // 4
        at = lambda r, c, k: r * 4 + c * 2 + k
        self.me = me
        self.sib = at(row, col, 1 - core)
        self.xn, self.yn, self.dg = at(row, 1 - col, core), at(1 - row, col, core), at(1 - row, 1 - col, core)
        self.xs, self.ys, self.ds = at(row, 1 - col, 1 - core), at(1 - row, col, 1 - core), at(1 - row, 1 - col, 1 - core)


def remote(src, dst, send_sem, recv_sem, dev):
    return pltpu.make_async_remote_copy(src_ref=src, dst_ref=dst, send_sem=send_sem, recv_sem=recv_sem,
                                        device_id={"dp": dev}, device_id_type=pl.DeviceIdType.MESH)


def greet(devs):
    sem = pltpu.get_barrier_semaphore()
    for dev in devs:
        pl.semaphore_signal(sem, inc=1, device_id={"dp": dev}, device_id_type=pl.DeviceIdType.MESH)
    pl.semaphore_wait(sem, len(devs))


def gather_body(n, plan, n_in, n_out, *refs):
    ins, outs = refs[:n_in], refs[n_in:n_in + n_out]
    (stage, keep, gain_got, gain_row, raw, normed, load_sems, pack_sems, keep_sems, gain_send, gain_recv, row_sems, own_sems,
     send_sems, recv_sems) = refs[n_in + n_out:]
    at = Place()
    me = at.me
    gain_ref, hidden = ins[:2]
    gains_out, normed_out = outs[:2]
    jobs, pack_in, pack_out = plan(ins[2:], outs[2:], stage, keep)
    count = len(jobs)
    loads, taken = [], 0
    for pieces, _, _, _ in jobs:
        loads.append([pltpu.make_async_copy(src, dst, load_sems.at[taken + i]) for i, (src, dst) in enumerate(pieces)])
        taken += len(pieces)
    for copy in sum(loads, []):
        copy.start()
    batch = hidden.shape[0]
    row_in = [pltpu.make_async_copy(hidden.at[i], raw.at[i % 2], row_sems.at[0, i]) for i in range(batch)]
    row_out = [pltpu.make_async_copy(normed.at[i % 2], normed_out.at[i], row_sems.at[1, i]) for i in range(batch)]
    pack_in = [pltpu.make_async_copy(src, dst, pack_sems.at[i]) for i, (src, dst) in enumerate(pack_in)]
    pack_out = [pltpu.make_async_copy(src, dst, keep_sems.at[i]) for i, (src, dst) in enumerate(pack_out)]
    peers = [lax.rem(me + j, n) for j in range(1, n)]
    greet(peers)

    def gain_to(j):
        return remote(gain_ref, gain_got.at[me], gain_send.at[j], gain_recv.at[me], peers[j])

    def gain_from(j):
        return remote(gain_ref, gain_got.at[peers[j]], gain_send.at[j], gain_recv.at[peers[j]], peers[j])

    def share_gains():
        for j in range(n - 1):
            gain_to(j).start()
        gain_got[me] = gain_ref[...]

    def normalize():
        for j in range(n - 1):
            gain_from(j).wait_recv()
            gain_from(j).wait_send()
        gains_out[...] = gain_got[...]
        width = gain_ref.shape[1]
        for i in range(n):
            gain_row[:, pl.ds(i * width, width)] = gain_got[i, pl.ds(0, 1)]
        block = 32
        for i in range(batch):
            row_in[i].wait()
            if i >= 2:
                row_out[i - 2].wait()

            def step(r, carry, i=i):
                rows = pl.ds(pl.multiple_of(r * block, block), block)
                normed[i % 2, rows] = rms_norm(raw[i % 2, rows], gain_row[...])
                return carry

            lax.fori_loop(0, raw.shape[1] // block, step, 0)
            row_out[i].start()
            if i + 2 < batch:
                row_in[i + 2].start()

    def hop(k, i):
        _, buf, full, half = jobs[i]
        route = (
            (buf, full(at.me), at.xn, full(at.xn)),
            (buf, full(at.me), at.yn, full(at.yn)),
            (buf, full(at.me), at.sib, full(at.sib)),
            (half(at.xn, 0), half(at.xn, 0), at.yn, half(at.dg, 0)),
            (half(at.yn, 1), half(at.yn, 1), at.xn, half(at.dg, 1)),
            (full(at.xn), full(at.xn), at.sib, full(at.xs)),
            (full(at.yn), full(at.yn), at.sib, full(at.ys)),
            (half(at.dg, 0), half(at.dg, 0), at.sib, half(at.ds, 0)),
            (half(at.dg, 1), half(at.dg, 1), at.sib, half(at.ds, 1)),
        )
        return route[k]

    def start(k, i):
        src, dst, dev, _ = hop(k, i)
        remote(src, dst, send_sems.at[k, i], recv_sems.at[k, i], dev).start()

    def arrived(k, i):
        src, _, dev, land = hop(k, i)
        remote(src, land, send_sems.at[k, i], recv_sems.at[k, i], dev).wait_recv()

    def sent(k, i):
        src, dst, dev, _ = hop(k, i)
        remote(src, dst, send_sems.at[k, i], recv_sems.at[k, i], dev).wait_send()

    def relay(i):
        arrived(0, i)
        start(3, i)
        start(5, i)
        arrived(1, i)
        start(4, i)
        start(6, i)

    def relay_diagonal(i):
        arrived(3, i)
        start(7, i)
        arrived(4, i)
        start(8, i)

    own = []
    for i, (_, buf, full, _) in enumerate(jobs):
        for copy in loads[i]:
            copy.wait()
        for k in range(3):
            start(k, i)
        own.append(pltpu.make_async_copy(buf, full(me), own_sems.at[i]))
        own[-1].start()
        if i == 0:
            share_gains()
            for copy in row_in[:2] + pack_in:
                copy.start()
        if i == 1:
            for copy in pack_in:
                copy.wait()
            for copy in pack_out:
                copy.start()
            normalize()
        if i >= 1:
            relay(i - 1)
        if i >= 2:
            relay_diagonal(i - 2)
    relay(count - 1)
    relay_diagonal(count - 2)
    relay_diagonal(count - 1)
    for i in range(count):
        for k in (2, 5, 6, 7, 8):
            arrived(k, i)
        for k in range(9):
            sent(k, i)
        own[i].wait()
    for copy in pack_out + row_out[-2:]:
        copy.wait()


def first_gather(gains, hidden, w_query, w_key, w_value, w_out, w_gate, w_up, w_down, n):
    hd, kd = w_query.shape[1:]
    d = w_out.shape[2]
    block = w_down.shape[1]
    rest = block - kd

    def plan(ins, outs, stage, keep):
        wq, wk, wv, wo, wg, wu, wd = ins
        gqkv, go, gg, gu, gd, pg, pd, pk, pv = outs
        cols, rows = stage
        kg, kdn, kk, kv = keep

        def by_columns(src, buf, first):
            column = lambda dev: pl.ds(pl.multiple_of(dev * kd, kd), kd)
            full = lambda dev: gqkv.at[pl.ds(first, hd), column(dev)]
            half = lambda dev, h: gqkv.at[pl.ds(first + h * (hd // 2), hd // 2), column(dev)]
            return [(src, buf)], buf, full, half

        def by_rows(pieces, buf, out):
            full = lambda dev: out.at[pl.ds(pl.multiple_of(dev * kd, kd), kd)]
            half = lambda dev, h: out.at[pl.ds(pl.multiple_of(dev * kd + h * (kd // 2), kd // 2), kd // 2)]
            return pieces, buf, full, half

        def blocks(w, first, size, buf):
            return [(w.at[0, :, pl.ds(e * block + first, size)], buf.at[:, pl.ds(e * size, size)]) for e in range(n)]

        jobs = [by_columns(w.at[0], cols.at[i], i * hd) for i, w in enumerate((wq, wk, wv))]
        jobs += [
            by_rows([(wo.at[0], rows.at[0])], rows.at[0], go),
            by_rows(blocks(wg, 0, kd, rows.at[1]), rows.at[1], gg), by_rows(blocks(wu, 0, kd, rows.at[2]), rows.at[2], gu),
            by_rows([(wd.at[0, pl.ds(0, kd)], rows.at[3])], rows.at[3], gd),
        ]
        pack_in = blocks(wg, kd, rest, kg.at[0]) + blocks(wu, kd, rest, kg.at[1])
        pack_in += [(wd.at[0, pl.ds(kd, rest)], kdn), (wk.at[1], kk), (wv.at[1], kv)]
        return jobs, pack_in, [(kg, pg), (kdn, pd), (kk, pk), (kv, pv)]

    count = 7
    shape = lambda *dims: jax.ShapeDtypeStruct(dims, BF16)
    outs = [jax.ShapeDtypeStruct((n,) + gains.shape, F32), shape(*hidden.shape)]
    outs += [shape(3 * hd, d)] + [shape(n * kd, d)] * 4
    outs += [shape(2, kd, n * rest), shape(rest, d), shape(hd, kd), shape(hd, kd)]
    batch, seq, _ = hidden.shape
    dma = pltpu.SemaphoreType.DMA
    return pl.pallas_call(
        functools.partial(gather_body, n, plan, 9, len(outs)),
        out_shape=outs,
        in_specs=[VM] + [HBM] * 8,
        out_specs=[VM] + [HBM] * (len(outs) - 1),
        scratch_shapes=[
            (pltpu.VMEM((3, hd, kd), BF16), pltpu.VMEM((4, kd, d), BF16)),
            (pltpu.VMEM((2, kd, n * rest), BF16), pltpu.VMEM((rest, d), BF16), pltpu.VMEM((hd, kd), BF16), pltpu.VMEM((hd, kd), BF16)),
            pltpu.VMEM((n,) + gains.shape, F32), pltpu.VMEM((1, d), F32),
            pltpu.VMEM((2, seq, d), BF16), pltpu.VMEM((2, seq, d), BF16),
            dma((5 + 2 * n,)), dma((2 * n + 3,)), dma((4,)), dma((n - 1,)), dma((n,)), dma((2, batch)),
            dma((count,)), dma((9, count)), dma((9, count)),
        ],
        compiler_params=params(48, 2),
        cost_estimate=cost(50_000_000_000, 50_000_000),
        name="first_gather",
    )(gains, hidden, w_query, w_key, w_value, w_out, w_gate, w_up, w_down)


GROUPS = 6
TABLE_STEP = 512


def tail_body(n, layer, o_ref, x_ref, gm_ref, gf_ref, wo_hbm, wg_hbm, wu_hbm, wd_hbm, emb_hbm, out_ref,
              wo, wg, wu, wd, emb, got, lhs, send, back, mid_ref, rows_ref, sib_send, sib_got, gate_send, gate_got, z_row, z_got, z_lhs,
              log_send, log_got, local_sems, pair_sems, send_sems, recv_sems):
    ex = Exchange(n, send_sems, recv_sems)
    me = ex.me
    pairs = ((wo_hbm.at[layer], wo), (wg_hbm.at[layer], wg), (wu_hbm.at[layer], wu), (wd_hbm.at[layer], wd), (emb_hbm, emb))
    loads = [pltpu.make_async_copy(src, dst, local_sems.at[i]) for i, (src, dst) in enumerate(pairs)]
    for load in loads:
        load.start()
    ex.barrier()

    x = spread(ex, 0, o_ref, got, lhs)
    loads[0].wait()
    mid = (x_ref[...] + reduce_rows(ex, 1, dot(x, wo[...]), send, back)).astype(BF16).astype(F32)
    mid_ref[...] = mid

    rows_ref[...] = rms_norm(mid, gm_ref[...]).astype(F32)
    x = spread(ex, 2, rows_ref, got, lhs)
    loads[1].wait()
    loads[2].wait()
    block = wd.shape[0]

    def gate_up(p):
        cols = pl.ds(pl.multiple_of(p * block, block), block)
        return dot(x, wg[:, cols]), dot(x, wu[:, cols])

    at = Place()
    across = (at.xs, at.ys, at.ds, at.sib)
    along = (at.xn, at.yn, at.dg, me)
    to_sib = [remote(sib_send.at[k], sib_got.at[k], pair_sems.at[0, k], pair_sems.at[1, k], at.sib) for k in range(4)]
    to_chip = [remote(gate_send.at[k], gate_got.at[k], pair_sems.at[2, k], pair_sems.at[3, k], along[k]) for k in range(3)]
    order = (2, 0, 1, 3)
    for k in order:
        gate, up = gate_up(across[k])
        sib_send[k, 0] = gate
        sib_send[k, 1] = up
        to_sib[k].start()
    for k in order:
        gate, up = gate_up(along[k])
        to_sib[k].wait_recv()
        gate = gate + sib_got[k, 0]
        up = up + sib_got[k, 1]
        if along[k] is not me:
            gate_send[k, 0] = gate
            gate_send[k, 1] = up
            to_chip[k].start()
    for k in range(3):
        to_chip[k].wait_recv()
        gate = gate + gate_got[k, 0]
        up = up + gate_got[k, 1]
    for copy in to_sib + to_chip:
        copy.wait_send()
    act = (gate * (1.0 / (1.0 + jnp.exp(-gate))) * up).astype(BF16)

    loads[3].wait()
    h = (mid_ref[...] + reduce_rows(ex, 4, dot(act, wd[...]), send, back)).astype(BF16).astype(F32)

    z_row[...] = rms_norm(h, gf_ref[...])
    rows = rows_ref.shape[0]
    ex.start(5, lambda j: z_row, z_got.at[me])
    z_got[me] = z_row[...]
    ex.wait(5, lambda j: z_row, lambda p: z_got.at[p])
    for i in range(n):
        z_lhs[pl.ds(i * rows, rows)] = z_got[i].astype(F32)
    z = z_lhs[...].astype(BF16)
    loads[4].wait()
    vocab = emb.shape[0]
    group = vocab // GROUPS
    for g in range(GROUPS):
        def step(c, carry):
            first = pl.multiple_of(g * group + c * TABLE_STEP, TABLE_STEP)
            part = dot_nt(z, emb[pl.ds(first, TABLE_STEP)])
            for i in range(n):
                log_send[i, :, pl.ds(first, TABLE_STEP)] = part[i * rows:(i + 1) * rows]
            return carry

        lax.fori_loop(0, group // TABLE_STEP, step, 0)
        src = lambda j, g=g: log_send.at[ex.peer(j), :, pl.ds(g * group, group)]
        dst = lambda p, g=g: log_got.at[:, pl.ds(pl.multiple_of(p * vocab + g * group, group), group)]
        ex.start(6 + g, src, dst(me))
    log_got[:, pl.ds(pl.multiple_of(me * vocab, vocab), vocab)] = log_send[me]
    for g in range(GROUPS):
        src = lambda j, g=g: log_send.at[ex.peer(j), :, pl.ds(g * group, group)]
        dst = lambda p, g=g: log_got.at[:, pl.ds(pl.multiple_of(p * vocab + g * group, group), group)]
        ex.wait(6 + g, src, dst)
    out_ref[...] = log_got[...]


def tail(o, x, gm, gf, w_out, w_gate, w_up, w_down, emb, layer, n):
    rows, d = x.shape
    kd, ffn, block, vocab = w_gate.shape[1], w_gate.shape[2], w_down.shape[1], emb.shape[0]
    stages = 6 + GROUPS
    weights = kd * d + 2 * kd * ffn + block * d + vocab * d
    return pl.pallas_call(
        functools.partial(tail_body, n, layer),
        out_shape=jax.ShapeDtypeStruct((rows, n * vocab), F32),
        in_specs=[VM, VM, VM, VM] + [HBM] * 5,
        out_specs=VM,
        scratch_shapes=[
            pltpu.VMEM((kd, d), BF16), pltpu.VMEM((kd, ffn), BF16), pltpu.VMEM((kd, ffn), BF16),
            pltpu.VMEM((block, d), BF16), pltpu.VMEM((vocab, d), BF16),
            pltpu.VMEM((n, rows, kd), F32), pltpu.VMEM((n * rows, kd), F32),
            pltpu.VMEM((n, rows, d), F32), pltpu.VMEM((n, rows, d), F32),
            pltpu.VMEM((rows, d), F32), pltpu.VMEM((rows, d), F32),
            pltpu.VMEM((4, 2, n * rows, block), F32), pltpu.VMEM((4, 2, n * rows, block), F32),
            pltpu.VMEM((3, 2, n * rows, block), F32), pltpu.VMEM((3, 2, n * rows, block), F32),
            pltpu.VMEM((rows, d), BF16), pltpu.VMEM((n, rows, d), BF16), pltpu.VMEM((n * rows, d), F32),
            pltpu.VMEM((n, rows, vocab), F32), pltpu.VMEM((rows, n * vocab), F32),
            pltpu.SemaphoreType.DMA((5,)), pltpu.SemaphoreType.DMA((4, 4)), pltpu.SemaphoreType.DMA((stages, n)), pltpu.SemaphoreType.DMA((stages, n)),
        ],
        compiler_params=params(58, 1),
        cost_estimate=cost(n * rows * weights, weights),
        name="tail",
    )(o, x, gm, gf, w_out, w_gate, w_up, w_down, emb)


def solution(mesh):
    row_spec = P(("part", "dp"))
    layer_spec = P(None, "dp")

    def device_step(hidden, prompt_lens, g_attn, w_query, w_key, w_value, w_out, g_mlp, w_gate, w_up, w_down, g_final, embedding):
        batch, seq_len, dim = hidden.shape
        heads, head_dim = w_query.shape[2], w_query.shape[3]
        n_dev = dim // w_query.shape[1]
        freqs = rope_frequencies(head_dim)
        angles = freqs[:, None] * np.arange(seq_len, dtype=np.float32)[None]
        cos_es, sin_es = jnp.asarray(np.cos(angles)), jnp.asarray(np.sin(angles))

        def headed(w):
            return w.transpose(0, 2, 3, 1).reshape(w.shape[0], heads * head_dim, -1)

        wq_t, wk_t, wv_t = headed(w_query), headed(w_key), headed(w_value)
        kd = dim // n_dev
        gains_loc = jnp.concatenate([g_attn, g_mlp, g_final[None], jnp.zeros((3, kd), BF16)], axis=0).astype(F32)
        gains, normed, gqkv, go, gg1, gup1, gd1, pg2, pd2, pk1, pv1 = first_gather(
            gains_loc, hidden, wq_t, wk_t, wv_t, w_out, w_gate, w_up, w_down, n_dev)
        gains = gains.transpose(1, 0, 2).reshape(8, dim)
        gu2 = lax.all_gather(pg2, "dp", axis=1, tiled=True)
        gd2 = lax.all_gather(pd2, "dp", axis=0, tiled=True)
        gk1 = lax.all_gather(pk1, "dp", axis=1, tiled=True)
        gv1 = lax.all_gather(pv1, "dp", axis=1, tiled=True)
        ga0, ga1, gm0, gm1, gf, *_ = gains
        hd = heads * head_dim

        lens = prompt_lens
        rope = (cos_es, sin_es, head_dim)
        rows = batch * seq_len
        q0, k_cache, v_cache = project(normed.reshape(rows, dim), gqkv, *rope, (True, True, False), (1, 2, 2), 0)
        attended = attention(lens, q0, k_cache, v_cache, head_dim)
        proj = jnp.einsum("bks,kd->bsd", attended, go, preferred_element_type=F32)
        mid = (hidden.astype(F32) + proj).astype(BF16)
        mid = mid.reshape(rows, dim)
        act, normed_mlp = gate_up(mid, gm0[None], (gg1, gup1), gg1.shape[1])
        part = down(act, gd1, rows)
        [act] = gate_up(normed_mlp, None, (gu2,), gu2.shape[2])
        h1 = down(act, gd2, BAND, (mid, part))

        last = lens - 1
        x = jnp.take_along_axis(h1.reshape(batch, seq_len, dim), last[:, None, None], axis=1, mode="clip")[:, 0]
        q1 = last_query(rms_norm(x, ga1).astype(F32), wq_t, 1, n_dev).reshape(batch, heads, head_dim)
        half = head_dim // 2
        turn = last.astype(F32)[:, None, None] * freqs
        cos_b, sin_b = jnp.cos(turn), jnp.sin(turn)
        low, high = q1[..., :half], q1[..., half:]
        q1 = jnp.concatenate([low * cos_b - high * sin_b, high * cos_b + low * sin_b], axis=-1).astype(BF16)
        own = np.arange(hd)[None, :] // head_dim == np.arange(heads)[:, None]
        q_diag = jnp.where(own[None], q1.reshape(batch, 1, hd), jnp.zeros((), BF16))

        k_cache, normed1 = project(h1, gk1, *rope, (True,), (2,), 1, k_cache, ga1[None])
        [v_cache] = project(normed1, gv1, *rope, (False,), (2,), 1, v_cache)

        o1 = last_attention(lens, q_diag, k_cache, v_cache, head_dim, 1)
        logits = tail(o1, x.astype(F32), gm1[None], gf[None], w_out, w_gate, w_up, w_down, embedding, 1, n_dev)

        def cache(c):
            return c.reshape(2, batch, heads, head_dim, seq_len).transpose(0, 1, 4, 2, 3)

        return cache(k_cache), cache(v_cache), logits

    cache_spec = P(None, ("part", "dp"))
    return jax.shard_map(
        device_step,
        mesh=mesh,
        in_specs=(row_spec, row_spec) + (layer_spec,) * 9 + (P("dp"), P("dp")),
        out_specs=(cache_spec, cache_spec, row_spec),
        check_vma=False,
    )
```

time: 909 us -> 820 us (0.902)
  Pallas kernels: 275 us -> 762 us
  matrix products: 282 us -> 22.2 us
  waiting for transfers between devices: 241 us -> 1.96 us
  local copies, waits for them, and re-layouts: 41.3 us -> 8.01 us
  other arithmetic: 33.7 us -> 3.64 us
  blocking collectives: 14.5 us -> 0 us
    pallas_call x6 -> x9, Pallas kernels: 136 us -> 633 us  [the longest x1 247 us: first_gather(): pl.pallas_call(functools.partial(gather_body, n, plan, 9, len(outs)), out...]
    dot_general x4 -> x1, matrix products: 282 us -> 22.2 us  [device_step(): proj = jnp.einsum('bks,kd->bsd', attended, go, preferred_element_type=F32)]
    all_gather x5 -> x4, waiting for transfers between devices: 241 us -> 0.05 us  [the longest x1 0.02 us: device_step(): gk1 = lax.all_gather(pk1, 'dp', axis=1, tiled=True)]
    slice x8 -> x0, local copies, waits for them, and re-layouts: 24.5 us -> none  [the longest x1 4.75 us: device_step(): wd = lax.all_gather(w_down[0], 'dp', axis=0, tiled=True)]
    convert_element_type x2, other arithmetic: 17.2 us -> 1.34 us  [the longest x1 0.77 us: device_step(): jnp.concatenate([g_attn, g_mlp, g_final[None], jnp.zeros((3, kd), BF16)],...]
    all_gather x1 -> x0, blocking collectives: 14.5 us -> none  [device_step(): gains = lax.all_gather(gains_loc, 'dp', axis=1, tiled=True).astype(F32)]
    pallas_call x1, Pallas kernels: 63.9 us -> 54.2 us  [tail(): pl.pallas_call(functools.partial(tail_body, n, layer), out_shape=jax.Shap...]
    unnamed x46 -> x28, local copies, waits for them, and re-layouts: 14.1 us -> 4.99 us
  transfers between devices with their start and end apart: 5 -> 4, of which waited for: 3 -> 0; matrix products, arithmetic and copies ran while one was open for 37% -> 3% of each run, Pallas kernels for 17% -> 53%
where the time goes in v3:
time: 820 us; the launch traced here: 812 us
  Pallas kernels  762 us (93%)
  matrix products  22.2 us (3%)
  between operations  14.4 us (2%)
    pallas_call x1, Pallas kernels, first_gather(): pl.pallas_call(functools.partial(gather_body, n, plan, 9, len(outs)), out...  247 us
    pallas_call x2, Pallas kernels, gate_up(): pl.pallas_call(body, out_shape=out_shape, grid=(width // TILE, rows // BA...  163 us
    pallas_call x3, Pallas kernels, project(): pl.pallas_call(functools.partial(proj_body, ropes, per, head_dim, len(ali...  126 us
    pallas_call x2, Pallas kernels, down(): pl.pallas_call(functools.partial(down_body, bool(base)), out_shape=jax.Sh...  87.3 us
    pallas_call x1, Pallas kernels, attention(): pl.pallas_call(functools.partial(attn_body, head_dim), out_shape=jax.Shap...  65.4 us
    pallas_call x1, Pallas kernels, tail(): pl.pallas_call(functools.partial(tail_body, n, layer), out_shape=jax.Shap...  54.2 us
    dot_general x1, matrix products, device_step(): proj = jnp.einsum('bks,kd->bsd', attended, go, preferred_element_type=F32)  22.2 us
  transfers between devices with their start and end apart: 4, of which 0 were waited for; matrix products, arithmetic and copies ran while one was open for 3% of the time, Pallas kernels for 53%

profile of v3, /device:TPU:0, one launch (start us, length us, event | category | flops | bytes accessed | tf_op | source)
XLA Modules:
  0.0 812.3 jit_solution(302811141352405636)
XLA Ops:
  7.2 0.0 all-gather.7.cloned.1.call-start
  7.2 0.7 broadcast_in_dim.32
  7.9 0.1 pad.7.clone
  8.0 0.8 maximum_convert_fusion.refs_0_
  8.7 1.6 copy-done
  10.3 246.7 %first_gather.1 = (f32[8,8,256]{2,1,0:T(8,128)S(1)}, bf16[4,512,2048]{2,1,0:T(8,128)(2,1)}, bf16[6144,2048]{1,0:T(8,128)(2,1)}, bf16[2048,2048]{1,0:T(8,128)(2,1...) custom-call(f32[8,256]{1,0:T(8,128)S(1)} %maximum_convert_fusion.ref, ...), custom_call_target="tpu_custom_call" | custom-call | flops 99999997952 | bytes 100000000 | tf_op jit(solution)/shard_map/first_gather/pallas_call | solution.py:586
  257.0 0.0 copy-start.2
  257.0 0.0 copy-start.5
  257.0 0.0 all-gather.7.cloned.1.call-update
  257.1 0.0 all-gather.9.cloned.1.call-start
  257.1 0.7 all-gather.9.cloned.1.call-update
  257.8 0.0 all-gather.5.cloned.1.call-start
  257.9 0.7 all-gather.5.cloned.1.call-update
  258.5 0.0 all-gather.11.cloned.1.call-start
  258.6 0.5 all-gather.11.cloned.1.call-update
  259.1 0.6 fusion.6
  259.8 0.6 add_convert_fusion.2
  260.3 0.5 or_bitcast_fusion
  260.9 0.7 copy.30
  261.5 67.7 %project.3 = (bf16[1,4,2048,512]{3,2,1,0:T(8,128)(2,1)}, bf16[2,4,2048,512]{3,2,1,0:T(8,128)(2,1)}, bf16[2,4,2048,512]{3,2,1,0:T(8,128)(2,1)}) custom-call(bf16[6144,2048]{1,0:T(8,128)(2,1)} %get-tuple-element.22.w_ref, bf16[2048,2048]{1,0:T(8,128)(2,1)} %bitcast.53, f32[32,512]{1,0:T(8,128)} %constant.28.clone.cos_ref, f32[32,512]{1,0:T(8,128)} %constant.29.clone.sin_ref), custom_call_target="tpu_custom_call" | custom-call | flops 51539607552 | bytes 41943040 | tf_op jit(solution)/shard_map/project/pallas_call | solution.py:122
  329.2 65.4 %attention.1 = bf16[4,2048,512]{2,1,0:T(8,128)(2,1)S(1)} custom-call(s32[4]{0:T(128)S(1)} %copy-done.2, bf16[1,4,2048,512]{3,2,1,0:T(8,128)(2,1)} %get-tuple-element.24.q_ref, bf16[2,4,2048,512]{3,2,1,0:T(8,128)(2,1)} %get-tuple-element.25.k_ref.rest_1_, bf16[2,4,2048,512]{3,2,1,0:T(8,128)(2,1)} %get-tuple-element.26.v_ref.rest_0_), custom_call_target="tpu_custom_call" | custom-call | flops 68719476736 | bytes 33554432 | tf_op jit(solution)/shard_map/attention/pallas_call | solution.py:242
  394.6 22.2 %add_convert_fusion = bf16[4,512,2048]{2,1,0:T(8,128)(2,1)} fusion(bf16[4,512,2048]{2,1,0:T(8,128)(2,1)} %refs_1_.1, bf16[4,2048,512]{2,1,0:T(8,128)(2,1)S(1)} %attention.1, bf16[2048,2048]{1,0:T(8,128)(2,1)} %get-tuple-element.27), kind=kOutput, calls=%fused_computation.1 | convolution fusion | flops 17192452096 | bytes 33554432 | tf_op jit(solution)/shard_map/bks,kd->bsd/dot_general | solution.py:758
  416.8 47.9 %gate_up.2 = (bf16[2048,2048]{1,0:T(8,128)(2,1)}, bf16[2048,2048]{1,0:T(8,128)(2,1)}) custom-call(bf16[2048,2048]{1,0:T(8,128)(2,1)} %bitcast.54, f32[1,2048]{1,0:T(1,128)} %bitcast.49, bf16[2048,2048]{1,0:T(8,128)(2,1)} %get-tuple-element.29.wg_ref, bf16[2048,2048]{1,0:T(8,128)(2,1)} %get-tuple-element.30.wu_ref), custom_call_target="tpu_custom_call" | custom-call | flops 34359738368 | bytes 33554432 | tf_op jit(solution)/shard_map/gate_up/pallas_call | solution.py:181
  464.7 24.3 %down.2.rest_1_ = f32[2048,2048]{1,0:T(8,128)} custom-call(bf16[2048,2048]{1,0:T(8,128)(2,1)} %get-tuple-element.34.a_ref, bf16[2048,2048]{1,0:T(8,128)(2,1)} %get-tuple-element.35.w_ref), custom_call_target="tpu_custom_call" | custom-call | flops 17179869184 | bytes 41943040 | tf_op jit(solution)/shard_map/down/pallas_call | solution.py:207
  489.0 0.7 multiply_cosine_fusion
  489.7 115.4 %gate_up.3.a_ref = bf16[2048,6144]{1,0:T(8,128)(2,1)} custom-call(bf16[2048,2048]{1,0:T(8,128)(2,1)} %get-tuple-element.31.m_ref, bf16[2,2048,6144]{2,1,0:T(8,128)(2,1)} %all-gather.7.cloned.1.call-done.wg_ref.wu_ref, bf16[2,2048,6144]{2,1,0:T(8,128)(2,1)} %all-gather.7.cloned.1.call-done.wg_ref.wu_ref), custom_call_target="tpu_custom_call" | custom-call | flops 103079215104 | bytes 83886080 | tf_op jit(solution)/shard_map/gate_up/pallas_call | solution.py:181
  605.1 0.0 copy-start.4
  605.1 0.0 all-gather.9.cloned.1.call-done.w_ref
  605.1 63.0 %down.3.a_ref = bf16[2048,2048]{1,0:T(8,128)(2,1)} custom-call(bf16[2048,6144]{1,0:T(8,128)(2,1)} %gate_up.3.a_ref, bf16[6144,2048]{1,0:T(8,128)(2,1)} %all-gather.9.cloned.1.call-done.w_ref, bf16[2048,2048]{1,0:T(8,128)(2,1)} %bitcast.55, f32[2048,2048]{1,0:T(8,128)} %down.2.rest_1_), custom_call_target="tpu_custom_call" | custom-call | flops 51539607552 | bytes 75497472 | tf_op jit(solution)/shard_map/down/pallas_call | solution.py:207
  668.1 0.0 copy-done.7
  668.1 1.4 gather_fusion
  669.6 0.6 convert_element_type.42.x_ref
  670.2 0.1 multiply_reduce_fusion
  670.3 0.1 fusion.4.a_ref
  670.4 10.4 %last_query.1 = f32[4,2048]{1,0:T(4,128)S(1)} custom-call(f32[4,2048]{1,0:T(4,128)S(1)} %fusion.4.a_ref, bf16[2,2048,256]{2,1,0:T(8,128)(2,1)S(1)} %bitcast.40), custom_call_target="tpu_custom_call" | custom-call | flops 33554432 | bytes 1048576 | tf_op jit(solution)/shard_map/last_query/pallas_call | solution.py:368
  680.8 0.1 reshape.117
  681.0 0.1 subtract_convert_fusion
  681.1 0.1 pad_maximum_fusion
  681.1 0.1 convert_element_type.40
  681.2 0.1 broadcast_select_fusion.q_ref
  681.3 0.0 all-gather.5.cloned.1.call-done.w_ref
  681.3 32.5 %project.4 = (bf16[2,4,2048,512]{3,2,1,0:T(8,128)(2,1)}, bf16[2048,2048]{1,0:T(8,128)(2,1)}) custom-call(bf16[2048,2048]{1,0:T(8,128)(2,1)} %all-gather.5.cloned.1.call-done.w_ref, bf16[2048,2048]{1,0:T(8,128)(2,1)} %down.3.a_ref, f32[32,512]{1,0:T(8,128)} %constant.28.clone.cos_ref, ...), custom_call_target="tpu_custom_call", output_to_operand_aliasing={{0}: (5, {})} | custom-call | flops 17179869184 | bytes 25165824 | tf_op jit(solution)/shard_map/project/pallas_call | solution.py:122
  713.9 25.3 %project.5.v_ref = bf16[2,4,2048,512]{3,2,1,0:T(8,128)(2,1)} custom-call(bf16[2048,2048]{1,0:T(8,128)(2,1)} %all-gather.11.cloned.1.call-done.w_ref, bf16[2048,2048]{1,0:T(8,128)(2,1)} %get-tuple-element.38.a_ref, f32[32,512]{1,0:T(8,128)} %constant.28.clone.cos_ref, f32[32,512]{1,0:T(8,128)} %constant.29.clone.sin_ref, ...), custom_call_target="tpu_custom_call", output_to_operand_aliasing={{}: (4, {})} | custom-call | flops 17179869184 | bytes 25165824 | tf_op jit(solution)/shard_map/project/pallas_call | solution.py:122
  739.2 0.0 copy-done.3
  739.2 9.2 %last_attention.1 = f32[4,1,2048]{2,1,0:T(1,128)S(1)} custom-call(s32[4]{0:T(128)S(1)} %copy-done.3, bf16[4,32,2048]{2,1,0:T(8,128)(2,1)S(1)} %broadcast_select_fusion.q_ref, bf16[2,4,2048,512]{3,2,1,0:T(8,128)(2,1)} %get-tuple-element.36.k_ref, bf16[2,4,2048,512]{3,2,1,0:T(8,128)(2,1)} %project.5.v_ref), custom_call_target="tpu_custom_call" | custom-call | flops 536870912 | bytes 16777216 | tf_op jit(solution)/shard_map/last_attention/pallas_call | solution.py:276
  748.4 0.6 copy.26
  749.1 54.2 %tail.1 = f32[4,49152]{1,0:T(4,128)} custom-call(f32[4,2048]{1,0:T(4,128)} %bitcast.44, f32[4,2048]{1,0:T(4,128)} %convert_element_type.42.x_ref, f32[1,2048]{1,0:T(1,128)} %bitcast.46, f32[1,2048]{1,0:T(1,128)} %bitcast.45, bf16[2,256,2048]{2,1,0:T(8,128)(2,1)} %wo_hbm.1, bf16[2,256,8192]{2,1,0:T(8,128)(2,1)} %wg_hbm.1, bf16[2,256,8192]{2,1,0:T(8,128)(2,1)} %wu_hbm.1, ...), custom_call_target="tpu_custom_call" | custom-call | flops 1241513984 | bytes 38797312 | tf_op jit(solution)/shard_map/tail/pallas_call | solution.py:702
  803.3 2.1 copy.31
  (24 shorter events, 0.1 us)
Async XLA Ops:
  7.2 482.5 %all-gather.7.cloned.1.call-start = ((), (), s32[]{:S(2)}) async-start(), calls=%async_computation.1 | async-start | bytes 56623104 | tf_op jit(solution)/shard_map/all_gather | solution.py:746
  8.7 1.6 copy-start
  257.0 2.7 copy-start.2
  257.0 3.9 copy-start.5
  257.1 348.1 %all-gather.9.cloned.1.call-start = ((), (), s32[]{:S(2)}) async-start(), calls=%async_computation.2 | async-start | bytes 28311552 | tf_op jit(solution)/shard_map/all_gather | solution.py:747
  257.8 423.5 %all-gather.5.cloned.1.call-start = ((), (), s32[]{:S(2)}) async-start(), calls=%async_computation | async-start | bytes 9437184 | tf_op jit(solution)/shard_map/all_gather | solution.py:748
  258.5 455.3 %all-gather.11.cloned.1.call-start = ((), (), s32[]{:S(2)}) async-start(), calls=%async_computation.3 | async-start | bytes 9437184 | tf_op jit(solution)/shard_map/all_gather | solution.py:749
  464.7 24.3 %copy-start.10 = (f32[32]{0:T(128)S(1)}, f32[32]{0:T(128)}, u32[]{:S(2)}) copy-start(f32[32]{0:T(128)} %constant.30.clone) | copy-start | bytes 388
  464.7 24.3 %copy-start.11 = (f32[4]{0:T(128)S(1)}, f32[4]{0:T(128)}, u32[]{:S(2)}) copy-start(f32[4]{0:T(128)} %get-tuple-element.47) | copy-start | bytes 52
  605.0 63.1 %copy-start.7 = (s32[4]{0:T(128)S(1)}, s32[4]{0:T(128)}, u32[]{:S(2)}) copy-start(s32[4]{0:T(128)} %or_bitcast_fusion) | copy-start | bytes 52
  605.0 65.3 %copy-start.6 = (f32[1,8,256]{2,0,1:T(1,128)S(1)}, f32[1,8,256]{2,0,1:T(1,128)}, u32[]{:S(2)}) copy-start(f32[1,8,256]{2,0,1:T(1,128)} %get-tuple-element.43) | copy-start | bytes 24580
  605.0 65.3 %copy-start.1 = (bf16[2,256,32,64]{1,3,2,0:T(8,128)(2,1)S(1)}, bf16[2,256,32,64]{1,3,2,0:T(8,128)(2,1)}, u32[]{:S(2)}) copy-start(bf16[2,256,32,64]{1,3,2,0:T(8,128)(2,1)} %param.20) | copy-start | bytes 6291460
  605.1 75.9 %copy-start.8 = (f32[4,32]{1,0:T(4,128)S(1)}, f32[4,32]{1,0:T(4,128)}, u32[]{:S(2)}) copy-start(f32[4,32]{1,0:T(4,128)} %get-tuple-element.45) | copy-start | bytes 1540
  605.1 75.9 %copy-start.9 = (f32[4,32]{1,0:T(4,128)S(1)}, f32[4,32]{1,0:T(4,128)}, u32[]{:S(2)}) copy-start(f32[4,32]{1,0:T(4,128)} %get-tuple-element.46) | copy-start | bytes 1540
  605.1 76.2 %copy-start.4 = (pred[32,2048]{1,0:T(8,128)(4,1)S(1)}, pred[32,2048]{1,0:T(8,128)(4,1)}, u32[]{:S(2)}) copy-start(pred[32,2048]{1,0:T(8,128)(4,1)} %copy.30) | copy-start | bytes 196612
  713.9 25.3 %copy-start.3 = (s32[4]{0:T(128)S(1)}, s32[4]{0:T(128)}, u32[]{:S(2)}) copy-start(s32[4]{0:T(128)} %lens_ref.3) | copy-start | bytes 52
Sparse Core Ops, SparseCore 0:
  257.2 226.3 all-gather.6
  485.3 119.6 all-gather.8
  606.8 49.9 all-gather.4
  658.5 52.6 all-gather.10

commit v4 on v3

--- a/solution.py
+++ b/solution.py
@@ -61,13 +61,10 @@
         gain_ref, a_src, a_ref = rest[0], a_ref, rest[-1]
         rest = rest[1:-1]
 
-        @pl.when((pl.program_id(0) == 0) & (pl.program_id(1) == 0))
-        def _():
-            normalize(a_src, gain_ref, a_ref)
+        pl.when(pl.program_id(1) == 0)(lambda: normalize(a_src, gain_ref, a_ref))
 
     outs = rest[n_prev:]
-    first = pl.multiple_of(pl.program_id(1) * PAIR * s, PAIR * s)
-    y = dot_nt(w_ref[...], a_ref[pl.ds(first, PAIR * s)])
+    y = dot_nt(w_ref[...], a_ref[...])
 
     def store(rope, out_ref):
         for t in range(PAIR):
@@ -83,7 +80,7 @@
                 out_ref[0, t, pl.ds(i * head_dim + half, half)] = (high * cos + low * sin).astype(BF16)
 
     for k, (rope, out_ref) in enumerate(zip(ropes, outs)):
-        pl.when(pl.program_id(0) // per == k)(functools.partial(store, rope, out_ref))
+        pl.when(pl.program_id(1) // per == k)(functools.partial(store, rope, out_ref))
 
 
 def project(a, w, cos, sin, head_dim, ropes, layers, layer, prev=None, gain=None):
@@ -91,20 +88,20 @@
     s = cos.shape[1]
     b, width = rows // s, w.shape[0] // len(ropes)
     per = width // ROWS
-    last = b // PAIR - 1
+    band = pl.BlockSpec((PAIR * s, d), lambda j, i: (j, 0))
 
     def place(k):
-        def index(i, j):
+        def index(j, i):
             at = i - k * per
-            inside = (at >= 0) & (at < per)
-            return layer, jnp.where(inside, j, jnp.where(at < 0, 0, last)), jnp.clip(at, 0, per - 1), 0
+            waits = (at < 0) & (j > 0)
+            return layer, jnp.where(waits, j - 1, j), jnp.where(waits, per - 1, jnp.clip(at, 0, per - 1)), 0
         return pl.BlockSpec((1, PAIR, ROWS, s), index)
 
     in_specs = [
-        pl.BlockSpec((ROWS, d), lambda i, j: (i, 0)),
-        pl.BlockSpec((rows, d), lambda i, j: (0, 0)),
-        pl.BlockSpec(cos.shape, lambda i, j: (0, 0)),
-        pl.BlockSpec(sin.shape, lambda i, j: (0, 0)),
+        pl.BlockSpec((ROWS, d), lambda j, i: (i, 0)),
+        band,
+        pl.BlockSpec(cos.shape, lambda j, i: (0, 0)),
+        pl.BlockSpec(sin.shape, lambda j, i: (0, 0)),
     ]
     args = [w, a, cos, sin]
     alias = {}
@@ -114,7 +111,7 @@
         in_specs.append(pl.BlockSpec(gain.shape, lambda i, j: (0, 0)))
         args.append(gain)
         out_shape.append(jax.ShapeDtypeStruct(a.shape, BF16))
-        out_specs.append(pl.BlockSpec(a.shape, lambda i, j: (0, 0)))
+        out_specs.append(band)
     if prev is not None:
         alias = {len(args): 0}
         in_specs.append(HBM)
@@ -122,7 +119,7 @@
     return pl.pallas_call(
         functools.partial(proj_body, ropes, per, head_dim, len(alias), gain is not None),
         out_shape=out_shape,
-        grid=(w.shape[0] // ROWS, b // PAIR),
+        grid=(b // PAIR, w.shape[0] // ROWS),
         in_specs=in_specs,
         out_specs=out_specs,
         input_output_aliases=alias,
@@ -637,21 +634,27 @@
     along = (at.xn, at.yn, at.dg, me)
     to_sib = [remote(sib_send.at[k], sib_got.at[k], pair_sems.at[0, k], pair_sems.at[1, k], at.sib) for k in range(4)]
     to_chip = [remote(gate_send.at[k], gate_got.at[k], pair_sems.at[2, k], pair_sems.at[3, k], along[k]) for k in range(3)]
-    order = (2, 0, 1, 3)
-    for k in order:
-        gate, up = gate_up(across[k])
-        sib_send[k, 0] = gate
-        sib_send[k, 1] = up
+
+    def pass_across(k):
+        sib_send[k, 0], sib_send[k, 1] = gate_up(across[k])
         to_sib[k].start()
-    for k in order:
+
+    def pass_along(k):
         gate, up = gate_up(along[k])
         to_sib[k].wait_recv()
         gate = gate + sib_got[k, 0]
         up = up + sib_got[k, 1]
         if along[k] is not me:
-            gate_send[k, 0] = gate
-            gate_send[k, 1] = up
+            gate_send[k, 0], gate_send[k, 1] = gate, up
             to_chip[k].start()
+        return gate, up
+
+    order = (2, 0, 1, 3)
+    pass_across(order[0])
+    for k, after in zip(order, order[1:]):
+        pass_across(after)
+        pass_along(k)
+    gate, up = pass_along(order[-1])
     for k in range(3):
         to_chip[k].wait_recv()
         gate = gate + gate_got[k, 0]

time: 820 us -> 816 us (level)
  transfers between devices with their start and end apart: 4 -> 4, of which waited for: 0 -> 2; matrix products, arithmetic and copies ran while one was open for 3% -> 3% of each run, Pallas kernels for 53% -> 52%
where the time goes in v4:
time: 816 us; the launch traced here: 809 us
  Pallas kernels  757 us (93%)
  matrix products  22.2 us (3%)
  between operations  14.3 us (2%)
    pallas_call x1, Pallas kernels, first_gather(): pl.pallas_call(functools.partial(gather_body, n, plan, 9, len(outs)), out...  247 us
    pallas_call x2, Pallas kernels, gate_up(): pl.pallas_call(body, out_shape=out_shape, grid=(width // TILE, rows // BA...  163 us
    pallas_call x3, Pallas kernels, project(): pl.pallas_call(functools.partial(proj_body, ropes, per, head_dim, len(ali...  121 us
    pallas_call x2, Pallas kernels, down(): pl.pallas_call(functools.partial(down_body, bool(base)), out_shape=jax.Sh...  87.1 us
    pallas_call x1, Pallas kernels, attention(): pl.pallas_call(functools.partial(attn_body, head_dim), out_shape=jax.Shap...  65.4 us
    pallas_call x1, Pallas kernels, tail(): pl.pallas_call(functools.partial(tail_body, n, layer), out_shape=jax.Shap...  54.4 us
    dot_general x1, matrix products, device_step(): proj = jnp.einsum('bks,kd->bsd', attended, go, preferred_element_type=F32)  22.2 us
  transfers between devices with their start and end apart: 4, of which 2 were waited for; matrix products, arithmetic and copies ran while one was open for 3% of the time, Pallas kernels for 52%

profile of v4, /device:TPU:0, one launch (start us, length us, event | category | flops | bytes accessed | tf_op | source)
XLA Modules:
  0.0 809.0 jit_solution(10433451095034058537)
XLA Ops:
  7.2 0.0 all-gather.7.cloned.1.call-start
  7.2 0.7 broadcast_in_dim.32
  7.9 0.1 pad.7.clone
  8.0 0.8 maximum_convert_fusion.refs_0_
  8.7 1.6 copy-done
  10.3 246.7 %first_gather.1 = (f32[8,8,256]{2,1,0:T(8,128)S(1)}, bf16[4,512,2048]{2,1,0:T(8,128)(2,1)}, bf16[6144,2048]{1,0:T(8,128)(2,1)}, bf16[2048,2048]{1,0:T(8,128)(2,1...) custom-call(f32[8,256]{1,0:T(8,128)S(1)} %maximum_convert_fusion.ref, ...), custom_call_target="tpu_custom_call" | custom-call | flops 99999997952 | bytes 100000000 | tf_op jit(solution)/shard_map/first_gather/pallas_call | solution.py:583
  257.0 0.0 copy-start.2
  257.0 0.0 copy-start.5
  257.0 0.0 all-gather.7.cloned.1.call-update
  257.1 0.0 all-gather.9.cloned.1.call-start
  257.1 0.7 all-gather.9.cloned.1.call-update
  257.8 0.0 all-gather.5.cloned.1.call-start
  257.9 0.7 all-gather.5.cloned.1.call-update
  258.5 0.0 all-gather.11.cloned.1.call-start
  258.6 0.5 all-gather.11.cloned.1.call-update
  259.1 0.6 fusion.6
  259.8 0.6 add_convert_fusion.2
  260.3 0.5 or_bitcast_fusion
  260.9 0.0 copy-done.5
  260.9 0.7 copy.30
  261.5 66.5 %project.3 = (bf16[1,4,2048,512]{3,2,1,0:T(8,128)(2,1)}, bf16[2,4,2048,512]{3,2,1,0:T(8,128)(2,1)}, bf16[2,4,2048,512]{3,2,1,0:T(8,128)(2,1)}) custom-call(bf16[6144,2048]{1,0:T(8,128)(2,1)} %get-tuple-element.22.w_ref, bf16[2048,2048]{1,0:T(8,128)(2,1)} %bitcast.53, f32[32,512]{1,0:T(8,128)} %constant.28.clone.cos_ref, f32[32,512]{1,0:T(8,128)} %constant.29.clone.sin_ref), custom_call_target="tpu_custom_call" | custom-call | flops 51539607552 | bytes 41943040 | tf_op jit(solution)/shard_map/project/pallas_call | solution.py:119
  328.1 65.4 %attention.1 = bf16[4,2048,512]{2,1,0:T(8,128)(2,1)S(1)} custom-call(s32[4]{0:T(128)S(1)} %copy-done.2, bf16[1,4,2048,512]{3,2,1,0:T(8,128)(2,1)} %get-tuple-element.24.q_ref, bf16[2,4,2048,512]{3,2,1,0:T(8,128)(2,1)} %get-tuple-element.25.k_ref.rest_1_, bf16[2,4,2048,512]{3,2,1,0:T(8,128)(2,1)} %get-tuple-element.26.v_ref.rest_0_), custom_call_target="tpu_custom_call" | custom-call | flops 68719476736 | bytes 33554432 | tf_op jit(solution)/shard_map/attention/pallas_call | solution.py:239
  393.4 22.2 %add_convert_fusion = bf16[4,512,2048]{2,1,0:T(8,128)(2,1)} fusion(bf16[4,512,2048]{2,1,0:T(8,128)(2,1)} %refs_1_.1, bf16[4,2048,512]{2,1,0:T(8,128)(2,1)S(1)} %attention.1, bf16[2048,2048]{1,0:T(8,128)(2,1)} %get-tuple-element.27), kind=kOutput, calls=%fused_computation.1 | convolution fusion | flops 17192452096 | bytes 33554432 | tf_op jit(solution)/shard_map/bks,kd->bsd/dot_general | solution.py:761
  415.6 47.9 %gate_up.2 = (bf16[2048,2048]{1,0:T(8,128)(2,1)}, bf16[2048,2048]{1,0:T(8,128)(2,1)}) custom-call(bf16[2048,2048]{1,0:T(8,128)(2,1)} %bitcast.54, f32[1,2048]{1,0:T(1,128)} %bitcast.49, bf16[2048,2048]{1,0:T(8,128)(2,1)} %get-tuple-element.29.wg_ref, bf16[2048,2048]{1,0:T(8,128)(2,1)} %get-tuple-element.30.wu_ref), custom_call_target="tpu_custom_call" | custom-call | flops 34359738368 | bytes 33554432 | tf_op jit(solution)/shard_map/gate_up/pallas_call | solution.py:178
  463.5 24.3 %down.2.rest_1_ = f32[2048,2048]{1,0:T(8,128)} custom-call(bf16[2048,2048]{1,0:T(8,128)(2,1)} %get-tuple-element.34.a_ref, bf16[2048,2048]{1,0:T(8,128)(2,1)} %get-tuple-element.35.w_ref), custom_call_target="tpu_custom_call" | custom-call | flops 17179869184 | bytes 41943040 | tf_op jit(solution)/shard_map/down/pallas_call | solution.py:204
  487.8 0.7 multiply_cosine_fusion
  488.5 115.4 %gate_up.3.a_ref = bf16[2048,6144]{1,0:T(8,128)(2,1)} custom-call(bf16[2048,2048]{1,0:T(8,128)(2,1)} %get-tuple-element.31.m_ref, bf16[2,2048,6144]{2,1,0:T(8,128)(2,1)} %all-gather.7.cloned.1.call-done.wg_ref.wu_ref, bf16[2,2048,6144]{2,1,0:T(8,128)(2,1)} %all-gather.7.cloned.1.call-done.wg_ref.wu_ref), custom_call_target="tpu_custom_call" | custom-call | flops 103079215104 | bytes 83886080 | tf_op jit(solution)/shard_map/gate_up/pallas_call | solution.py:178
  603.9 0.0 copy-start.4
  603.9 1.1 all-gather.9.cloned.1.call-done.w_ref
  605.1 62.8 %down.3.a_ref = bf16[2048,2048]{1,0:T(8,128)(2,1)} custom-call(bf16[2048,6144]{1,0:T(8,128)(2,1)} %gate_up.3.a_ref, bf16[6144,2048]{1,0:T(8,128)(2,1)} %all-gather.9.cloned.1.call-done.w_ref, bf16[2048,2048]{1,0:T(8,128)(2,1)} %bitcast.55, f32[2048,2048]{1,0:T(8,128)} %down.2.rest_1_), custom_call_target="tpu_custom_call" | custom-call | flops 51539607552 | bytes 75497472 | tf_op jit(solution)/shard_map/down/pallas_call | solution.py:204
  667.9 1.4 gather_fusion
  669.4 0.6 convert_element_type.42.x_ref
  670.0 0.1 multiply_reduce_fusion
  670.1 0.1 fusion.4.a_ref
  670.2 10.6 %last_query.1 = f32[4,2048]{1,0:T(4,128)S(1)} custom-call(f32[4,2048]{1,0:T(4,128)S(1)} %fusion.4.a_ref, bf16[2,2048,256]{2,1,0:T(8,128)(2,1)S(1)} %bitcast.40), custom_call_target="tpu_custom_call" | custom-call | flops 33554432 | bytes 1048576 | tf_op jit(solution)/shard_map/last_query/pallas_call | solution.py:365
  680.8 0.1 reshape.117
  680.9 0.1 subtract_convert_fusion
  681.0 0.1 pad_maximum_fusion
  681.1 0.1 convert_element_type.40
  681.2 0.1 broadcast_select_fusion.q_ref
  681.2 0.0 all-gather.5.cloned.1.call-done.w_ref
  681.3 30.1 %project.4 = (bf16[2,4,2048,512]{3,2,1,0:T(8,128)(2,1)}, bf16[2048,2048]{1,0:T(8,128)(2,1)}) custom-call(bf16[2048,2048]{1,0:T(8,128)(2,1)} %all-gather.5.cloned.1.call-done.w_ref, bf16[2048,2048]{1,0:T(8,128)(2,1)} %down.3.a_ref, f32[32,512]{1,0:T(8,128)} %constant.28.clone.cos_ref, ...), custom_call_target="tpu_custom_call", output_to_operand_aliasing={{0}: (5, {})} | custom-call | flops 17179869184 | bytes 25165824 | tf_op jit(solution)/shard_map/project/pallas_call | solution.py:119
  711.4 0.2 all-gather.11.cloned.1.call-done.w_ref
  711.6 24.1 %project.5.v_ref = bf16[2,4,2048,512]{3,2,1,0:T(8,128)(2,1)} custom-call(bf16[2048,2048]{1,0:T(8,128)(2,1)} %all-gather.11.cloned.1.call-done.w_ref, bf16[2048,2048]{1,0:T(8,128)(2,1)} %get-tuple-element.38.a_ref, f32[32,512]{1,0:T(8,128)} %constant.28.clone.cos_ref, f32[32,512]{1,0:T(8,128)} %constant.29.clone.sin_ref, ...), custom_call_target="tpu_custom_call", output_to_operand_aliasing={{}: (4, {})} | custom-call | flops 17179869184 | bytes 25165824 | tf_op jit(solution)/shard_map/project/pallas_call | solution.py:119
  735.7 9.2 %last_attention.1 = f32[4,1,2048]{2,1,0:T(1,128)S(1)} custom-call(s32[4]{0:T(128)S(1)} %copy-done.3, bf16[4,32,2048]{2,1,0:T(8,128)(2,1)S(1)} %broadcast_select_fusion.q_ref, bf16[2,4,2048,512]{3,2,1,0:T(8,128)(2,1)} %get-tuple-element.36.k_ref, bf16[2,4,2048,512]{3,2,1,0:T(8,128)(2,1)} %project.5.v_ref), custom_call_target="tpu_custom_call" | custom-call | flops 536870912 | bytes 16777216 | tf_op jit(solution)/shard_map/last_attention/pallas_call | solution.py:273
  744.9 0.6 copy.26
  745.5 54.4 %tail.1 = f32[4,49152]{1,0:T(4,128)} custom-call(f32[4,2048]{1,0:T(4,128)} %bitcast.44, f32[4,2048]{1,0:T(4,128)} %convert_element_type.42.x_ref, f32[1,2048]{1,0:T(1,128)} %bitcast.46, f32[1,2048]{1,0:T(1,128)} %bitcast.45, bf16[2,256,2048]{2,1,0:T(8,128)(2,1)} %wo_hbm.1, bf16[2,256,8192]{2,1,0:T(8,128)(2,1)} %wg_hbm.1, bf16[2,256,8192]{2,1,0:T(8,128)(2,1)} %wu_hbm.1, ...), custom_call_target="tpu_custom_call" | custom-call | flops 1241513984 | bytes 38797312 | tf_op jit(solution)/shard_map/tail/pallas_call | solution.py:705
  799.9 2.1 copy.31
  (24 shorter events, 0.1 us)
Async XLA Ops:
  7.2 481.4 %all-gather.7.cloned.1.call-start = ((), (), s32[]{:S(2)}) async-start(), calls=%async_computation.1 | async-start | bytes 56623104 | tf_op jit(solution)/shard_map/all_gather | solution.py:749
  8.7 1.6 copy-start
  257.0 2.7 copy-start.2
  257.0 3.9 copy-start.5
  257.1 348.0 %all-gather.9.cloned.1.call-start = ((), (), s32[]{:S(2)}) async-start(), calls=%async_computation.2 | async-start | bytes 28311552 | tf_op jit(solution)/shard_map/all_gather | solution.py:750
  257.8 423.5 %all-gather.5.cloned.1.call-start = ((), (), s32[]{:S(2)}) async-start(), calls=%async_computation | async-start | bytes 9437184 | tf_op jit(solution)/shard_map/all_gather | solution.py:751
  258.5 453.1 %all-gather.11.cloned.1.call-start = ((), (), s32[]{:S(2)}) async-start(), calls=%async_computation.3 | async-start | bytes 9437184 | tf_op jit(solution)/shard_map/all_gather | solution.py:752
  463.5 24.3 %copy-start.10 = (f32[32]{0:T(128)S(1)}, f32[32]{0:T(128)}, u32[]{:S(2)}) copy-start(f32[32]{0:T(128)} %constant.30.clone) | copy-start | bytes 388
  463.5 24.3 %copy-start.11 = (f32[4]{0:T(128)S(1)}, f32[4]{0:T(128)}, u32[]{:S(2)}) copy-start(f32[4]{0:T(128)} %get-tuple-element.47) | copy-start | bytes 52
  603.9 64.0 %copy-start.7 = (s32[4]{0:T(128)S(1)}, s32[4]{0:T(128)}, u32[]{:S(2)}) copy-start(s32[4]{0:T(128)} %or_bitcast_fusion) | copy-start | bytes 52
  603.9 66.2 %copy-start.6 = (f32[1,8,256]{2,0,1:T(1,128)S(1)}, f32[1,8,256]{2,0,1:T(1,128)}, u32[]{:S(2)}) copy-start(f32[1,8,256]{2,0,1:T(1,128)} %get-tuple-element.43) | copy-start | bytes 24580
  603.9 66.3 %copy-start.1 = (bf16[2,256,32,64]{1,3,2,0:T(8,128)(2,1)S(1)}, bf16[2,256,32,64]{1,3,2,0:T(8,128)(2,1)}, u32[]{:S(2)}) copy-start(bf16[2,256,32,64]{1,3,2,0:T(8,128)(2,1)} %param.20) | copy-start | bytes 6291460
  603.9 77.0 %copy-start.8 = (f32[4,32]{1,0:T(4,128)S(1)}, f32[4,32]{1,0:T(4,128)}, u32[]{:S(2)}) copy-start(f32[4,32]{1,0:T(4,128)} %get-tuple-element.45) | copy-start | bytes 1540
  603.9 77.0 %copy-start.9 = (f32[4,32]{1,0:T(4,128)S(1)}, f32[4,32]{1,0:T(4,128)}, u32[]{:S(2)}) copy-start(f32[4,32]{1,0:T(4,128)} %get-tuple-element.46) | copy-start | bytes 1540
  603.9 77.3 %copy-start.4 = (pred[32,2048]{1,0:T(8,128)(4,1)S(1)}, pred[32,2048]{1,0:T(8,128)(4,1)}, u32[]{:S(2)}) copy-start(pred[32,2048]{1,0:T(8,128)(4,1)} %copy.30) | copy-start | bytes 196612
  711.6 24.1 %copy-start.3 = (s32[4]{0:T(128)S(1)}, s32[4]{0:T(128)}, u32[]{:S(2)}) copy-start(s32[4]{0:T(128)} %lens_ref.3) | copy-start | bytes 52
Sparse Core Ops, SparseCore 0:
  257.2 226.3 all-gather.6
  485.4 119.6 all-gather.8
  606.9 49.9 all-gather.4
  658.6 53.0 all-gather.10

commit v5 on v4

--- a/solution.py
+++ b/solution.py
@@ -269,15 +269,16 @@
 def last_attention(lens, q_diag, k, v, head_dim, layer):
     b, heads, width = q_diag.shape
     s = k.shape[-1]
-    kv = pl.BlockSpec((1, 1, width, s), lambda i, lens: (layer, i, 0, 0))
+    parts = 2
+    kv = pl.BlockSpec((1, 1, width // parts, s), lambda i, p, lens: (layer, i, p, 0))
     return pl.pallas_call(
         functools.partial(last_body, head_dim),
         out_shape=jax.ShapeDtypeStruct((b, 1, width), F32),
         grid_spec=pltpu.PrefetchScalarGridSpec(
             num_scalar_prefetch=1,
-            grid=(b,),
-            in_specs=[pl.BlockSpec((1, heads, width), lambda i, lens: (i, 0, 0)), kv, kv],
-            out_specs=pl.BlockSpec((1, 1, width), lambda i, lens: (i, 0, 0)),
+            grid=(b, parts),
+            in_specs=[pl.BlockSpec((1, heads // parts, width // parts), lambda i, p, lens: (i, p, p)), kv, kv],
+            out_specs=pl.BlockSpec((1, 1, width // parts), lambda i, p, lens: (i, 0, p)),
         ),
         compiler_params=params(40),
         cost_estimate=cost(2 * b * s * width * heads, 2 * b * s * width, b * s * heads),

time: 816 us -> 818 us (level)
  no operation moved by 1% of the time
where the time goes in v5:
time: 818 us; the launch traced here: 811 us
  Pallas kernels  759 us (93%)
  matrix products  22.2 us (3%)
  between operations  14.3 us (2%)
    pallas_call x1, Pallas kernels, first_gather(): pl.pallas_call(functools.partial(gather_body, n, plan, 9, len(outs)), out...  247 us
    pallas_call x2, Pallas kernels, gate_up(): pl.pallas_call(body, out_shape=out_shape, grid=(width // TILE, rows // BA...  163 us
    pallas_call x3, Pallas kernels, project(): pl.pallas_call(functools.partial(proj_body, ropes, per, head_dim, len(ali...  121 us
    pallas_call x2, Pallas kernels, down(): pl.pallas_call(functools.partial(down_body, bool(base)), out_shape=jax.Sh...  87.1 us
    pallas_call x1, Pallas kernels, attention(): pl.pallas_call(functools.partial(attn_body, head_dim), out_shape=jax.Shap...  65.4 us
    pallas_call x1, Pallas kernels, tail(): pl.pallas_call(functools.partial(tail_body, n, layer), out_shape=jax.Shap...  54.4 us
    dot_general x1, matrix products, device_step(): proj = jnp.einsum('bks,kd->bsd', attended, go, preferred_element_type=F32)  22.2 us
  transfers between devices with their start and end apart: 4, of which 2 were waited for; matrix products, arithmetic and copies ran while one was open for 3% of the time, Pallas kernels for 52%

profile of v5, /device:TPU:0, one launch (start us, length us, event | category | flops | bytes accessed | tf_op | source)
XLA Modules:
  0.0 810.9 jit_solution(2109162136937338509)
XLA Ops:
  7.2 0.0 all-gather.7.cloned.1.call-start
  7.2 0.7 broadcast_in_dim.32
  7.9 0.1 pad.7.clone
  8.0 0.8 maximum_convert_fusion.refs_0_
  8.7 1.6 copy-done
  10.3 246.7 %first_gather.1 = (f32[8,8,256]{2,1,0:T(8,128)S(1)}, bf16[4,512,2048]{2,1,0:T(8,128)(2,1)}, bf16[6144,2048]{1,0:T(8,128)(2,1)}, bf16[2048,2048]{1,0:T(8,128)(2,1...) custom-call(f32[8,256]{1,0:T(8,128)S(1)} %maximum_convert_fusion.ref, ...), custom_call_target="tpu_custom_call" | custom-call | flops 99999997952 | bytes 100000000 | tf_op jit(solution)/shard_map/first_gather/pallas_call | solution.py:584
  257.0 0.0 copy-start.2
  257.0 0.0 copy-start.5
  257.0 0.0 all-gather.7.cloned.1.call-update
  257.1 0.0 all-gather.9.cloned.1.call-start
  257.1 0.7 all-gather.9.cloned.1.call-update
  257.8 0.0 all-gather.5.cloned.1.call-start
  257.9 0.7 all-gather.5.cloned.1.call-update
  258.5 0.0 all-gather.11.cloned.1.call-start
  258.6 0.5 all-gather.11.cloned.1.call-update
  259.1 0.6 fusion.6
  259.8 0.6 add_convert_fusion.2
  260.3 0.5 or_bitcast_fusion
  260.9 0.7 copy.30
  261.5 66.5 %project.3 = (bf16[1,4,2048,512]{3,2,1,0:T(8,128)(2,1)}, bf16[2,4,2048,512]{3,2,1,0:T(8,128)(2,1)}, bf16[2,4,2048,512]{3,2,1,0:T(8,128)(2,1)}) custom-call(bf16[6144,2048]{1,0:T(8,128)(2,1)} %get-tuple-element.22.w_ref, bf16[2048,2048]{1,0:T(8,128)(2,1)} %bitcast.53, f32[32,512]{1,0:T(8,128)} %constant.28.clone.cos_ref, f32[32,512]{1,0:T(8,128)} %constant.29.clone.sin_ref), custom_call_target="tpu_custom_call" | custom-call | flops 51539607552 | bytes 41943040 | tf_op jit(solution)/shard_map/project/pallas_call | solution.py:119
  328.1 65.4 %attention.1 = bf16[4,2048,512]{2,1,0:T(8,128)(2,1)S(1)} custom-call(s32[4]{0:T(128)S(1)} %copy-done.2, bf16[1,4,2048,512]{3,2,1,0:T(8,128)(2,1)} %get-tuple-element.24.q_ref, bf16[2,4,2048,512]{3,2,1,0:T(8,128)(2,1)} %get-tuple-element.25.k_ref.rest_1_, bf16[2,4,2048,512]{3,2,1,0:T(8,128)(2,1)} %get-tuple-element.26.v_ref.rest_0_), custom_call_target="tpu_custom_call" | custom-call | flops 68719476736 | bytes 33554432 | tf_op jit(solution)/shard_map/attention/pallas_call | solution.py:239
  393.4 22.2 %add_convert_fusion = bf16[4,512,2048]{2,1,0:T(8,128)(2,1)} fusion(bf16[4,512,2048]{2,1,0:T(8,128)(2,1)} %refs_1_.1, bf16[4,2048,512]{2,1,0:T(8,128)(2,1)S(1)} %attention.1, bf16[2048,2048]{1,0:T(8,128)(2,1)} %get-tuple-element.27), kind=kOutput, calls=%fused_computation.1 | convolution fusion | flops 17192452096 | bytes 33554432 | tf_op jit(solution)/shard_map/bks,kd->bsd/dot_general | solution.py:762
  415.6 47.9 %gate_up.2 = (bf16[2048,2048]{1,0:T(8,128)(2,1)}, bf16[2048,2048]{1,0:T(8,128)(2,1)}) custom-call(bf16[2048,2048]{1,0:T(8,128)(2,1)} %bitcast.54, f32[1,2048]{1,0:T(1,128)} %bitcast.49, bf16[2048,2048]{1,0:T(8,128)(2,1)} %get-tuple-element.29.wg_ref, bf16[2048,2048]{1,0:T(8,128)(2,1)} %get-tuple-element.30.wu_ref), custom_call_target="tpu_custom_call" | custom-call | flops 34359738368 | bytes 33554432 | tf_op jit(solution)/shard_map/gate_up/pallas_call | solution.py:178
  463.5 24.3 %down.2.rest_1_ = f32[2048,2048]{1,0:T(8,128)} custom-call(bf16[2048,2048]{1,0:T(8,128)(2,1)} %get-tuple-element.34.a_ref, bf16[2048,2048]{1,0:T(8,128)(2,1)} %get-tuple-element.35.w_ref), custom_call_target="tpu_custom_call" | custom-call | flops 17179869184 | bytes 41943040 | tf_op jit(solution)/shard_map/down/pallas_call | solution.py:204
  487.8 0.0 copy-done.11
  487.8 0.7 multiply_cosine_fusion
  488.5 115.4 %gate_up.3.a_ref = bf16[2048,6144]{1,0:T(8,128)(2,1)} custom-call(bf16[2048,2048]{1,0:T(8,128)(2,1)} %get-tuple-element.31.m_ref, bf16[2,2048,6144]{2,1,0:T(8,128)(2,1)} %all-gather.7.cloned.1.call-done.wg_ref.wu_ref, bf16[2,2048,6144]{2,1,0:T(8,128)(2,1)} %all-gather.7.cloned.1.call-done.wg_ref.wu_ref), custom_call_target="tpu_custom_call" | custom-call | flops 103079215104 | bytes 83886080 | tf_op jit(solution)/shard_map/gate_up/pallas_call | solution.py:178
  603.9 0.0 copy-start.4
  603.9 1.1 all-gather.9.cloned.1.call-done.w_ref
  605.1 62.8 %down.3.a_ref = bf16[2048,2048]{1,0:T(8,128)(2,1)} custom-call(bf16[2048,6144]{1,0:T(8,128)(2,1)} %gate_up.3.a_ref, bf16[6144,2048]{1,0:T(8,128)(2,1)} %all-gather.9.cloned.1.call-done.w_ref, bf16[2048,2048]{1,0:T(8,128)(2,1)} %bitcast.55, f32[2048,2048]{1,0:T(8,128)} %down.2.rest_1_), custom_call_target="tpu_custom_call" | custom-call | flops 51539607552 | bytes 75497472 | tf_op jit(solution)/shard_map/down/pallas_call | solution.py:204
  667.9 1.4 gather_fusion
  669.4 0.6 convert_element_type.42.x_ref
  670.0 0.1 multiply_reduce_fusion
  670.1 0.1 fusion.4.a_ref
  670.2 10.6 %last_query.1 = f32[4,2048]{1,0:T(4,128)S(1)} custom-call(f32[4,2048]{1,0:T(4,128)S(1)} %fusion.4.a_ref, bf16[2,2048,256]{2,1,0:T(8,128)(2,1)S(1)} %bitcast.40), custom_call_target="tpu_custom_call" | custom-call | flops 33554432 | bytes 1048576 | tf_op jit(solution)/shard_map/last_query/pallas_call | solution.py:366
  680.8 0.1 reshape.117
  680.9 0.1 subtract_convert_fusion
  681.0 0.1 pad_maximum_fusion
  681.1 0.1 convert_element_type.40
  681.2 0.1 broadcast_select_fusion.q_ref
  681.2 0.0 all-gather.5.cloned.1.call-done.w_ref
  681.3 30.1 %project.4 = (bf16[2,4,2048,512]{3,2,1,0:T(8,128)(2,1)}, bf16[2048,2048]{1,0:T(8,128)(2,1)}) custom-call(bf16[2048,2048]{1,0:T(8,128)(2,1)} %all-gather.5.cloned.1.call-done.w_ref, bf16[2048,2048]{1,0:T(8,128)(2,1)} %down.3.a_ref, f32[32,512]{1,0:T(8,128)} %constant.28.clone.cos_ref, ...), custom_call_target="tpu_custom_call", output_to_operand_aliasing={{0}: (5, {})} | custom-call | flops 17179869184 | bytes 25165824 | tf_op jit(solution)/shard_map/project/pallas_call | solution.py:119
  711.4 0.2 all-gather.11.cloned.1.call-done.w_ref
  711.6 24.1 %project.5.v_ref = bf16[2,4,2048,512]{3,2,1,0:T(8,128)(2,1)} custom-call(bf16[2048,2048]{1,0:T(8,128)(2,1)} %all-gather.11.cloned.1.call-done.w_ref, bf16[2048,2048]{1,0:T(8,128)(2,1)} %get-tuple-element.38.a_ref, f32[32,512]{1,0:T(8,128)} %constant.28.clone.cos_ref, f32[32,512]{1,0:T(8,128)} %constant.29.clone.sin_ref, ...), custom_call_target="tpu_custom_call", output_to_operand_aliasing={{}: (4, {})} | custom-call | flops 17179869184 | bytes 25165824 | tf_op jit(solution)/shard_map/project/pallas_call | solution.py:119
  735.7 11.1 %last_attention.1 = f32[4,1,2048]{2,1,0:T(1,128)S(1)} custom-call(s32[4]{0:T(128)S(1)} %copy-done.3, bf16[4,32,2048]{2,1,0:T(8,128)(2,1)S(1)} %broadcast_select_fusion.q_ref, bf16[2,4,2048,512]{3,2,1,0:T(8,128)(2,1)} %get-tuple-element.36.k_ref, bf16[2,4,2048,512]{3,2,1,0:T(8,128)(2,1)} %project.5.v_ref), custom_call_target="tpu_custom_call" | custom-call | flops 536870912 | bytes 16777216 | tf_op jit(solution)/shard_map/last_attention/pallas_call | solution.py:274
  746.8 0.6 copy.26
  747.4 54.4 %tail.1 = f32[4,49152]{1,0:T(4,128)} custom-call(f32[4,2048]{1,0:T(4,128)} %bitcast.44, f32[4,2048]{1,0:T(4,128)} %convert_element_type.42.x_ref, f32[1,2048]{1,0:T(1,128)} %bitcast.46, f32[1,2048]{1,0:T(1,128)} %bitcast.45, bf16[2,256,2048]{2,1,0:T(8,128)(2,1)} %wo_hbm.1, bf16[2,256,8192]{2,1,0:T(8,128)(2,1)} %wg_hbm.1, bf16[2,256,8192]{2,1,0:T(8,128)(2,1)} %wu_hbm.1, ...), custom_call_target="tpu_custom_call" | custom-call | flops 1241513984 | bytes 38797312 | tf_op jit(solution)/shard_map/tail/pallas_call | solution.py:706
  801.8 2.1 copy.31
  (24 shorter events, 0.1 us)
Async XLA Ops:
  7.2 481.4 %all-gather.7.cloned.1.call-start = ((), (), s32[]{:S(2)}) async-start(), calls=%async_computation.1 | async-start | bytes 56623104 | tf_op jit(solution)/shard_map/all_gather | solution.py:750
  8.7 1.6 copy-start
  257.0 2.7 copy-start.2
  257.0 3.9 copy-start.5
  257.1 348.0 %all-gather.9.cloned.1.call-start = ((), (), s32[]{:S(2)}) async-start(), calls=%async_computation.2 | async-start | bytes 28311552 | tf_op jit(solution)/shard_map/all_gather | solution.py:751
  257.8 423.5 %all-gather.5.cloned.1.call-start = ((), (), s32[]{:S(2)}) async-start(), calls=%async_computation | async-start | bytes 9437184 | tf_op jit(solution)/shard_map/all_gather | solution.py:752
  258.5 453.1 %all-gather.11.cloned.1.call-start = ((), (), s32[]{:S(2)}) async-start(), calls=%async_computation.3 | async-start | bytes 9437184 | tf_op jit(solution)/shard_map/all_gather | solution.py:753
  463.5 24.3 %copy-start.10 = (f32[32]{0:T(128)S(1)}, f32[32]{0:T(128)}, u32[]{:S(2)}) copy-start(f32[32]{0:T(128)} %constant.30.clone) | copy-start | bytes 388
  463.5 24.3 %copy-start.11 = (f32[4]{0:T(128)S(1)}, f32[4]{0:T(128)}, u32[]{:S(2)}) copy-start(f32[4]{0:T(128)} %get-tuple-element.47) | copy-start | bytes 52
  603.9 64.0 %copy-start.7 = (s32[4]{0:T(128)S(1)}, s32[4]{0:T(128)}, u32[]{:S(2)}) copy-start(s32[4]{0:T(128)} %or_bitcast_fusion) | copy-start | bytes 52
  603.9 66.2 %copy-start.6 = (f32[1,8,256]{2,0,1:T(1,128)S(1)}, f32[1,8,256]{2,0,1:T(1,128)}, u32[]{:S(2)}) copy-start(f32[1,8,256]{2,0,1:T(1,128)} %get-tuple-element.43) | copy-start | bytes 24580
  603.9 66.3 %copy-start.1 = (bf16[2,256,32,64]{1,3,2,0:T(8,128)(2,1)S(1)}, bf16[2,256,32,64]{1,3,2,0:T(8,128)(2,1)}, u32[]{:S(2)}) copy-start(bf16[2,256,32,64]{1,3,2,0:T(8,128)(2,1)} %param.20) | copy-start | bytes 6291460
  603.9 77.0 %copy-start.8 = (f32[4,32]{1,0:T(4,128)S(1)}, f32[4,32]{1,0:T(4,128)}, u32[]{:S(2)}) copy-start(f32[4,32]{1,0:T(4,128)} %get-tuple-element.45) | copy-start | bytes 1540
  603.9 77.0 %copy-start.9 = (f32[4,32]{1,0:T(4,128)S(1)}, f32[4,32]{1,0:T(4,128)}, u32[]{:S(2)}) copy-start(f32[4,32]{1,0:T(4,128)} %get-tuple-element.46) | copy-start | bytes 1540
  603.9 77.3 %copy-start.4 = (pred[32,2048]{1,0:T(8,128)(4,1)S(1)}, pred[32,2048]{1,0:T(8,128)(4,1)}, u32[]{:S(2)}) copy-start(pred[32,2048]{1,0:T(8,128)(4,1)} %copy.30) | copy-start | bytes 196612
  711.6 24.1 %copy-start.3 = (s32[4]{0:T(128)S(1)}, s32[4]{0:T(128)}, u32[]{:S(2)}) copy-start(s32[4]{0:T(128)} %lens_ref.3) | copy-start | bytes 52
Sparse Core Ops, SparseCore 0:
  257.2 226.3 all-gather.6
  485.4 119.6 all-gather.8
  606.9 49.9 all-gather.4
  658.6 53.0 all-gather.10
